TPU v7x, 32 devices: a whole 2x2x4 slice. The times are simulated.
32 devices in a mesh: dp: 8 (over z, x), tensor: 4 (over y, core).
Axes of the slice: x: 2, y: 2, z: 4, core: 2. Of those that a mesh axis runs over, the one named last changes fastest.
Arguments:
- hidden_in: bfloat16 [8192, 2048], P('dp', 'tensor'), may hold values from -6 to 6
- seg_ids: int32 [16, 512], P('dp'), may hold values from 0 to 15, never falling along the last dimension, each value on 1 to 256 neighbouring positions
- attn_gain: float32 [2048], replicated, may hold values from 0.5 to 1.5
- query_key_value_weight: bfloat16 [3, 2048, 2048], P(None, None, 'tensor'), may hold values from -0.125 to 0.125
- conv_weight: bfloat16 [3, 4, 2048], P(None, None, 'tensor'), may hold values from -3 to 3
- write_strength_weight: bfloat16 [2048, 16], P(None, 'tensor'), may hold values from -0.125 to 0.125
- onorm_gain: float32 [128], replicated, may hold values from 0.5 to 1.5
- output_projection_weight: bfloat16 [2048, 2048], P('tensor'), may hold values from -0.125 to 0.125
- mlp_gain: float32 [2048], replicated, may hold values from 0.5 to 1.5
- gate_up_projection_weight: bfloat16 [2, 2048, 5632], P(None, None, 'tensor'), may hold values from -0.125 to 0.125
- down_projection_weight: bfloat16 [5632, 2048], P('tensor'), may hold values from -0.078125 to 0.078125
- cotangent: bfloat16 [8192, 2048], P('dp', 'tensor'), may hold values from -6 to 6
Outputs:
- layer_out: bfloat16 [8192, 2048], P('dp', 'tensor')
- grad_in: bfloat16 [8192, 2048], P('dp', 'tensor')
- grad_attn_gain: float32 [2048], replicated
- grad_qkv: float32 [3, 2048, 2048], P(None, 'dp', 'tensor')
- grad_conv: float32 [3, 4, 2048], P(None, None, 'tensor')
- grad_beta: float32 [2048, 16], P('dp', 'tensor')
- grad_onorm: float32 [128], replicated
- grad_out: float32 [2048, 2048], P('tensor', 'dp')
- grad_mlp_gain: float32 [2048], replicated
- grad_gate_up: float32 [2, 2048, 5632], P(None, 'dp', 'tensor')
- grad_down: float32 [5632, 2048], P('tensor', 'dp')
Inputs may be any that keep to these rules, and one draw needn't show every extreme that they name: seg_ids never fall along a sequence; tokens with equal ids in one sequence form one document.
All inputs are finite; a program needn't handle non-finite values.
Results may differ from a plain program's by a relative error of at most 0.018.
Values may be sent and summed in bfloat16 or wider, within the bound.
A program may use at most 320 MiB of HBM per device.

v0:
```python
import jax
import jax.numpy as jnp
from jax import lax
from jax.sharding import PartitionSpec as P

HEAD_DIM = 128
CONV_SIZE = 4
SPAN = 64


EPS = 1e-06
HIGH_ACCURACY = lax.Precision.HIGHEST


def rms_scale(values):
    return lax.rsqrt(jnp.mean(values * values, axis=-1, keepdims=True) + EPS)


def unit_length(values):
    return values * lax.rsqrt(jnp.sum(values * values, axis=-1, keepdims=True) + EPS)


def rounded(values):
    return lax.optimization_barrier(values.astype(jnp.bfloat16)).astype(jnp.float32)


def norm_back(grad_normed, unit_rows, scale_rows, gain):
    scaled_grad = grad_normed * gain
    grad_rows = scale_rows * (
        scaled_grad - unit_rows * jnp.mean(scaled_grad * unit_rows, axis=-1, keepdims=True)
    )
    return (grad_rows, jnp.sum(grad_normed * unit_rows, axis=0))


def short_conv(projected_rows, segments, weight):
    length = projected_rows.shape[2]
    result = jnp.zeros_like(projected_rows)
    for offset in range(CONV_SIZE):
        moved = jnp.pad(projected_rows, ((0, 0), (0, 0), (offset, 0), (0, 0)))[:, :, :length]
        moved_seg = jnp.pad(segments, ((0, 0), (offset, 0)), constant_values=-1)[:, :length]
        same_doc = (moved_seg == segments).astype(jnp.float32)
        result = (
            result
            + weight[:, CONV_SIZE - 1 - offset][:, None, None, :]
            * moved
            * same_doc[None, :, :, None]
        )
    return result


def prepare(proj_seq, weight, segments):
    act = jax.nn.silu(short_conv(proj_seq, segments, weight))
    shaped = act.reshape(act.shape[:3] + (-1, HEAD_DIM))
    return (unit_length(shaped[0]), unit_length(shaped[1]), shaped[2])


def finish(mixed, gain):
    return mixed * rms_scale(mixed) * gain


def unit_lower_inverse(strict_part, identity):
    power = -strict_part
    inverse = identity + power
    reach = 2
    while reach < SPAN:
        power = jnp.einsum("shij,shjk->shik", power, power, precision=HIGH_ACCURACY)
        inverse = inverse + jnp.einsum("shij,shjk->shik", inverse, power, precision=HIGH_ACCURACY)
        reach = reach * 2
    return inverse


def delta_kernel(queries, keys_in, values, beta_rate, segments):
    seq_count = queries.shape[0]
    length = queries.shape[1]
    head_count = queries.shape[2]
    head_width = queries.shape[3]
    blocks = length // SPAN

    def split(array):
        return array.reshape(seq_count, blocks, SPAN, head_count, head_width).transpose(
            1, 0, 3, 2, 4
        )

    query_blocks = split(queries) * head_width ** (-0.5)
    key_blocks = split(keys_in)
    value_blocks = split(values)
    rate_blocks = beta_rate.reshape(seq_count, blocks, SPAN, head_count).transpose(1, 0, 3, 2)
    seg_blocks = segments.reshape(seq_count, blocks, SPAN).transpose(1, 0, 2)
    before = jnp.concatenate(
        [jnp.full((1, seq_count), -1, jnp.int32), seg_blocks[:-1, :, -1]], axis=0
    )
    carry_in = (seg_blocks == before[:, :, None]).astype(jnp.float32)
    same_doc = seg_blocks[:, :, :, None] == seg_blocks[:, :, None, :]
    positions = jnp.arange(SPAN)
    incl_mask = (same_doc & (positions[:, None] >= positions[None, :])).astype(jnp.float32)
    strict_mask = (same_doc & (positions[:, None] > positions[None, :])).astype(jnp.float32)
    tail_mask = (seg_blocks == seg_blocks[:, :, -1:]).astype(jnp.float32)
    identity = jnp.eye(SPAN, dtype=jnp.float32)

    def block_step(memory, inputs):
        query_c, key_c, value_c, rate_c, carry_c, incl_c, strict_c, tail_c = inputs
        gram = jnp.einsum("shik,shjk->shij", key_c, key_c, precision=HIGH_ACCURACY)
        strict_part = rate_c[:, :, :, None] * gram * strict_c[:, None]
        inverse = unit_lower_inverse(strict_part, identity)
        recalled = jnp.einsum("shik,shkv->shiv", key_c, memory, precision=HIGH_ACCURACY)
        target = rate_c[:, :, :, None] * (value_c - carry_c[:, None, :, None] * recalled)
        delta = jnp.einsum("shij,shjv->shiv", inverse, target, precision=HIGH_ACCURACY)
        scores = (
            jnp.einsum("shik,shjk->shij", query_c, key_c, precision=HIGH_ACCURACY) * incl_c[:, None]
        )
        output_c = carry_c[:, None, :, None] * jnp.einsum(
            "shik,shkv->shiv", query_c, memory, precision=HIGH_ACCURACY
        )
        output_c = output_c + jnp.einsum("shij,shjv->shiv", scores, delta, precision=HIGH_ACCURACY)
        memory = carry_c[:, -1][:, None, None, None] * memory + jnp.einsum(
            "shjk,shjv->shkv", key_c * tail_c[:, None, :, None], delta, precision=HIGH_ACCURACY
        )
        return (memory, output_c)

    start = jnp.zeros((seq_count, head_count, head_width, head_width), jnp.float32)
    final_state, outputs = lax.scan(
        block_step,
        start,
        (
            query_blocks,
            key_blocks,
            value_blocks,
            rate_blocks,
            carry_in,
            incl_mask,
            strict_mask,
            tail_mask,
        ),
    )
    return outputs.transpose(1, 0, 3, 2, 4).reshape(seq_count, length, head_count, head_width)


def body(
    hidden_in,
    seg_ids,
    attn_gain,
    query_key_value_weight,
    conv_weight,
    write_strength_weight,
    onorm_gain,
    output_projection_weight,
    mlp_gain,
    gate_up_projection_weight,
    down_projection_weight,
    cotangent,
):
    tokens = hidden_in.shape[0]
    seq_count = seg_ids.shape[0]
    length = seg_ids.shape[1]
    head_count = write_strength_weight.shape[1]
    contract_rows = (((0,), (0,)), ((), ()))
    contract_cols = (((1,), (1,)), ((), ()))
    full_in = lax.all_gather(hidden_in, "tensor", axis=1, tiled=True).astype(jnp.float32)
    scale_one = rms_scale(full_in)
    unit_one = full_in * scale_one
    normed_one = (unit_one * attn_gain).astype(jnp.bfloat16)
    projected_rows = jnp.einsum(
        "td,cdk->ctk", normed_one, query_key_value_weight, preferred_element_type=jnp.float32
    )
    output_logits = jnp.dot(normed_one, write_strength_weight, preferred_element_type=jnp.float32)
    beta_rate = jax.nn.sigmoid(output_logits)
    beta_seq = beta_rate.reshape(seq_count, length, head_count)

    def prepare_fn(proj_seq, weight):
        return prepare(proj_seq, weight, seg_ids)

    (queries, keys_in, values), prep_back = jax.vjp(
        prepare_fn,
        projected_rows.reshape(3, seq_count, length, -1),
        conv_weight.astype(jnp.float32),
    )
    query_low = rounded(queries)
    key_low = rounded(keys_in)
    value_low = rounded(values)

    def mixer(query_arg, key_arg, value_arg, rate_arg):
        return delta_kernel(query_arg, key_arg, value_arg, rate_arg, seg_ids)

    mixed, mixer_back = jax.vjp(mixer, query_low, key_low, value_low, beta_seq)
    normalized_output, post_back = jax.vjp(finish, mixed, onorm_gain)
    out_low = normalized_output.reshape(tokens, -1).astype(jnp.bfloat16)
    attn_part = jnp.dot(out_low, output_projection_weight, preferred_element_type=jnp.float32)
    middle = hidden_in.astype(jnp.float32) + lax.psum_scatter(
        attn_part, "tensor", scatter_dimension=1, tiled=True
    )
    full_mid = lax.all_gather(middle, "tensor", axis=1, tiled=True)
    scale_two = rms_scale(full_mid)
    unit_two = full_mid * scale_two
    normed_two = (unit_two * mlp_gain).astype(jnp.bfloat16)
    gate_up_product = jnp.einsum(
        "td,cdf->ctf", normed_two, gate_up_projection_weight, preferred_element_type=jnp.float32
    )
    gate_pre = gate_up_product[0]
    up_pre = gate_up_product[1]
    gate_sig = jax.nn.sigmoid(gate_pre)
    hidden_activation = (gate_pre * gate_sig * up_pre).astype(jnp.bfloat16)
    ffn_part = jnp.dot(
        hidden_activation, down_projection_weight, preferred_element_type=jnp.float32
    )
    layer_out = (
        middle
        + lax.psum_scatter(
            ffn_part.astype(jnp.bfloat16), "tensor", scatter_dimension=1, tiled=True
        ).astype(jnp.float32)
    ).astype(jnp.bfloat16)
    full_cot = lax.all_gather(cotangent, "tensor", axis=1, tiled=True)
    grad_down = lax.dot_general(
        hidden_activation, full_cot, contract_rows, preferred_element_type=jnp.float32
    )
    grad_hidden = lax.dot_general(
        full_cot, down_projection_weight, contract_cols, preferred_element_type=jnp.float32
    )
    grad_up = grad_hidden * gate_pre * gate_sig
    grad_gate = grad_hidden * up_pre * gate_sig * (1.0 + gate_pre * (1.0 - gate_sig))
    grad_pair = jnp.stack([grad_gate, grad_up]).astype(jnp.bfloat16)
    grad_gate_up = jnp.einsum(
        "td,ctf->cdf", normed_two, grad_pair, preferred_element_type=jnp.float32
    )
    grad_nmid = jnp.einsum(
        "ctf,cdf->td", grad_pair, gate_up_projection_weight, preferred_element_type=jnp.float32
    )
    part_two, gain_two = norm_back(grad_nmid, unit_two, scale_two, mlp_gain)
    grad_middle = cotangent.astype(jnp.float32) + lax.psum_scatter(
        part_two.astype(jnp.bfloat16), "tensor", scatter_dimension=1, tiled=True
    ).astype(jnp.float32)
    full_grad_mid = lax.all_gather(grad_middle.astype(jnp.bfloat16), "tensor", axis=1, tiled=True)
    grad_out = lax.dot_general(
        out_low, full_grad_mid, contract_rows, preferred_element_type=jnp.float32
    )
    grad_nout = lax.dot_general(
        full_grad_mid, output_projection_weight, contract_cols, preferred_element_type=jnp.float32
    )
    grad_mixed, gain_onorm = post_back(grad_nout.reshape(normalized_output.shape))
    grad_query, grad_key, grad_value, grad_rate = mixer_back(grad_mixed)
    grad_proj, grad_conv = prep_back((grad_query, grad_key, grad_value))
    grad_proj_low = grad_proj.reshape(3, tokens, -1).astype(jnp.bfloat16)
    grad_logits = (grad_rate.reshape(tokens, head_count) * beta_rate * (1.0 - beta_rate)).astype(
        jnp.bfloat16
    )
    grad_qkv = jnp.einsum(
        "td,ctk->cdk", normed_one, grad_proj_low, preferred_element_type=jnp.float32
    )
    grad_beta = lax.dot_general(
        normed_one, grad_logits, contract_rows, preferred_element_type=jnp.float32
    )
    grad_nin = jnp.einsum(
        "ctk,cdk->td", grad_proj_low, query_key_value_weight, preferred_element_type=jnp.float32
    )
    grad_nin = grad_nin + lax.dot_general(
        grad_logits, write_strength_weight, contract_cols, preferred_element_type=jnp.float32
    )
    part_one, gain_one = norm_back(grad_nin, unit_one, scale_one, attn_gain)
    grad_in = (
        grad_middle
        + lax.psum_scatter(
            part_one.astype(jnp.bfloat16), "tensor", scatter_dimension=1, tiled=True
        ).astype(jnp.float32)
    ).astype(jnp.bfloat16)
    grad_attn_gain, grad_mlp_gain, grad_onorm = lax.psum(
        (gain_one, gain_two, gain_onorm), ("dp", "tensor")
    )
    grad_conv = lax.psum(grad_conv, "dp")
    grad_qkv, grad_beta, grad_out, grad_gate_up, grad_down = (
        lax.psum_scatter(
            grad_qkv.astype(jnp.bfloat16), "dp", scatter_dimension=1, tiled=True
        ).astype(jnp.float32),
        lax.psum_scatter(
            grad_beta.astype(jnp.bfloat16), "dp", scatter_dimension=0, tiled=True
        ).astype(jnp.float32),
        lax.psum_scatter(
            grad_out.astype(jnp.bfloat16), "dp", scatter_dimension=1, tiled=True
        ).astype(jnp.float32),
        lax.psum_scatter(
            grad_gate_up.astype(jnp.bfloat16), "dp", scatter_dimension=1, tiled=True
        ).astype(jnp.float32),
        lax.psum_scatter(
            grad_down.astype(jnp.bfloat16), "dp", scatter_dimension=1, tiled=True
        ).astype(jnp.float32),
    )
    return (
        layer_out,
        grad_in,
        grad_attn_gain,
        grad_qkv,
        grad_conv,
        grad_beta,
        grad_onorm,
        grad_out,
        grad_mlp_gain,
        grad_gate_up,
        grad_down,
    )


def solution(mesh):
    return jax.shard_map(
        body,
        mesh=mesh,
        in_specs=(
            P("dp", "tensor"),
            P("dp", None),
            P(),
            P(None, None, "tensor"),
            P(None, None, "tensor"),
            P(None, "tensor"),
            P(),
            P("tensor", None),
            P(),
            P(None, None, "tensor"),
            P("tensor", None),
            P("dp", "tensor"),
        ),
        out_specs=(
            P("dp", "tensor"),
            P("dp", "tensor"),
            P(),
            P(None, "dp", "tensor"),
            P(None, None, "tensor"),
            P("dp", "tensor"),
            P(),
            P("tensor", "dp"),
            P(),
            P(None, "dp", "tensor"),
            P("tensor", "dp"),
        ),
        check_vma=False,
    )
```

profile of v0, /device:TPU:0, one launch (start us, length us, event | category | flops | bytes accessed | tf_op | source)
XLA Modules:
  0.0 1657.4 jit_solution(5726786623971570717)
XLA Ops:
  13.2 33.6 %all-gather.5.cloned.1.call-done = bf16[1024,2048]{1,0:T(8,128)(2,1)} async-done(((bf16[1024,512]{1,0:T(8,128)(2,1)}), bf16[1024,2048]{1,0:T(8,128)(2,1)}) %all-gather.5.cloned.1.call-update) | async-done | bytes 4194320 | tf_op jit(solution)/shard_map/all_gather | solution.py:158
  46.8 3.2 fusion.199
  50.2 10.6 fusion.210
  60.9 6.7 copy.315
  67.7 16.7 %fusion.207 = (f32[3,2,512,512]{2,3,1,0:T(8,128)S(1)}, f32[3,2,512,512]{2,3,1,0:T(8,128)}) fusion(f32[2,512]{1,0:T(2,128)S(1)} %get-tuple-element.1959, f32[3,2,512,512]{2,3,1,0:T(8,128)} %copy.315, f32[3,512]{1,0:T(4,128)S(1)} %get-tuple-element.1964, f32[2,512]{1,0:T(2,128)S(1)} %get-tuple-element.1958, f32[3,512]{1,0:T(4,128)S(1)} %get-tuple-element.1965, ...), kind=kLoop, calls=%fused_computation.315 | loop fusion | flops 22020096 | bytes 18911232 | tf_op jit(solution)/shard_map/jvp(jit(silu))/mul | solution.py:52
  90.0 2.9 copy.324
  92.9 3.3 copy.329
  97.8 2.6 copy.319
  100.4 3.2 copy.326
  103.6 2.6 copy.323
  106.2 3.5 fusion.219
  110.3 240.3 %while.90 = (s32[]{:T(128)}, f32[2,4,128,128]{3,2,1,0:T(8,128)S(1)}, f32[8,2,4,64,128]{4,3,2,1,0:T(8,128)}, f32[8,2,4,64,64]{4,3,2,1,0:T(8,128)}, f32[8,2,4,64,1...) while((s32[]{:T(128)}, ...), condition=%wide.region_4.5_spmd.clone, body=%wide.region_3.4_spmd.clone.sunk | while | flops 756850688 | bytes 20113280 | solution.py:121
  111.4 2.5 bitcast_dynamic-update-slice_fusion.38
  141.5 2.5 bitcast_dynamic-update-slice_fusion.38
  171.4 2.5 bitcast_dynamic-update-slice_fusion.38
  201.4 2.5 bitcast_dynamic-update-slice_fusion.38
  291.4 2.5 bitcast_dynamic-update-slice_fusion.38
  353.1 3.0 copy.330
  359.7 5.7 fusion.234
  365.4 71.3 %reduce-scatter.12.cloned.1.call-done = f32[1024,512]{1,0:T(8,128)} async-done(((f32[1024,2048]{1,0:T(8,128)}), f32[1024,512]{1,0:T(8,128)}) %reduce-scatter.12.cloned.1.call-update) | async-done | bytes 2097168 | tf_op jit(solution)/shard_map/reduce_scatter | solution.py:188
  436.8 3.3 convert_add_fusion.1
  440.7 57.8 %all-gather.7.cloned.1.call-done = f32[1024,2048]{1,0:T(8,128)} async-done(((f32[1024,512]{1,0:T(8,128)}), f32[1024,2048]{1,0:T(8,128)}) %all-gather.7.cloned.1.call-update) | async-done | bytes 8388624 | tf_op jit(solution)/shard_map/all_gather | solution.py:191
  498.5 4.1 multiply_reduce_fusion.1
  504.2 26.0 %convolution_bitcast_fusion = f32[2,1024,1408]{2,1,0:T(8,128)} fusion(bf16[2,2048,1408]{2,1,0:T(8,128)(2,1)} %param.25, f32[1024,2048]{1,0:T(8,128)S(1)} %copy-done.9, f32[2048]{0:T(1024)S(1)} %copy-done.55, f32[1024]{0:T(1024)S(1)} %add_rsqrt_fusion.2), kind=kOutput, calls=%fused_computation.299 | convolution fusion | flops 11817451520 | bytes 31469568 | tf_op jit(solution)/shard_map/td,cdf->ctf/dot_general | solution.py:195
  530.2 4.2 all-gather.9.cloned.1.call-done
  534.4 16.6 %fusion.214 = (bf16[1,1024,1408]{2,1,0:T(8,128)(2,1)}, bf16[1,1024,1408]{2,1,0:T(8,128)(2,1)}, bf16[1024,1408]{1,0:T(8,128)(2,1)}) fusion(f32[2,1024,1408]{2,1,0:T(8,128)} %convolution_bitcast_fusion, bf16[1024,2048]{1,0:T(8,128)(2,1)} %all-gather.9.cloned.1.call-done, bf16[1408,2048]{1,0:T(8,128)(2,1)} %param.26), kind=kOutput, calls=%fused_computation.338 | convolution fusion | flops 5928648704 | bytes 30146560 | tf_op jit(solution)/shard_map/dot_general | solution.py:215
  551.0 21.1 %fusion.200 = (f32[2048]{0:T(1024)}, f32[1024]{0:T(1024)S(1)}, f32[1024,2048,1]{1,0,2:T(8,128)}) fusion(f32[1024,2048]{1,0:T(8,128)} %all-gather.7.cloned.1.call-done, f32[1024]{0:T(1024)S(1)} %add_rsqrt_fusion.2, f32[2048]{0:T(1024)S(1)} %copy-done.55, bf16[2,2048,1408]{2,1,0:T(8,128)(2,1)} %param.25, bf16[1,1024,1408]{2,1,0:T(8,128)(2,1)} %get-tuple-element.1942, ...), kind=kOutput, calls=%fused_computation.287 | convolution fusion | flops 11826623488 | bytes 34103296 | tf_op jit(solution)/shard_map/ctf,cdf->td/dot_general | solution.py:224
  572.0 9.2 multiply_convert_fusion
  581.3 44.5 %reduce-scatter.16.cloned.1.call-done = bf16[1024,512]{1,0:T(8,128)(2,1)} async-done(((bf16[1024,2048]{1,0:T(8,128)(2,1)}), bf16[1024,512]{1,0:T(8,128)(2,1)}) %reduce-scatter.16.cloned.1.call-update) | async-done | bytes 1048592 | tf_op jit(solution)/shard_map/reduce_scatter | solution.py:228
  625.8 2.5 fusion.216
  628.3 10.9 convolution_convert_fusion.1
  639.3 10.5 convolution_convert_fusion
  649.9 13.0 all-gather.11.cloned.1.call-done
  662.9 7.7 multiply_reduce_fusion.6
  670.6 3.2 reshape.355
  673.8 2.7 multiply_reduce_fusion.9
  683.6 460.2 %while.91 = (s32[]{:T(128)}, f32[2,4,128,128]{3,2,1,0:T(8,128)S(1)}, f32[8,2,4,64,128]{4,3,0,2,1:T(8,128)}, f32[8,2,4,64,128]{4,3,0,2,1:T(8,128)}, f32[8,2,4,64,...) while((s32[]{:T(128)}, ...), condition=%wide.region_15.16_spmd.clone, body=%wide.region_12.15_spmd.clone.sunk | while | flops 1512635904 | bytes 39142420 | solution.py:121
  1143.9 3.4 convolution_convert_fusion.3
  1148.5 6.0 convolution_convert_fusion.2
  1154.5 19.4 %convert_bitcast_fusion.1 = bf16[2,2048,1408]{1,2,0:T(8,128)(2,1)} fusion(bf16[1,1024,1408]{2,1,0:T(8,128)(2,1)} %get-tuple-element.1942, bf16[1,1024,1408]{2,1,0:T(8,128)(2,1)} %get-tuple-element.1941, f32[1024,2048]{1,0:T(8,128)} %all-gather.7.cloned.1.call-done, f32[2048]{0:T(1024)S(1)} %copy-done.55, f32[1024]{0:T(1024)S(1)} %add_rsqrt_fusion.2), kind=kOutput, calls=%fused_computation.269 | convolution fusion | flops 11826102272 | bytes 25702400 | tf_op jit(solution)/shard_map/td,ctf->cdf/dot_general | solution.py:221
  1174.0 3.2 copy.347
  1179.0 2.9 copy.346
  1181.9 3.3 broadcast_multiply_fusion
  1185.2 3.0 copy.349
  1188.2 2.8 multiply_reduce_fusion.8
  1197.1 3.0 pad_add_fusion
  1200.2 6.6 copy.351
  1206.8 16.4 multiply_reduce_fusion.5
  1223.2 3.6 multiply_multiply_fusion
  1226.9 8.6 fusion.204
  1235.5 4.8 copy.352
  1240.3 10.2 fusion.235
  1250.4 3.2 fusion.198
  1253.7 3.4 fusion.197
  1257.2 11.5 convert_bitcast_fusion.2
  1270.3 2.5 add_convert_fusion.1
  1275.2 38.6 %psum.29 = f32[3,4,512]{2,0,1:T(4,128)S(1)} all-reduce(f32[3,4,512]{2,0,1:T(4,128)S(1)} %pad_add_fusion.1), channel_id=1, replica_groups=mesh['dp'=8,'tensor'=4] {'dp'}, use_global_device_ids=true, to_apply=%region_27.28 | all-reduce | flops 6144 | bytes 49152 | tf_op jit(solution)/shard_map/psum | solution.py:267
  1314.4 41.4 %all-reduce.17 = (f32[2048]{0:T(1024)}, f32[128]{0:T(128)}, f32[2048]{0:T(1024)}) all-reduce(f32[2048]{0:T(1024)S(1)} %get-tuple-element.1746, f32[128]{0:T(128)S(1)} %bitcast_reduce_fusion, f32[2048]{0:T(1024)S(1)} %copy-done.56), channel_id=1, replica_groups=mesh['dp'=8,'tensor'=4] {'dp','tensor'}, use_global_device_ids=true, to_apply=%region_21.22 | all-reduce | flops 4224 | bytes 33792 | tf_op jit(solution)/shard_map/psum | solution.py:264
  1359.1 121.0 %reduce-scatter.24.cloned.1.call-done = bf16[2,256,1408]{1,2,0:T(8,128)(2,1)} async-done(((bf16[2,2048,1408]{1,2,0:T(8,128)(2,1)}), bf16[2,256,1408]{1,2,0:T(8,128)(2,1)}) %reduce-scatter.24.cloned.1.call-update) | async-done | bytes 1441808 | tf_op jit(solution)/shard_map/reduce_scatter | solution.py:278
  1480.1 3.0 copy.359
  1483.1 43.0 %reduce-scatter.18.cloned.1.call-done = bf16[1024,512]{1,0:T(8,128)(2,1)} async-done(((bf16[1024,2048]{1,0:T(8,128)(2,1)}), bf16[1024,512]{1,0:T(8,128)(2,1)}) %reduce-scatter.18.cloned.1.call-update) | async-done | bytes 1048592 | tf_op jit(solution)/shard_map/reduce_scatter | solution.py:260
  1526.1 3.1 add_convert_fusion
  1529.1 119.0 %reduce-scatter.20.cloned.1.call-done = bf16[3,256,512]{1,2,0:T(8,128)(2,1)} async-done(((bf16[3,2048,512]{1,2,0:T(8,128)(2,1)}), bf16[3,256,512]{1,2,0:T(8,128)(2,1)}) %reduce-scatter.20.cloned.1.call-update) | async-done | bytes 786448 | tf_op jit(solution)/shard_map/reduce_scatter | solution.py:269
  1648.1 2.6 copy.357
  (825 shorter events, 731.1 us)
Async XLA Ops:
  7.2 352.5 %copy-start = (bf16[512,2048]{1,0:T(8,128)(2,1)S(1)}, bf16[512,2048]{1,0:T(8,128)(2,1)}, u32[]{:S(2)}) copy-start(bf16[512,2048]{1,0:T(8,128)(2,1)} %param.23) | copy-start | bytes 6291460
  7.2 39.6 %all-gather.5.cloned.1.call-start = ((), (), s32[]{:S(2)}) async-start(), calls=%async_computation.9 | async-start | bytes 5242880 | tf_op jit(solution)/shard_map/all_gather | solution.py:158
  7.9 428.8 %reduce-scatter.12.cloned.1.call-start = ((), (), s32[]{:S(2)}) async-start(), calls=%async_computation.10 | async-start | bytes 10485760 | tf_op jit(solution)/shard_map/reduce_scatter | solution.py:188
  11.1 56.5 %copy-start.43 = (f32[2,512]{1,0:T(2,128)}, f32[2,512]{1,0:T(2,128)S(1)}, u32[]{:S(2)}) copy-start(f32[2,512]{1,0:T(2,128)S(1)} %get-tuple-element.1957) | copy-start | bytes 12292
  11.1 56.5 %copy-start.45 = (f32[2,512]{1,0:T(2,128)}, f32[2,512]{1,0:T(2,128)S(1)}, u32[]{:S(2)}) copy-start(f32[2,512]{1,0:T(2,128)S(1)} %get-tuple-element.1958) | copy-start | bytes 12292
  11.1 56.5 %copy-start.47 = (f32[2,512]{1,0:T(2,128)}, f32[2,512]{1,0:T(2,128)S(1)}, u32[]{:S(2)}) copy-start(f32[2,512]{1,0:T(2,128)S(1)} %get-tuple-element.1959) | copy-start | bytes 12292
  12.1 55.5 %copy-start.33 = (f32[3,512]{1,0:T(4,128)}, f32[3,512]{1,0:T(4,128)S(1)}, u32[]{:S(2)}) copy-start(f32[3,512]{1,0:T(4,128)S(1)} %get-tuple-element.1964) | copy-start | bytes 18436
  12.1 55.5 %copy-start.35 = (f32[3,512]{1,0:T(4,128)}, f32[3,512]{1,0:T(4,128)S(1)}, u32[]{:S(2)}) copy-start(f32[3,512]{1,0:T(4,128)S(1)} %get-tuple-element.1965) | copy-start | bytes 18436
  12.1 55.5 %copy-start.37 = (f32[3,512]{1,0:T(4,128)}, f32[3,512]{1,0:T(4,128)S(1)}, u32[]{:S(2)}) copy-start(f32[3,512]{1,0:T(4,128)S(1)} %get-tuple-element.1966) | copy-start | bytes 18436
  12.2 55.5 %copy-start.39 = (f32[3,512]{1,0:T(4,128)}, f32[3,512]{1,0:T(4,128)S(1)}, u32[]{:S(2)}) copy-start(f32[3,512]{1,0:T(4,128)S(1)} %get-tuple-element.1967) | copy-start | bytes 18436
  13.2 36.8 %copy-start.51 = (f32[2048]{0:T(1024)S(1)}, f32[2048]{0:T(1024)}, u32[]{:S(2)}) copy-start(f32[2048]{0:T(1024)} %param.18) | copy-start | bytes 24580
  46.8 3.4 copy-start.6
  50.2 56.0 %copy-start.49 = (f32[1024]{0:T(1024)}, f32[1024]{0:T(1024)S(1)}, u32[]{:S(2)}) copy-start(f32[1024]{0:T(1024)S(1)} %add_rsqrt_fusion.3) | copy-start | bytes 12292
  92.9 3.3 copy-start.5
  96.5 3.9 copy-start.31
  96.6 3.9 copy-start.27
  103.6 2.6 copy-start.53
  365.3 71.4 %copy-start.22 = (bf16[1024,512]{1,0:T(8,128)(2,1)S(1)}, bf16[1024,512]{1,0:T(8,128)(2,1)}, u32[]{:S(2)}) copy-start(bf16[1024,512]{1,0:T(8,128)(2,1)} %param.16) | copy-start | bytes 3145732
  365.4 133.1 %all-gather.7.cloned.1.call-start = ((), (), s32[]{:S(2)}) async-start(), calls=%async_computation.11 | async-start | bytes 10485760 | tf_op jit(solution)/shard_map/all_gather | solution.py:191
  440.0 94.3 %all-gather.9.cloned.1.call-start = ((), (), s32[]{:S(2)}) async-start(), calls=%async_computation.13 | async-start | bytes 5242880 | tf_op jit(solution)/shard_map/all_gather | solution.py:211
  440.6 62.0 %copy-start.55 = (f32[2048]{0:T(1024)S(1)}, f32[2048]{0:T(1024)}, u32[]{:S(2)}) copy-start(f32[2048]{0:T(1024)} %param.24) | copy-start | bytes 24580
  440.6 185.1 %reduce-scatter.16.cloned.1.call-start = ((), (), s32[]{:S(2)}) async-start(), calls=%async_computation.14 | async-start | bytes 5242880 | tf_op jit(solution)/shard_map/reduce_scatter | solution.py:228
  498.5 5.8 copy-start.9
  581.2 44.6 %copy-start.14 = (bf16[1024,512]{1,0:T(8,128)(2,1)S(1)}, bf16[1024,512]{1,0:T(8,128)(2,1)}, u32[]{:S(2)}) copy-start(bf16[1024,512]{1,0:T(8,128)(2,1)} %param.27) | copy-start | bytes 3145732
  581.2 81.7 %all-gather.11.cloned.1.call-start = ((), (), s32[]{:S(2)}) async-start(), calls=%async_computation.15 | async-start | bytes 5242880 | tf_op jit(solution)/shard_map/all_gather | solution.py:231
  628.3 640.5 %reduce-scatter.14.cloned.1.call-start = ((), (), s32[]{:S(2)}) async-start(), calls=%async_computation.12 | async-start | bytes 5242880 | tf_op jit(solution)/shard_map/reduce_scatter | solution.py:207
  639.3 633.6 %reduce-scatter.26.cloned.1.call-start = ((), (), s32[]{:S(2)}) async-start(), calls=%async_computation.20 | async-start | bytes 6488064 | tf_op jit(solution)/shard_map/reduce_scatter | solution.py:281
  649.8 706.0 %reduce-scatter.28.cloned.1.call-start = ((), (), s32[]{:S(2)}) async-start(), calls=%async_computation.21 | async-start | bytes 589824
  670.6 3.2 copy-start.8
  670.6 3.2 copy-start.57
  673.8 2.7 copy-start.12
  683.6 460.3 %copy-start.42 = (f32[1024,4]{0,1:T(4,128)S(1)}, f32[1024,4]{0,1:T(4,128)}, u32[]{:S(2)}) copy-start(f32[1024,4]{0,1:T(4,128)} %copy-done.41) | copy-start | bytes 49156
  683.6 460.3 %copy-start.50 = (f32[1024]{0:T(1024)S(1)}, f32[1024]{0:T(1024)}, u32[]{:S(2)}) copy-start(f32[1024]{0:T(1024)} %copy-done.49) | copy-start | bytes 12292
  683.6 460.3 %copy-start.52 = (f32[2048]{0:T(1024)S(1)}, f32[2048]{0:T(1024)}, u32[]{:S(2)}) copy-start(f32[2048]{0:T(1024)} %param.18) | copy-start | bytes 24580
  724.4 8.5 copy-start.2
  782.0 8.4 copy-start.2
  839.4 8.4 copy-start.2
  896.8 8.4 copy-start.2
  954.2 8.4 copy-start.2
  1011.7 8.4 copy-start.2
  1069.1 8.4 copy-start.2
  1126.5 8.4 copy-start.2
  1143.9 4.6 copy-start.24
  1148.4 208.9 %reduce-scatter.22.cloned.1.call-start = ((), (), s32[]{:S(2)}) async-start(), calls=%async_computation.18 | async-start | bytes 2359296 | tf_op jit(solution)/shard_map/reduce_scatter | solution.py:275
  1154.5 325.7 %reduce-scatter.24.cloned.1.call-start = ((), (), s32[]{:S(2)}) async-start(), calls=%async_computation.19 | async-start | bytes 12976128 | tf_op jit(solution)/shard_map/reduce_scatter | solution.py:278
  1173.9 352.1 %reduce-scatter.18.cloned.1.call-start = ((), (), s32[]{:S(2)}) async-start(), calls=%async_computation.16 | async-start | bytes 5242880 | tf_op jit(solution)/shard_map/reduce_scatter | solution.py:260
  1174.0 3.2 copy-start.4
  1185.2 6.4 copy-start.30
  1188.2 2.9 copy-start.32
  1188.2 2.9 copy-start.20
  1200.1 6.6 copy-start.44
  1200.1 6.6 copy-start.46
  1200.1 6.6 copy-start.48
  1206.8 16.4 copy-start.34
  1206.8 16.4 copy-start.36
  1206.8 16.4 copy-start.38
  1223.2 3.6 copy-start.40
  1240.3 10.2 copy-start.7
  1240.3 10.2 copy-start.54
  1257.1 391.0 %reduce-scatter.20.cloned.1.call-start = ((), (), s32[]{:S(2)}) async-start(), calls=%async_computation.17 | async-start | bytes 7077888 | tf_op jit(solution)/shard_map/reduce_scatter | solution.py:269
  1272.8 41.6 %copy-start.58 = (f32[512]{0:T(512)S(1)}, f32[512]{0:T(512)}, u32[]{:S(2)}) copy-start(f32[512]{0:T(512)} %get-tuple-element.1962) | copy-start | bytes 6148
  1272.9 41.6 %copy-start.56 = (f32[2048]{0:T(1024)S(1)}, f32[2048]{0:T(1024)}, u32[]{:S(2)}) copy-start(f32[2048]{0:T(1024)} %get-tuple-element.1744) | copy-start | bytes 24580
  1359.1 166.9 %copy-start.15 = (bf16[1024,512]{1,0:T(8,128)(2,1)S(1)}, bf16[1024,512]{1,0:T(8,128)(2,1)}, u32[]{:S(2)}) copy-start(bf16[1024,512]{1,0:T(8,128)(2,1)} %param.27) | copy-start | bytes 3145732
  1526.1 124.6 %copy-start.1 = (bf16[512,2048]{1,0:T(8,128)(2,1)S(1)}, bf16[512,2048]{1,0:T(8,128)(2,1)}, u32[]{:S(2)}) copy-start(bf16[512,2048]{1,0:T(8,128)(2,1)} %param.23) | copy-start | bytes 6291460
  (15 other events, 25.7 us)
Sparse Core Ops, SparseCore 0:
  9.6 37.1 all-gather.4
  365.5 71.2 reduce-scatter.11
  440.2 58.2 all-gather.6
  499.9 34.4 all-gather.8
  581.3 44.3 reduce-scatter.15
  628.4 34.4 all-gather.10
  665.4 44.3 reduce-scatter.13
  713.5 111.0 reduce-scatter.25
  1148.5 63.1 reduce-scatter.27
  1215.1 68.3 reduce-scatter.21
  1287.2 192.9 reduce-scatter.23
  1482.5 43.4 reduce-scatter.17
  1529.7 118.4 reduce-scatter.19
where the time goes:
time: 1680 us; the launch traced here: 1660 us
  matrix products  780 us (46%)
  waiting for transfers between devices  509 us (30%)
  other arithmetic  137 us (8%)
  local copies, waits for them, and re-layouts  133 us (8%)
  blocking collectives  80 us (5%)
    dot_general x120, matrix products, unit_lower_inverse(): power = jnp.einsum('shij,shjk->shik', power, power, precision=HIGH_ACCURACY)  167 us
    dot_general x120, matrix products, unit_lower_inverse(): jnp.einsum('shij,shjk->shik', inverse, power, precision=HIGH_ACCURACY)  159 us
    reduce_scatter x1, waiting for transfers between devices, body(): lax.psum_scatter(grad_gate_up.astype(jnp.bfloat16), 'dp', scatter_dimensi...  121 us
    reduce_scatter x1, waiting for transfers between devices, body(): lax.psum_scatter(grad_qkv.astype(jnp.bfloat16), 'dp', scatter_dimension=1...  119 us
    reduce_scatter x1, waiting for transfers between devices, body(): lax.psum_scatter(attn_part, 'tensor', scatter_dimension=1, tiled=True)  71.3 us
    all_gather x1, waiting for transfers between devices, body(): full_mid = lax.all_gather(middle, 'tensor', axis=1, tiled=True)  57.8 us
    dot_general x24, matrix products, block_step(): jnp.einsum('shik,shkv->shiv', query_c, memory, precision=HIGH_ACCURACY)  47.4 us
    dot_general x24, matrix products, block_step(): jnp.einsum('shjk,shjv->shkv', key_c * tail_c[:, None, :, None], delta, pr...  46.4 us
  transfers between devices with their start and end apart: 13, of which 9 were waited for; matrix products, arithmetic and copies ran while one was open for 40% of the time, Pallas kernels for 0%

commit v1 on v0

v1 whole, which is shorter than its diff:
```python
import jax
import jax.numpy as jnp
from jax import lax
from jax.experimental import pallas as pl
from jax.experimental.pallas import tpu as pltpu
from jax.sharding import PartitionSpec as P

HEAD_DIM = 128
TAPS = 4
CHUNK = 128
HALO = 8
EPS = 1e-06
PAIR = 2
F32 = jnp.float32
BF16 = jnp.bfloat16


def dot_nn(a, b):
    return jnp.dot(a.astype(BF16), b.astype(BF16), preferred_element_type=F32)


def dot_nt(a, b):
    return lax.dot_general(a.astype(BF16), b.astype(BF16), (((1,), (1,)), ((), ())), preferred_element_type=F32)


def dot_tn(a, b):
    return lax.dot_general(a.astype(BF16), b.astype(BF16), (((0,), (0,)), ((), ())), preferred_element_type=F32)


def column(row):
    return jnp.broadcast_to(row, (CHUNK, CHUNK)).T


def load_segments(seg_ref, segcol, length):
    segcol[0:HALO, :] = jnp.full((HALO, CHUNK), -1.0, F32)
    segcol[HALO + length :, :] = jnp.full((HALO, CHUNK), -2.0, F32)
    for n in range(length // CHUNK):
        row = seg_ref[0, :, n * CHUNK : (n + 1) * CHUNK].astype(F32)
        segcol[HALO + n * CHUNK : HALO + (n + 1) * CHUNK, :] = column(row)


def seg_rows(segcol, n, shift):
    base = HALO + n * CHUNK + shift
    return segcol[base : base + CHUNK, :]


def back_masks(segcol, n):
    here = seg_rows(segcol, n, 0)
    return [None] + [(seg_rows(segcol, n, -s) == here).astype(F32) for s in range(1, TAPS)]


def state_masks(seg_ref, segcol, n):
    here = seg_rows(segcol, n, 0)
    row = jnp.broadcast_to(seg_ref[0, :, n * CHUNK : (n + 1) * CHUNK].astype(F32), (CHUNK, CHUNK))
    same = here == row
    before = segcol[HALO + n * CHUNK - 1 : HALO + n * CHUNK, :]
    last = segcol[HALO + (n + 1) * CHUNK - 1 : HALO + (n + 1) * CHUNK, :]
    carry = (here == before).astype(F32)
    tail = (here == last).astype(F32)
    carry_last = (last == before).astype(F32)
    return same, carry, tail, carry_last


def taps_in(proj_ref, c, h, n):
    lanes = slice(h * HEAD_DIM, (h + 1) * HEAD_DIM)
    if n == 0:
        return jnp.concatenate([jnp.zeros((HALO, HEAD_DIM), F32), proj_ref[c, 0:CHUNK, lanes].astype(F32)], axis=0)
    return proj_ref[c, n * CHUNK - HALO : (n + 1) * CHUNK, lanes].astype(F32)


def conv_rows(window, weight_ref, c, h, masks):
    lanes = slice(h * HEAD_DIM, (h + 1) * HEAD_DIM)
    total = weight_ref[c, TAPS - 1 : TAPS, lanes] * window[HALO:]
    for s in range(1, TAPS):
        total = total + weight_ref[c, TAPS - 1 - s : TAPS - s, lanes] * (masks[s] * window[HALO - s : HALO - s + CHUNK])
    return total


def grid_ids():
    rows = lax.broadcasted_iota(jnp.int32, (CHUNK, CHUNK), 0)
    cols = lax.broadcasted_iota(jnp.int32, (CHUNK, CHUNK), 1)
    return rows, cols


def forward_kernel(proj_ref, seg_ref, weight_ref, logit_ref, gain_ref, out_ref, mixed_ref, inv_ref, score_ref, state_ref, delta_ref, err_ref, segcol):
    length = proj_ref.shape[1]
    chunks = length // CHUNK
    load_segments(seg_ref, segcol, length)
    rows, cols = grid_ids()
    apart = rows ^ cols
    lower = rows > cols
    lower_incl = rows >= cols
    scale = HEAD_DIM**-0.5
    pieces, systems, inverses = {}, {}, {}
    for n in range(chunks):
        masks = back_masks(segcol, n)
        same, carry, tail, carry_last = state_masks(seg_ref, segcol, n)
        span = slice(n * CHUNK, (n + 1) * CHUNK)
        for h in range(PAIR):
            acts = []
            for c in range(3):
                conv = conv_rows(taps_in(proj_ref, c, h, n), weight_ref, c, h, masks)
                acts.append(conv * jax.nn.sigmoid(conv))
            q = (acts[0] * lax.rsqrt(jnp.sum(acts[0] * acts[0], axis=-1, keepdims=True) + EPS)).astype(BF16)
            k = (acts[1] * lax.rsqrt(jnp.sum(acts[1] * acts[1], axis=-1, keepdims=True) + EPS)).astype(BF16)
            v = acts[2].astype(BF16).astype(F32)
            rate = jax.nn.sigmoid(column(logit_ref[h, :, span]))
            gram = jnp.where(same & lower, dot_nt(k, k), 0.0)
            scores = (jnp.where(same & lower_incl, dot_nt(q, k), 0.0) * scale).astype(BF16)
            system = rate * gram
            score_ref[h, span, :] = scores
            systems[n, h] = system
            inverses[n, h] = jnp.where(rows == cols, 1.0, 0.0) - jnp.where(apart == 1, system, 0.0)
            pieces[n, h] = (q, k.astype(F32), v, gram, scores, rate, carry, tail, carry_last)
    level = 1
    while (2 << level) <= CHUNK:
        crossed = {}
        for key, inverse in inverses.items():
            crossed[key] = dot_nn(jnp.where((apart >> level) == 1, systems[key], 0.0), inverse)
        for key, inverse in inverses.items():
            inverses[key] = inverse - dot_nn(inverse, crossed[key])
        level += 1
    for n, h in pieces:
        q, kf, v, gram, scores, rate, carry, tail, carry_last = pieces[n, h]
        inverse = inverses[n, h].astype(BF16)
        inv_ref[h, n * CHUNK : (n + 1) * CHUNK, :] = inverse
        base = dot_nn(inverse, rate * v)
        back = dot_nn(inverse, rate * carry * kf)
        pieces[n, h] = (q, kf, v, gram, scores, base, back, carry, tail, carry_last)
    for h in range(PAIR):
        lanes = slice(h * HEAD_DIM, (h + 1) * HEAD_DIM)
        state = None
        for n in range(chunks):
            span = slice(n * CHUNK, (n + 1) * CHUNK)
            q, kf, v, gram, scores, base, back, carry, tail, carry_last = pieces[n, h]
            if n == 0:
                delta = base
                rest = v
                state_ref[h, span, :] = jnp.zeros((CHUNK, CHUNK), BF16)
            else:
                low = state.astype(BF16)
                state_ref[h, span, :] = low
                delta = base - dot_nn(back, low)
                rest = v - carry * dot_nn(kf, low)
            delta_low = delta.astype(BF16)
            moved = dot_tn(tail * kf, delta_low)
            mixed = dot_nn(scores, delta_low)
            if n > 0:
                mixed = mixed + (carry * scale) * dot_nn(q, low)
                moved = moved + carry_last * state
            state = moved
            delta_ref[span, lanes] = delta_low
            err_ref[span, lanes] = (rest - dot_nn(gram, delta_low)).astype(BF16)
            mixed_ref[span, lanes] = mixed
            root = lax.rsqrt(jnp.mean(mixed * mixed, axis=-1, keepdims=True) + EPS)
            out_ref[span, lanes] = (mixed * root * gain_ref[...]).astype(BF16)


def backward_kernel(proj_ref, seg_ref, weight_ref, logit_ref, gain_ref, mixed_ref, inv_ref, score_ref, state_ref, delta_ref, err_ref, nout_ref,
                    gproj_ref, glogit_ref, gconv_ref, gonorm_ref, segcol, gin_ref, act_ref, q_ref, k_ref, head_ref, dq_ref, dk_ref):
    length = proj_ref.shape[1]
    chunks = length // CHUNK
    pair, seq = pl.program_id(0), pl.program_id(1)
    load_segments(seg_ref, segcol, length)
    rows, cols = grid_ids()
    lower = rows > cols
    lower_incl = rows >= cols
    scale = HEAD_DIM**-0.5

    @pl.when((pair == 0) & (seq == 0))
    def _():
        gonorm_ref[...] = jnp.zeros_like(gonorm_ref)

    @pl.when(seq == 0)
    def _():
        gconv_ref[...] = jnp.zeros_like(gconv_ref)

    onorm = jnp.zeros((1, HEAD_DIM), F32)
    pieces = {}
    for n in range(chunks):
        masks = back_masks(segcol, n)
        same, carry, tail, carry_last = state_masks(seg_ref, segcol, n)
        span = slice(n * CHUNK, (n + 1) * CHUNK)
        for h in range(PAIR):
            lanes = slice(h * HEAD_DIM, (h + 1) * HEAD_DIM)
            for c in range(3):
                act_ref[h, c, span, :] = conv_rows(taps_in(proj_ref, c, h, n), weight_ref, c, h, masks)
            conv = act_ref[h, 0, span, :]
            act = conv * jax.nn.sigmoid(conv)
            q = (act * lax.rsqrt(jnp.sum(act * act, axis=-1, keepdims=True) + EPS)).astype(BF16)
            conv = act_ref[h, 1, span, :]
            act = conv * jax.nn.sigmoid(conv)
            k = (act * lax.rsqrt(jnp.sum(act * act, axis=-1, keepdims=True) + EPS)).astype(BF16)
            q_ref[h, span, :] = q
            k_ref[h, span, :] = k
            mixed = mixed_ref[span, lanes]
            root = lax.rsqrt(jnp.mean(mixed * mixed, axis=-1, keepdims=True) + EPS)
            unit = mixed * root
            grad = nout_ref[span, lanes].astype(F32)
            onorm = onorm + jnp.sum(grad * unit, axis=0, keepdims=True)
            scaled = grad * gain_ref[...]
            gmix = root * (scaled - unit * jnp.mean(scaled * unit, axis=-1, keepdims=True))
            glow = gmix.astype(BF16)
            inverse = inv_ref[h, span, :]
            delta = delta_ref[span, lanes]
            gscore = (jnp.where(same & lower_incl, dot_nt(glow, delta), 0.0) * scale).astype(BF16)
            dq = dot_nn(gscore, k)
            held = (scale * carry * gmix).astype(BF16)
            if n > 0:
                dq = dq + dot_nt(held, state_ref[h, span, :])
            dq_ref[h, span, :] = dq
            dk_ref[h, span, :] = dot_tn(gscore, q)
            start = dot_tn(inverse, dot_tn(score_ref[h, span, :], glow))
            kf = k.astype(F32)
            reach = dot_tn(inverse, tail * kf).astype(BF16)
            feed = dot_tn(q, held)
            pieces[n, h] = (start, reach, feed)
    gonorm_ref[...] += onorm
    for h in range(PAIR):
        lanes = slice(h * HEAD_DIM, (h + 1) * HEAD_DIM)
        flow = None
        for n in reversed(range(chunks)):
            span = slice(n * CHUNK, (n + 1) * CHUNK)
            same, carry, tail, carry_last = state_masks(seg_ref, segcol, n)
            rate = jax.nn.sigmoid(column(logit_ref[h, :, span]))
            start, reach, feed = pieces[n, h]
            k = k_ref[h, span, :]
            delta = delta_ref[span, lanes]
            gtarget = start
            if flow is not None:
                low = flow.astype(BF16)
                gtarget = gtarget + dot_nn(reach, low)
            gval = rate * gtarget
            head_ref[h, span, :] = gval
            grecall = (carry * gval).astype(BF16)
            dk = dk_ref[h, span, :]
            if flow is not None:
                dk = dk + tail * dot_nt(delta, low)
            if n > 0:
                dk = dk - dot_nt(grecall, state_ref[h, span, :])
                nxt = feed - dot_tn(k, grecall)
                if flow is not None:
                    nxt = nxt + carry_last * flow
                flow = nxt
            ggram = jnp.where(same & lower, dot_nt(gval, delta), 0.0)
            dk_ref[h, span, :] = dk - dot_nn(ggram + ggram.T, k)
            grate = jnp.sum(err_ref[span, lanes].astype(F32) * gtarget, axis=-1, keepdims=True)
            glogit = jnp.broadcast_to(grate, (CHUNK, CHUNK)) * rate * (1.0 - rate)
            glogit_ref[h, :, span] = glogit.T[0:1, :].astype(BF16)
    for h in range(PAIR):
        lanes = slice(h * HEAD_DIM, (h + 1) * HEAD_DIM)
        for c in range(3):
            gin_ref[h, c, length:, :] = jnp.zeros((HALO, HEAD_DIM), F32)
        taps = [[jnp.zeros((1, HEAD_DIM), F32)] * TAPS for _ in range(3)]
        for n in range(chunks):
            masks = back_masks(segcol, n)
            span = slice(n * CHUNK, (n + 1) * CHUNK)
            for c in range(3):
                conv = act_ref[h, c, span, :]
                gate = jax.nn.sigmoid(conv)
                act = conv * gate
                if c == 2:
                    gact = head_ref[h, span, :]
                else:
                    gunit = (dq_ref if c == 0 else dk_ref)[h, span, :]
                    inv = lax.rsqrt(jnp.sum(act * act, axis=-1, keepdims=True) + EPS)
                    unit = act * inv
                    gact = inv * (gunit - unit * jnp.sum(gunit * unit, axis=-1, keepdims=True))
                gin = gact * (gate + act * (1.0 - gate))
                gin_ref[h, c, span, :] = gin
                window = taps_in(proj_ref, c, h, n)
                taps[c][TAPS - 1] = taps[c][TAPS - 1] + jnp.sum(gin * window[HALO:], axis=0, keepdims=True)
                for s in range(1, TAPS):
                    part = jnp.sum(gin * masks[s] * window[HALO - s : HALO - s + CHUNK], axis=0, keepdims=True)
                    taps[c][TAPS - 1 - s] = taps[c][TAPS - 1 - s] + part
        for c in range(3):
            gconv_ref[c, :, lanes] += jnp.concatenate(taps[c], axis=0)
        for n in range(chunks):
            span = slice(n * CHUNK, (n + 1) * CHUNK)
            here = seg_rows(segcol, n, 0)
            ahead = [None] + [(seg_rows(segcol, n, s) == here).astype(F32) for s in range(1, TAPS)]
            for c in range(3):
                total = weight_ref[c, TAPS - 1 : TAPS, lanes] * gin_ref[h, c, span, :]
                for s in range(1, TAPS):
                    later = gin_ref[h, c, n * CHUNK + s : (n + 1) * CHUNK + s, :]
                    total = total + weight_ref[c, TAPS - 1 - s : TAPS - s, lanes] * (ahead[s] * later)
                gproj_ref[c, span, lanes] = total.astype(BF16)


def mixer_shapes(proj, seg):
    seqs, length = seg.shape
    return seqs, length, proj.shape[2] // HEAD_DIM


def mixer_forward(proj, seg, weight, logits, gain):
    seqs, length, heads = mixer_shapes(proj, seg)
    tokens = seqs * length
    wide = PAIR * HEAD_DIM
    flat = pl.BlockSpec((length, wide), lambda s, p: (s, p))
    square = pl.BlockSpec((PAIR, length, CHUNK), lambda s, p: (p, s, 0))
    return pl.pallas_call(
        forward_kernel,
        grid=(seqs, heads // PAIR),
        in_specs=[
            pl.BlockSpec((3, length, wide), lambda s, p: (0, s, p)),
            pl.BlockSpec((1, 1, length), lambda s, p: (s, 0, 0)),
            pl.BlockSpec((3, TAPS, wide), lambda s, p: (0, 0, p)),
            pl.BlockSpec((PAIR, 1, length), lambda s, p: (p, 0, s)),
            pl.BlockSpec((1, HEAD_DIM), lambda s, p: (0, 0)),
        ],
        out_specs=[flat, flat, square, square, square, flat, flat],
        out_shape=[
            jax.ShapeDtypeStruct((tokens, heads * HEAD_DIM), BF16),
            jax.ShapeDtypeStruct((tokens, heads * HEAD_DIM), F32),
            jax.ShapeDtypeStruct((heads, tokens, CHUNK), BF16),
            jax.ShapeDtypeStruct((heads, tokens, CHUNK), BF16),
            jax.ShapeDtypeStruct((heads, tokens, CHUNK), BF16),
            jax.ShapeDtypeStruct((tokens, heads * HEAD_DIM), BF16),
            jax.ShapeDtypeStruct((tokens, heads * HEAD_DIM), BF16),
        ],
        scratch_shapes=[pltpu.VMEM((length + 2 * HALO, CHUNK), F32)],
        compiler_params=pltpu.CompilerParams(vmem_limit_bytes=48 << 20),
        name="mixer_forward",
    )(proj, seg.reshape(seqs, 1, length), weight, logits, gain.reshape(1, HEAD_DIM))


def mixer_backward(proj, seg, weight, logits, gain, kept, grad_nout):
    seqs, length, heads = mixer_shapes(proj, seg)
    tokens = seqs * length
    wide = PAIR * HEAD_DIM
    mixed, inverse, scores, states, delta, err = kept
    flat = pl.BlockSpec((length, wide), lambda p, s: (s, p))
    square = pl.BlockSpec((PAIR, length, CHUNK), lambda p, s: (p, s, 0))
    cube = pl.BlockSpec((3, length, wide), lambda p, s: (0, s, p))
    taps = pl.BlockSpec((3, TAPS, wide), lambda p, s: (0, 0, p))
    line = pl.BlockSpec((PAIR, 1, length), lambda p, s: (p, 0, s))
    vector = pl.BlockSpec((1, HEAD_DIM), lambda p, s: (0, 0))
    return pl.pallas_call(
        backward_kernel,
        grid=(heads // PAIR, seqs),
        in_specs=[cube, pl.BlockSpec((1, 1, length), lambda p, s: (s, 0, 0)), taps, line, vector, flat, square, square, square, flat, flat, flat],
        out_specs=[cube, line, taps, vector],
        out_shape=[
            jax.ShapeDtypeStruct(proj.shape, BF16),
            jax.ShapeDtypeStruct((heads, 1, tokens), BF16),
            jax.ShapeDtypeStruct(weight.shape, F32),
            jax.ShapeDtypeStruct((1, HEAD_DIM), F32),
        ],
        scratch_shapes=[
            pltpu.VMEM((length + 2 * HALO, CHUNK), F32),
            pltpu.VMEM((PAIR, 3, length + HALO, HEAD_DIM), F32),
            pltpu.VMEM((PAIR, 3, length, HEAD_DIM), F32),
            pltpu.VMEM((PAIR, length, HEAD_DIM), BF16),
            pltpu.VMEM((PAIR, length, HEAD_DIM), BF16),
            pltpu.VMEM((PAIR, length, HEAD_DIM), F32),
            pltpu.VMEM((PAIR, length, HEAD_DIM), F32),
            pltpu.VMEM((PAIR, length, HEAD_DIM), F32),
        ],
        compiler_params=pltpu.CompilerParams(vmem_limit_bytes=48 << 20),
        name="mixer_backward",
    )(proj, seg.reshape(seqs, 1, length), weight, logits, gain.reshape(1, HEAD_DIM), mixed, inverse, scores, states, delta, err, grad_nout)


ROWS = (((0,), (0,)), ((), ()))
COLS = (((1,), (1,)), ((), ()))


def rms_scale(values):
    return lax.rsqrt(jnp.mean(values * values, axis=-1, keepdims=True) + EPS)


def norm_back(grad_normed, unit_rows, scale_rows, gain):
    scaled_grad = grad_normed * gain
    grad_rows = scale_rows * (scaled_grad - unit_rows * jnp.mean(scaled_grad * unit_rows, axis=-1, keepdims=True))
    return grad_rows, jnp.sum(grad_normed * unit_rows, axis=0)


def butterfly(values, axis, size):
    step = 1
    while step < size:
        pairs = [(i, i ^ step) for i in range(size)]
        values = values + lax.ppermute(values, axis, pairs)
        step *= 2
    return values


def scatter_sum(values, axis, dim):
    return lax.psum_scatter(values.astype(BF16), axis, scatter_dimension=dim, tiled=True).astype(F32)


def make_body(dp_size, tensor_size):
    def body(hidden_in, seg_ids, attn_gain, wqkv, conv_weight, wrate, onorm_gain, wout, mlp_gain, wgu, wdown, cotangent):
        tokens = hidden_in.shape[0]
        heads = wrate.shape[1]
        dot = lambda a, b, dims: lax.dot_general(a, b, dims, preferred_element_type=F32)
        taps = conv_weight.astype(F32)
        full_in = lax.all_gather(hidden_in, "tensor", axis=1, tiled=True).astype(F32)
        scale_one = rms_scale(full_in)
        unit_one = full_in * scale_one
        normed_one = (unit_one * attn_gain).astype(BF16)
        proj = jnp.einsum("td,cdk->ctk", normed_one, wqkv, preferred_element_type=F32)
        logits = jnp.einsum("td,dh->ht", normed_one, wrate, preferred_element_type=F32).reshape(heads, 1, tokens)
        out_low, *kept = mixer_forward(proj, seg_ids, taps, logits, onorm_gain)
        attn_part = jnp.dot(out_low, wout, preferred_element_type=F32)
        middle = hidden_in.astype(F32) + scatter_sum(attn_part, "tensor", 1)
        full_mid = lax.all_gather(middle.astype(BF16), "tensor", axis=1, tiled=True).astype(F32)
        full_cot = lax.all_gather(cotangent, "tensor", axis=1, tiled=True)
        scale_two = rms_scale(full_mid)
        unit_two = full_mid * scale_two
        normed_two = (unit_two * mlp_gain).astype(BF16)
        gate_up = jnp.einsum("td,cdf->ctf", normed_two, wgu, preferred_element_type=F32)
        gate_pre, up_pre = gate_up[0], gate_up[1]
        gate_sig = jax.nn.sigmoid(gate_pre)
        hidden = (gate_pre * gate_sig * up_pre).astype(BF16)
        grad_hidden = dot(full_cot, wdown, COLS)
        grad_up = grad_hidden * gate_pre * gate_sig
        grad_gate = grad_hidden * up_pre * gate_sig * (1.0 + gate_pre * (1.0 - gate_sig))
        grad_pair = jnp.stack([grad_gate, grad_up]).astype(BF16)
        grad_nmid = jnp.einsum("ctf,cdf->td", grad_pair, wgu, preferred_element_type=F32)
        part_two, gain_two = norm_back(grad_nmid, unit_two, scale_two, mlp_gain)
        grad_middle = cotangent.astype(F32) + scatter_sum(part_two, "tensor", 1)
        full_grad_mid = lax.all_gather(grad_middle.astype(BF16), "tensor", axis=1, tiled=True)
        grad_down = dot(hidden, full_cot, ROWS)
        grad_gate_up = jnp.einsum("td,ctf->cdf", normed_two, grad_pair, preferred_element_type=F32)
        ffn_part = jnp.dot(hidden, wdown, preferred_element_type=F32)
        layer_out = (middle + scatter_sum(ffn_part, "tensor", 1)).astype(BF16)
        grad_nout = dot(full_grad_mid, wout, COLS)
        grad_out = dot(out_low, full_grad_mid, ROWS)
        grad_proj, grad_logits, grad_conv, gain_onorm = mixer_backward(proj, seg_ids, taps, logits, onorm_gain, kept, grad_nout)
        grad_logits = grad_logits.reshape(heads, tokens)
        grad_nin = jnp.einsum("ctk,cdk->td", grad_proj, wqkv, preferred_element_type=F32)
        grad_nin = grad_nin + jnp.einsum("ht,dh->td", grad_logits, wrate, preferred_element_type=F32)
        grad_qkv = jnp.einsum("td,ctk->cdk", normed_one, grad_proj, preferred_element_type=F32)
        grad_beta = jnp.einsum("td,ht->dh", normed_one, grad_logits, preferred_element_type=F32)
        part_one, gain_one = norm_back(grad_nin, unit_one, scale_one, attn_gain)
        grad_in = (grad_middle + scatter_sum(part_one, "tensor", 1)).astype(BF16)
        width = gain_one.shape[0]
        flat = jnp.concatenate([gain_one, gain_two, gain_onorm.reshape(-1), grad_conv.reshape(-1), grad_beta.reshape(-1)])
        shared = 2 * width + HEAD_DIM
        flat = butterfly(flat, "dp", dp_size)
        gains = butterfly(flat[:shared], "tensor", tensor_size)
        grad_conv = flat[shared : shared + grad_conv.size].reshape(grad_conv.shape)
        mine = grad_beta.shape[0] // dp_size
        grad_beta = flat[shared + grad_conv.size :].reshape(grad_beta.shape)
        grad_beta = lax.dynamic_slice_in_dim(grad_beta, lax.axis_index("dp") * mine, mine, 0)
        return (
            layer_out,
            grad_in,
            gains[:width],
            scatter_sum(grad_qkv, "dp", 1),
            grad_conv,
            grad_beta,
            gains[2 * width :],
            scatter_sum(grad_out, "dp", 1),
            gains[width : 2 * width],
            scatter_sum(grad_gate_up, "dp", 1),
            scatter_sum(grad_down, "dp", 1),
        )

    return body


def solution(mesh):
    return jax.shard_map(
        make_body(mesh.shape["dp"], mesh.shape["tensor"]),
        mesh=mesh,
        in_specs=(
            P("dp", "tensor"),
            P("dp", None),
            P(),
            P(None, None, "tensor"),
            P(None, None, "tensor"),
            P(None, "tensor"),
            P(),
            P("tensor", None),
            P(),
            P(None, None, "tensor"),
            P("tensor", None),
            P("dp", "tensor"),
        ),
        out_specs=(
            P("dp", "tensor"),
            P("dp", "tensor"),
            P(),
            P(None, "dp", "tensor"),
            P(None, None, "tensor"),
            P("dp", "tensor"),
            P(),
            P("tensor", "dp"),
            P(),
            P(None, "dp", "tensor"),
            P("tensor", "dp"),
        ),
        check_vma=False,
    )
```

time: 1680 us -> 954 us (0.57)
  matrix products: 780 us -> 155 us
  waiting for transfers between devices: 509 us -> 660 us
  local copies, waits for them, and re-layouts: 133 us -> 18.1 us
  other arithmetic: 137 us -> 32.6 us
  blocking collectives: 80 us -> 0 us
  Pallas kernels: 0 us -> 55.9 us
    dot_general x423 -> x15, matrix products: 780 us -> 155 us  [the longest x4 39.5 us: body(): lax.dot_general(a, b, dims, preferred_element_type=F32)]
    reduce_scatter x8, waiting for transfers between devices: 399 us -> 551 us  [scatter_sum(): lax.psum_scatter(values.astype(BF16), axis, scatter_dimension=dim, tiled=...]
    psum x2 -> x0, blocking collectives: 80 us -> none  [the longest x1 41.4 us: body(): lax.psum((gain_one, gain_two, gain_onorm), ('dp', 'tensor'))]
    pallas_call x0 -> x2, Pallas kernels: none -> 55.9 us  [the longest x1 32.5 us: mixer_backward(): pl.pallas_call(backward_kernel, grid=(heads // PAIR, seqs), in_specs=[cub...]
    reduce_sum x15 -> x0, other arithmetic: 31.8 us -> none  [the longest x1 16.4 us: short_conv(): weight[:, CONV_SIZE - 1 - offset][:, None, None, :] * moved]
    mul x6 -> x0, other arithmetic: 25.3 us -> none  [the longest x1 16.7 us: prepare(): act = jax.nn.silu(short_conv(proj_seq, segments, weight))]
    mul x51 -> x0, local copies, waits for them, and re-layouts: 24.1 us -> none  [the longest x16 13.6 us: block_step(): jnp.einsum('shik,shjk->shij', query_c, key_c, precision=HIGH_ACCURACY)]
    dynamic_update_slice x24 -> x0, other arithmetic: 20.8 us -> none  [delta_kernel(): lax.scan(block_step, start, (query_blocks, key_blocks, value_blocks, rate...]
  transfers between devices with their start and end apart: 13 -> 17, of which waited for: 9 -> 15; matrix products, arithmetic and copies ran while one was open for 40% -> 14% of each run, Pallas kernels for 0% -> 3%
where the time goes in v1:
time: 954 us; the launch traced here: 945 us
  waiting for transfers between devices  660 us (69%)
  matrix products  155 us (16%)
  Pallas kernels  55.9 us (6%)
  other arithmetic  32.6 us (3%)
  local copies, waits for them, and re-layouts  18.1 us (2%)
  between operations  15 us (2%)
    reduce_scatter x8, waiting for transfers between devices, scatter_sum(): lax.psum_scatter(values.astype(BF16), axis, scatter_dimension=dim, tiled=...  551 us
    dot_general x4, matrix products, body(): lax.dot_general(a, b, dims, preferred_element_type=F32)  39.5 us
    all_gather x1, waiting for transfers between devices, body(): lax.all_gather(hidden_in, 'tensor', axis=1, tiled=True).astype(F32)  37.4 us
    all_gather x1, waiting for transfers between devices, body(): lax.all_gather(middle.astype(BF16), 'tensor', axis=1, tiled=True)  34 us
    pallas_call x1, Pallas kernels, mixer_backward(): pl.pallas_call(backward_kernel, grid=(heads // PAIR, seqs), in_specs=[cub...  32.5 us
    pallas_call x1, Pallas kernels, mixer_forward(): pl.pallas_call(forward_kernel, grid=(seqs, heads // PAIR), in_specs=[pl.B...  23.4 us
    dot_general x1, matrix products, body(): jnp.einsum('td,ctf->cdf', normed_two, grad_pair, preferred_element_type=F32)  19.8 us
    dot_general x1, matrix products, body(): jnp.einsum('ctf,cdf->td', grad_pair, wgu, preferred_element_type=F32)  19.2 us
  transfers between devices with their start and end apart: 17, of which 15 were waited for; matrix products, arithmetic and copies ran while one was open for 14% of the time, Pallas kernels for 3%

profile of v1, /device:TPU:0, one launch (start us, length us, event | category | flops | bytes accessed | tf_op | source)
XLA Modules:
  0.0 944.9 jit_solution(15103385196377588979)
XLA Ops:
  7.2 0.7 all-gather.5.cloned.1.call-update
  8.0 0.7 reshape.83.seg_ref
  8.7 0.7 convert_element_type.94.weight_ref
  9.4 37.4 %all-gather.5.cloned.1.call-done = bf16[1024,2048]{1,0:T(8,128)(2,1)} async-done(((bf16[1024,512]{1,0:T(8,128)(2,1)}), bf16[1024,2048]{1,0:T(8,128)(2,1)}) %all-gather.5.cloned.1.call-update) | async-done | bytes 4194320 | tf_op jit(solution)/shard_map/all_gather | solution.py:397
  46.8 3.2 fusion.14
  50.1 3.6 convolution_bitcast_fusion.1
  53.7 0.5 slice-done.1
  54.2 8.8 fusion.29.proj_ref
  63.0 23.4 %mixer_forward.1 = (bf16[1024,512]{1,0:T(8,128)(2,1)S(1)}, f32[1024,512]{1,0:T(8,128)}, bf16[4,1024,128]{2,1,0:T(8,128)(2,1)S(1)}, bf16[4,1024,128]{2,1,0:T(8,12...) custom-call(f32[3,1024,512]{2,1,0:T(8,128)} %fusion.29.proj_ref, ...), custom_call_target="tpu_custom_call" | custom-call | tf_op jit(solution)/shard_map/mixer_forward/pallas_call | solution.py:301
  86.5 1.0 copy-done.1
  87.4 1.0 copy-done.3
  88.4 1.0 copy-done.5
  89.4 1.0 copy-done.9
  90.5 4.3 convolution_convert_fusion.2
  94.8 44.5 %reduce-scatter.9.cloned.1.call-done = bf16[1024,512]{1,0:T(8,128)(2,1)} async-done(((bf16[1024,2048]{1,0:T(8,128)(2,1)}), bf16[1024,512]{1,0:T(8,128)(2,1)}) %reduce-scatter.9.cloned.1.call-update) | async-done | bytes 1048592 | tf_op jit(solution)/shard_map/reduce_scatter | solution.py:388
  139.3 2.8 fusion.34
  142.2 0.5 all-gather.9.cloned.1.call-update
  142.8 34.0 %all-gather.7.cloned.1.call-done = bf16[1024,2048]{1,0:T(8,128)(2,1)} async-done(((bf16[1024,512]{1,0:T(8,128)(2,1)}), bf16[1024,2048]{1,0:T(8,128)(2,1)}) %all-gather.7.cloned.1.call-update) | async-done | bytes 4194320 | tf_op jit(solution)/shard_map/all_gather | solution.py:406
  176.8 3.1 fusion.21
  179.9 19.1 %convolution_bitcast_fusion = f32[2,1024,1408]{2,1,0:T(8,128)} fusion(bf16[2,2048,1408]{2,1,0:T(8,128)(2,1)} %param.21, bf16[1024,2048]{1,0:T(8,128)(2,1)} %all-gather.7.cloned.1.call-done, f32[2048]{0:T(1024)S(1)} %copy-done.17, f32[1024]{0:T(1024)S(1)} %add_rsqrt_fusion), kind=kOutput, calls=%fused_computation.30 | convolution fusion | flops 11819548672 | bytes 27275264 | tf_op jit(solution)/shard_map/td,cdf->ctf/dot_general | solution.py:411
  199.0 13.7 %all-gather.9.cloned.1.call-done = bf16[1024,2048]{1,0:T(8,128)(2,1)} async-done(((bf16[1024,512]{1,0:T(8,128)(2,1)}), bf16[1024,2048]{1,0:T(8,128)(2,1)}) %all-gather.9.cloned.1.call-update) | async-done | bytes 4194320 | tf_op jit(solution)/shard_map/all_gather | solution.py:407
  212.7 16.7 %fusion.28 = (bf16[1,1024,1408]{2,1,0:T(8,128)(2,1)}, bf16[1,1024,1408]{2,1,0:T(8,128)(2,1)}, bf16[1024,1408]{1,0:T(8,128)(2,1)}) fusion(f32[2,1024,1408]{2,1,0:T(8,128)} %convolution_bitcast_fusion, bf16[1024,2048]{1,0:T(8,128)(2,1)} %all-gather.9.cloned.1.call-done, bf16[1408,2048]{1,0:T(8,128)(2,1)} %param.22), kind=kOutput, calls=%fused_computation.48 | convolution fusion | flops 5928648704 | bytes 30146560 | tf_op jit(solution)/shard_map/dot_general | solution.py:395
  229.4 19.2 %fusion.20 = (f32[2048]{0:T(1024)S(1)}, f32[1024]{0:T(1024)S(1)}, f32[1024,2048,1]{1,0,2:T(8,128)}) fusion(bf16[1024,2048]{1,0:T(8,128)(2,1)S(1)} %copy-done.12, f32[1024]{0:T(1024)S(1)} %add_rsqrt_fusion, f32[2048]{0:T(1024)S(1)} %copy-done.17, bf16[2,2048,1408]{2,1,0:T(8,128)(2,1)} %param.21, bf16[1,1024,1408]{2,1,0:T(8,128)(2,1)} %get-tuple-element.60, ...), kind=kOutput, calls=%fused_computation.25 | convolution fusion | flops 11828720640 | bytes 29908992 | tf_op jit(solution)/shard_map/ctf,cdf->td/dot_general | solution.py:419
  248.7 6.2 fusion.19
  255.0 44.5 %reduce-scatter.13.cloned.1.call-done = bf16[1024,512]{1,0:T(8,128)(2,1)} async-done(((bf16[1024,2048]{1,0:T(8,128)(2,1)}), bf16[1024,512]{1,0:T(8,128)(2,1)}) %reduce-scatter.13.cloned.1.call-update) | async-done | bytes 1048592 | tf_op jit(solution)/shard_map/reduce_scatter | solution.py:388
  299.5 2.8 fusion.35
  302.3 11.0 %convolution_convert_fusion.1 = bf16[1024,2048]{1,0:T(8,128)(2,1)} fusion(bf16[1024,1408]{1,0:T(8,128)(2,1)} %get-tuple-element.61, bf16[1408,2048]{1,0:T(8,128)(2,1)} %param.22), kind=kOutput, calls=%fused_computation.43 | convolution fusion | flops 5907677184 | bytes 12845056 | tf_op jit(solution)/shard_map/dot_general | solution.py:425
  313.4 10.5 %convolution_convert_fusion = bf16[1408,2048]{1,0:T(8,128)(2,1)} fusion(bf16[1024,1408]{1,0:T(8,128)(2,1)} %get-tuple-element.61, bf16[1024,2048]{1,0:T(8,128)(2,1)} %all-gather.9.cloned.1.call-done), kind=kOutput, calls=%fused_computation.29 | convolution fusion | flops 5908463616 | bytes 12845056 | tf_op jit(solution)/shard_map/dot_general | solution.py:395
  324.0 12.9 %all-gather.11.cloned.1.call-done = bf16[1024,2048]{1,0:T(8,128)(2,1)} async-done(((bf16[1024,512]{1,0:T(8,128)(2,1)}), bf16[1024,2048]{1,0:T(8,128)(2,1)}) %all-gather.11.cloned.1.call-update) | async-done | bytes 4194320 | tf_op jit(solution)/shard_map/all_gather | solution.py:422
  336.9 6.2 convolution_convert_fusion.3
  343.2 19.8 %convert_bitcast_fusion = bf16[2,2048,1408]{1,2,0:T(8,128)(2,1)} fusion(bf16[1,1024,1408]{2,1,0:T(8,128)(2,1)} %get-tuple-element.60, bf16[1,1024,1408]{2,1,0:T(8,128)(2,1)} %get-tuple-element.59, bf16[1024,2048]{1,0:T(8,128)(2,1)} %all-gather.7.cloned.1.call-done, f32[2048]{0:T(1024)S(1)} %copy-done.17, f32[1024]{0:T(1024)S(1)} %add_rsqrt_fusion), kind=kOutput, calls=%fused_computation | convolution fusion | flops 11828199424 | bytes 21508096 | tf_op jit(solution)/shard_map/td,ctf->cdf/dot_general | solution.py:424
  363.1 6.0 fusion.48.nout_ref
  369.1 32.5 %mixer_backward.1 = (bf16[3,1024,512]{2,1,0:T(8,128)(2,1)}, bf16[4,1,1024]{2,1,0:T(2,128)(2,1)S(1)}, f32[3,4,512]{2,1,0:T(4,128)S(1)}, f32[1,128]{1,0:T(1,128)S(1)}) custom-call(f32[3,1024,512]{2,1,0:T(8,128)} %fusion.29.proj_ref, s32[2,1,512]{2,1,0:T(1,128)S(1)} %reshape.83.seg_ref, f32[3,4,512]{2,1,0:T(4,128)S(1)} %convert_element_type.94.weight_ref, ...), custom_call_target="tpu_custom_call" | custom-call | tf_op jit(solution)/shard_map/mixer_backward/pallas_call | solution.py:338
  401.6 10.0 %fusion.49 = f32[1024,2048,1]{1,0,2:T(8,128)S(1)} fusion(bf16[3,1024,512]{2,1,0:T(8,128)(2,1)} %get-tuple-element.29, bf16[3,2048,512]{2,1,0:T(8,128)(2,1)} %param.15), kind=kOutput, calls=%fused_computation.77 | convolution fusion | flops 6442450944 | bytes 17825792 | tf_op jit(solution)/shard_map/ctk,cdk->td/dot_general | solution.py:431
  411.6 3.2 fusion.13
  414.8 3.7 fusion.12
  418.6 11.6 %convert_bitcast_fusion.1 = bf16[3,2048,512]{1,2,0:T(8,128)(2,1)} fusion(bf16[3,1024,512]{2,1,0:T(8,128)(2,1)} %get-tuple-element.29, bf16[1024,2048]{1,0:T(8,128)(2,1)} %all-gather.5.cloned.1.call-done, f32[2048]{0:T(1024)S(1)} %copy-done.15, f32[1024]{0:T(1024)S(1)} %add_rsqrt_fusion.1), kind=kOutput, calls=%fused_computation.31 | convolution fusion | flops 6453985280 | bytes 13643776 | tf_op jit(solution)/shard_map/td,ctk->cdk/dot_general | solution.py:433
  430.3 4.9 fusion.36
  435.2 1.9 reshape.89
  437.1 1.4 collective-permute-start
  438.5 4.3 collective-permute-done
  442.8 1.9 collective-permute-start.1
  444.7 2.6 collective-permute-done.1
  447.3 2.8 collective-permute-start.2
  450.1 2.6 collective-permute-done.2
  452.8 3.0 add_convert_fusion.1
  455.8 43.7 %reduce-scatter.23.cloned.1.call-done = bf16[1408,256]{1,0:T(8,128)(2,1)} async-done(((bf16[1408,2048]{1,0:T(8,128)(2,1)}), bf16[1408,256]{1,0:T(8,128)(2,1)}) %reduce-scatter.23.cloned.1.call-update) | async-done | bytes 720912 | tf_op jit(solution)/shard_map/reduce_scatter | solution.py:388
  499.6 2.3 convert_element_type.120
  501.9 2.1 slice.40
  504.0 1.5 collective-permute-start.4
  505.5 0.9 constant_dynamic-slice_fusion
  506.5 0.6 reshape.90
  507.1 0.7 copy.31
  507.7 0.1 collective-permute-done.4
  507.8 0.5 slice.49
  508.3 0.6 fusion.47
  508.9 62.5 %reduce-scatter.19.cloned.1.call-done = bf16[512,256]{1,0:T(8,128)(2,1)} async-done(((bf16[512,2048]{1,0:T(8,128)(2,1)}), bf16[512,256]{1,0:T(8,128)(2,1)}) %reduce-scatter.19.cloned.1.call-update) | async-done | bytes 262160 | tf_op jit(solution)/shard_map/reduce_scatter | solution.py:388
  571.4 1.8 convert_element_type.115
  573.2 193.8 %reduce-scatter.21.cloned.1.call-done = bf16[2,256,1408]{1,2,0:T(8,128)(2,1)} async-done(((bf16[2,2048,1408]{1,2,0:T(8,128)(2,1)}), bf16[2,256,1408]{1,2,0:T(8,128)(2,1)}) %reduce-scatter.21.cloned.1.call-update) | async-done | bytes 1441808 | tf_op jit(solution)/shard_map/reduce_scatter | solution.py:388
  767.0 3.0 copy.32
  770.0 43.1 %reduce-scatter.15.cloned.1.call-done = bf16[1024,512]{1,0:T(8,128)(2,1)} async-done(((bf16[1024,2048]{1,0:T(8,128)(2,1)}), bf16[1024,512]{1,0:T(8,128)(2,1)}) %reduce-scatter.15.cloned.1.call-update) | async-done | bytes 1048592 | tf_op jit(solution)/shard_map/reduce_scatter | solution.py:388
  813.1 2.9 add_convert_fusion
  816.0 119.0 %reduce-scatter.17.cloned.1.call-done = bf16[3,256,512]{1,2,0:T(8,128)(2,1)} async-done(((bf16[3,2048,512]{1,2,0:T(8,128)(2,1)}), bf16[3,256,512]{1,2,0:T(8,128)(2,1)}) %reduce-scatter.17.cloned.1.call-update) | async-done | bytes 786448 | tf_op jit(solution)/shard_map/reduce_scatter | solution.py:388
  935.0 2.6 copy.30
  (80 shorter events, 1.0 us)
Async XLA Ops:
  7.2 83.3 %copy-start = (bf16[512,2048]{1,0:T(8,128)(2,1)S(1)}, bf16[512,2048]{1,0:T(8,128)(2,1)}, u32[]{:S(2)}) copy-start(bf16[512,2048]{1,0:T(8,128)(2,1)} %param.19) | copy-start | bytes 6291460
  7.2 39.6 %all-gather.5.cloned.1.call-start = ((), (), s32[]{:S(2)}) async-start(), calls=%async_computation.8 | async-start | bytes 5242880 | tf_op jit(solution)/shard_map/all_gather | solution.py:397
  7.9 131.4 %reduce-scatter.9.cloned.1.call-start = ((), (), s32[]{:S(2)}) async-start(), calls=%async_computation.9 | async-start | bytes 5242880 | tf_op jit(solution)/shard_map/reduce_scatter | solution.py:388
  46.8 6.9 slice-start
  50.0 3.7 copy-start.10
  50.0 3.7 copy-start.15
  50.0 4.2 slice-start.1
  54.2 8.8 copy-start.8
  86.5 1.0 copy-start.1
  87.4 1.0 copy-start.3
  88.4 1.0 copy-start.5
  89.4 1.0 copy-start.9
  94.8 85.1 %copy-start.17 = (f32[2048]{0:T(1024)S(1)}, f32[2048]{0:T(1024)}, u32[]{:S(2)}) copy-start(f32[2048]{0:T(1024)} %param.20) | copy-start | bytes 24580
  94.8 82.0 %all-gather.7.cloned.1.call-start = ((), (), s32[]{:S(2)}) async-start(), calls=%async_computation.10 | async-start | bytes 5242880 | tf_op jit(solution)/shard_map/all_gather | solution.py:406
  142.2 70.5 %all-gather.9.cloned.1.call-start = ((), (), s32[]{:S(2)}) async-start(), calls=%async_computation.12 | async-start | bytes 5242880 | tf_op jit(solution)/shard_map/all_gather | solution.py:407
  142.7 156.7 %reduce-scatter.13.cloned.1.call-start = ((), (), s32[]{:S(2)}) async-start(), calls=%async_computation.13 | async-start | bytes 5242880 | tf_op jit(solution)/shard_map/reduce_scatter | solution.py:388
  212.7 16.7 %copy-start.12 = (bf16[1024,2048]{1,0:T(8,128)(2,1)S(1)}, bf16[1024,2048]{1,0:T(8,128)(2,1)}, u32[]{:S(2)}) copy-start(bf16[1024,2048]{1,0:T(8,128)(2,1)} %all-gather.7.cloned.1.call-done) | copy-start | bytes 12582916
  254.9 82.0 %all-gather.11.cloned.1.call-start = ((), (), s32[]{:S(2)}) async-start(), calls=%async_computation.14 | async-start | bytes 5242880 | tf_op jit(solution)/shard_map/all_gather | solution.py:422
  302.3 150.5 %reduce-scatter.11.cloned.1.call-start = ((), (), s32[]{:S(2)}) async-start(), calls=%async_computation.11 | async-start | bytes 5242880 | tf_op jit(solution)/shard_map/reduce_scatter | solution.py:388
  313.3 186.3 %reduce-scatter.23.cloned.1.call-start = ((), (), s32[]{:S(2)}) async-start(), calls=%async_computation.19 | async-start | bytes 6488064 | tf_op jit(solution)/shard_map/reduce_scatter | solution.py:388
  323.9 247.5 %reduce-scatter.19.cloned.1.call-start = ((), (), s32[]{:S(2)}) async-start(), calls=%async_computation.17 | async-start | bytes 2359296 | tf_op jit(solution)/shard_map/reduce_scatter | solution.py:388
  343.1 423.9 %reduce-scatter.21.cloned.1.call-start = ((), (), s32[]{:S(2)}) async-start(), calls=%async_computation.18 | async-start | bytes 12976128 | tf_op jit(solution)/shard_map/reduce_scatter | solution.py:388
  363.0 450.1 %reduce-scatter.15.cloned.1.call-start = ((), (), s32[]{:S(2)}) async-start(), calls=%async_computation.15 | async-start | bytes 5242880 | tf_op jit(solution)/shard_map/reduce_scatter | solution.py:388
  363.0 6.1 copy-start.2
  363.0 6.1 copy-start.4
  363.1 6.0 copy-start.6
  363.1 6.0 copy-start.7
  401.6 10.0 %copy-start.11 = (bf16[1024,2048]{1,0:T(8,128)(2,1)S(1)}, bf16[1024,2048]{1,0:T(8,128)(2,1)}, u32[]{:S(2)}) copy-start(bf16[1024,2048]{1,0:T(8,128)(2,1)} %all-gather.5.cloned.1.call-done) | copy-start | bytes 12582916
  401.6 10.0 %copy-start.16 = (bf16[2048,4]{0,1:T(4,128)(2,1)S(1)}, bf16[2048,4]{0,1:T(4,128)(2,1)}, u32[]{:S(2)}) copy-start(bf16[2048,4]{0,1:T(4,128)(2,1)} %param.17) | copy-start | bytes 49156
  418.5 516.5 %reduce-scatter.17.cloned.1.call-start = ((), (), s32[]{:S(2)}) async-start(), calls=%async_computation.16 | async-start | bytes 7077888 | tf_op jit(solution)/shard_map/reduce_scatter | solution.py:388
  430.3 22.6 %copy-start.13 = (bf16[1024,512]{1,0:T(8,128)(2,1)S(1)}, bf16[1024,512]{1,0:T(8,128)(2,1)}, u32[]{:S(2)}) copy-start(bf16[1024,512]{1,0:T(8,128)(2,1)} %param.12) | copy-start | bytes 3145732
  437.1 5.7 collective-permute-start
  442.8 4.5 collective-permute-start.1
  447.3 5.4 collective-permute-start.2
  452.7 51.2 %collective-permute-start.3 = (f32[4224]{0:T(1024)S(1)}, f32[4224]{0:T(1024)S(1)}, u32[]{:S(2)}, u32[]{:S(2)}) collective-permute-start(f32[4224]{0:T(1024)S(1)} %slice.45), channel_id=1, source_target_pairs={{0,1},{1,0},{2,3},{3,2},{4,5},{5,4},{6,7},{7,6},{8,9},{9,8},{10,11... | collective-permute-start | bytes 50696 | tf_op jit(solution)/shard_map/ppermute | solution.py:382
  455.8 357.2 %copy-start.14 = (bf16[1024,512]{1,0:T(8,128)(2,1)S(1)}, bf16[1024,512]{1,0:T(8,128)(2,1)}, u32[]{:S(2)}) copy-start(bf16[1024,512]{1,0:T(8,128)(2,1)} %param.23) | copy-start | bytes 3145732
  504.0 3.8 collective-permute-start.4
Sparse Core Ops, SparseCore 0:
  9.6 37.1 all-gather.4
  94.9 44.3 reduce-scatter.8
  142.3 34.4 all-gather.6
  178.2 34.4 all-gather.8
  255.1 44.3 reduce-scatter.12
  302.4 34.4 all-gather.10
  339.4 44.4 reduce-scatter.10
  387.6 111.9 reduce-scatter.22
  503.1 68.2 reduce-scatter.18
  574.9 192.1 reduce-scatter.20
  769.5 43.4 reduce-scatter.14
  816.5 118.4 reduce-scatter.16

commit v2 on v1

--- a/solution.py
+++ b/solution.py
@@ -3,6 +3,7 @@
 from jax import lax
 from jax.experimental import pallas as pl
 from jax.experimental.pallas import tpu as pltpu
+from jax.experimental.layout import Layout, with_layout_constraint
 from jax.sharding import PartitionSpec as P
 
 HEAD_DIM = 128
@@ -29,6 +30,11 @@
 
 def column(row):
     return jnp.broadcast_to(row, (CHUNK, CHUNK)).T
+
+
+def logit_row(logit_ref, head, span):
+    values = logit_ref[:, span]
+    return jnp.sum(jnp.where(lax.broadcasted_iota(jnp.int32, values.shape, 0) == head, values, 0.0), axis=0, keepdims=True)
 
 
 def load_segments(seg_ref, segcol, length):
@@ -104,7 +110,7 @@
             q = (acts[0] * lax.rsqrt(jnp.sum(acts[0] * acts[0], axis=-1, keepdims=True) + EPS)).astype(BF16)
             k = (acts[1] * lax.rsqrt(jnp.sum(acts[1] * acts[1], axis=-1, keepdims=True) + EPS)).astype(BF16)
             v = acts[2].astype(BF16).astype(F32)
-            rate = jax.nn.sigmoid(column(logit_ref[h, :, span]))
+            rate = jax.nn.sigmoid(column(logit_row(logit_ref, PAIR * pl.program_id(1) + h, span)))
             gram = jnp.where(same & lower, dot_nt(k, k), 0.0)
             scores = (jnp.where(same & lower_incl, dot_nt(q, k), 0.0) * scale).astype(BF16)
             system = rate * gram
@@ -222,7 +228,7 @@
         for n in reversed(range(chunks)):
             span = slice(n * CHUNK, (n + 1) * CHUNK)
             same, carry, tail, carry_last = state_masks(seg_ref, segcol, n)
-            rate = jax.nn.sigmoid(column(logit_ref[h, :, span]))
+            rate = jax.nn.sigmoid(column(logit_row(logit_ref, PAIR * pair + h, span)))
             start, reach, feed = pieces[n, h]
             k = k_ref[h, span, :]
             delta = delta_ref[span, lanes]
@@ -305,7 +311,7 @@
             pl.BlockSpec((3, length, wide), lambda s, p: (0, s, p)),
             pl.BlockSpec((1, 1, length), lambda s, p: (s, 0, 0)),
             pl.BlockSpec((3, TAPS, wide), lambda s, p: (0, 0, p)),
-            pl.BlockSpec((PAIR, 1, length), lambda s, p: (p, 0, s)),
+            pl.BlockSpec((logits.shape[0], length), lambda s, p: (0, s)),
             pl.BlockSpec((1, HEAD_DIM), lambda s, p: (0, 0)),
         ],
         out_specs=[flat, flat, square, square, square, flat, flat],
@@ -338,7 +344,7 @@
     return pl.pallas_call(
         backward_kernel,
         grid=(heads // PAIR, seqs),
-        in_specs=[cube, pl.BlockSpec((1, 1, length), lambda p, s: (s, 0, 0)), taps, line, vector, flat, square, square, square, flat, flat, flat],
+        in_specs=[cube, pl.BlockSpec((1, 1, length), lambda p, s: (s, 0, 0)), taps, pl.BlockSpec((logits.shape[0], length), lambda p, s: (0, s)), vector, flat, square, square, square, flat, flat, flat],
         out_specs=[cube, line, taps, vector],
         out_shape=[
             jax.ShapeDtypeStruct(proj.shape, BF16),
@@ -361,8 +367,485 @@
     )(proj, seg.reshape(seqs, 1, length), weight, logits, gain.reshape(1, HEAD_DIM), mixed, inverse, scores, states, delta, err, grad_nout)
 
 
+MESH = pl.DeviceIdType.MESH
+ROWS_PER = 128
+
+
+def partners():
+    me = lax.axis_index("tensor")
+    near = me + 1 - 2 * lax.rem(me, 2)
+    far = lax.rem(me + 2, 4)
+    return me, near, far
+
+
+def greet(near, far):
+    barrier = pltpu.get_barrier_semaphore()
+    for other in (near, far):
+        pl.semaphore_signal(barrier, inc=1, device_id={"tensor": other}, device_id_type=MESH)
+    pl.semaphore_wait(barrier, 2)
+
+
+def push(src, dst, send, recv, other):
+    return pltpu.make_async_remote_copy(src_ref=src, dst_ref=dst, send_sem=send, recv_sem=recv, device_id={"tensor": other}, device_id_type=MESH)
+
+
+def band(m):
+    return pl.ds(pl.multiple_of(m * ROWS_PER, ROWS_PER), ROWS_PER)
+
+
+def part_of(q, width):
+    return pl.ds(pl.multiple_of(q * width, width), width)
+
+
+def loop(start, stop, body):
+    lax.fori_loop(start, stop, lambda m, carry: (body(m), carry)[1], 0)
+
+
+def project_kernel(x_ref, gain_ref, rate_ref, weight_ref, full_out, normed_out, proj_out, logit_ref,
+                   full, weight, normed, proj, weight_sem, far_send, far_recv, near_send, near_recv, pass_send, pass_recv, full_sem, normed_sem, proj_sem):
+    me, near, far = partners()
+    width = x_ref.shape[1]
+    chunks = x_ref.shape[0] // ROWS_PER
+    mine, theirs = part_of(me, width), part_of(far, width)
+    load = pltpu.make_async_copy(weight_ref, weight, weight_sem)
+    load.start()
+    greet(near, far)
+
+    def to_far(m):
+        return push(x_ref.at[band(m)], full.at[band(m), mine], far_send.at[m], far_recv.at[m], far)
+
+    def to_near(m):
+        return push(x_ref.at[band(m)], full.at[band(m), mine], near_send.at[m], near_recv.at[m], near)
+
+    def onward(m):
+        return push(full.at[band(m), theirs], full.at[band(m), theirs], pass_send.at[m], pass_recv.at[m], near)
+
+    def out_full(m):
+        return pltpu.make_async_copy(full.at[band(m)], full_out.at[band(m)], full_sem.at[m])
+
+    def out_normed(m):
+        return pltpu.make_async_copy(normed.at[band(m)], normed_out.at[band(m)], normed_sem.at[m])
+
+    def out_proj(m):
+        return pltpu.make_async_copy(proj.at[:, band(m)], proj_out.at[:, band(m)], proj_sem.at[m])
+
+    def begin(m):
+        to_far(m).start()
+        to_near(m).start()
+        full[band(m), mine] = x_ref[band(m), :]
+
+    def compute(m):
+        to_near(m).wait_recv()
+        onward(m).wait_recv()
+        values = full[band(m), :].astype(F32)
+        low = (values * lax.rsqrt(jnp.mean(values * values, axis=-1, keepdims=True) + EPS) * gain_ref[...]).astype(BF16)
+        normed[band(m), :] = low
+        for c in range(3):
+            proj[c, band(m), :] = jnp.dot(low, weight[c], preferred_element_type=F32)
+        logit_ref[:, band(m)] = lax.dot_general(rate_ref[...], low, (((1,), (1,)), ((), ())), preferred_element_type=F32)
+        out_full(m).start()
+        out_normed(m).start()
+        out_proj(m).start()
+
+    def relay(m):
+        to_far(m).wait_recv()
+        onward(m).start()
+
+    def both(m):
+        relay(m)
+        compute(m - 1)
+
+    def finish(m):
+        to_far(m).wait_send()
+        to_near(m).wait_send()
+        onward(m).wait_send()
+        out_full(m).wait()
+        out_normed(m).wait()
+        out_proj(m).wait()
+
+    loop(0, chunks, begin)
+    relay(0)
+    load.wait()
+    loop(1, chunks, both)
+    compute(chunks - 1)
+    loop(0, chunks, finish)
+
+
+def in_vmem():
+    return pl.BlockSpec(memory_space=pltpu.VMEM)
+
+
+def in_hbm():
+    return pl.BlockSpec(memory_space=pl.ANY)
+
+
+def project(hidden_in, gain, rate, weight):
+    tokens, _ = hidden_in.shape
+    wide = weight.shape[1]
+    chunks = tokens // ROWS_PER
+    sems = pltpu.SemaphoreType.DMA((chunks,))
+    return pl.pallas_call(
+        project_kernel,
+        in_specs=[in_vmem(), in_vmem(), in_vmem(), in_hbm()],
+        out_specs=[in_hbm(), in_hbm(), in_hbm(), in_vmem()],
+        out_shape=[
+            jax.ShapeDtypeStruct((tokens, wide), BF16),
+            jax.ShapeDtypeStruct((tokens, wide), BF16),
+            jax.ShapeDtypeStruct((3, tokens, weight.shape[2]), F32),
+            jax.ShapeDtypeStruct((rate.shape[0], tokens), F32),
+        ],
+        scratch_shapes=[
+            pltpu.VMEM((tokens, wide), BF16),
+            pltpu.VMEM(weight.shape, BF16),
+            pltpu.VMEM((tokens, wide), BF16),
+            pltpu.VMEM((3, tokens, weight.shape[2]), F32),
+            pltpu.SemaphoreType.DMA,
+        ] + [sems] * 9,
+        compiler_params=pltpu.CompilerParams(collective_id=0, has_side_effects=True, vmem_limit_bytes=56 << 20),
+        name="project",
+    )(hidden_in, gain.reshape(1, wide), rate, weight)
+
+
+def middle_kernel(low_ref, wout_ref, gain_ref, own_ref, other_ref, x_ref, wdown_ref, wgu_ref,
+                  middle_out, mid_out, normed_out, hidden_out, gate_out, up_out, cot_out,
+                  x_full, cot, wdown, wgu, keep, first, got_first, second, got_second, mid, middle, ghid, normed, acts,
+                  load_sem, cot_send, cot_recv, a_send, a_recv, b_send, b_recv, c_send, c_recv, middle_sem, mid_sem, normed_sem, act_sem, cot_sem):
+    me, near, far = partners()
+    width = own_ref.shape[1]
+    chunks = low_ref.shape[0] // ROWS_PER
+    side, spot = lax.rem(me, 2), lax.div(me, 2)
+    mine, theirs = part_of(me, width), part_of(far, width)
+    loads = [
+        pltpu.make_async_copy(own_ref, cot.at[:, mine], load_sem.at[0]),
+        pltpu.make_async_copy(other_ref, cot.at[:, theirs], load_sem.at[1]),
+        pltpu.make_async_copy(wdown_ref, wdown, load_sem.at[2]),
+        pltpu.make_async_copy(x_ref, x_full, load_sem.at[3]),
+        pltpu.make_async_copy(wgu_ref, wgu, load_sem.at[4]),
+    ]
+    for load in loads:
+        load.start()
+    greet(near, far)
+
+    def send_first(m):
+        return push(first.at[band(m)], got_first.at[band(m)], a_send.at[m], a_recv.at[m], near)
+
+    def send_second(m):
+        return push(second.at[band(m)], got_second.at[band(m)], b_send.at[m], b_recv.at[m], far)
+
+    def share(m, which):
+        at = (mine, theirs)[which]
+        return push(mid.at[band(m), at], mid.at[band(m), at], c_send.at[m, which], c_recv.at[m, which], near)
+
+    def out_middle(m):
+        return pltpu.make_async_copy(middle.at[band(m)], middle_out.at[band(m)], middle_sem.at[m])
+
+    def out_mid(m):
+        return pltpu.make_async_copy(mid.at[band(m)], mid_out.at[band(m)], mid_sem.at[m])
+
+    def out_normed(m):
+        slot = lax.rem(m, 2)
+        return pltpu.make_async_copy(normed.at[slot], normed_out.at[band(m)], normed_sem.at[slot])
+
+    def out_act(m, which):
+        slot = lax.rem(m, 2)
+        return pltpu.make_async_copy(acts.at[slot, which], (hidden_out, gate_out, up_out)[which].at[band(m)], act_sem.at[slot, which])
+
+    def project_out(m):
+        rows = low_ref[band(m), :]
+        for j in range(2):
+            slot = slice(j * width, (j + 1) * width)
+            first[band(m), slot] = jnp.dot(rows, wout_ref[:, part_of(2 * j + 1 - side, width)], preferred_element_type=F32).astype(BF16)
+        send_first(m).start()
+        for j in range(2):
+            slot = slice(j * width, (j + 1) * width)
+            keep[band(m), slot] = jnp.dot(rows, wout_ref[:, part_of(2 * j + side, width)], preferred_element_type=F32)
+
+    def pair_sum(m):
+        send_first(m).wait_recv()
+        second[band(m), :] = (keep[band(m), :] + got_first[band(m), :].astype(F32)).astype(BF16)
+        send_second(m).start()
+
+    def feed(m):
+        project_out(m)
+        pair_sum(m - 1)
+
+    def grad_hidden(m):
+        ghid[band(m), :] = lax.dot_general(cot[band(m), :], wdown[...], (((1,), (1,)), ((), ())), preferred_element_type=F32)
+
+    def total(m):
+        send_second(m).wait_recv()
+        for which, at, slot in ((0, mine, spot), (1, theirs, 1 - spot)):
+            piece = part_of(slot, width)
+            value = x_full[band(m), at].astype(F32) + (second[band(m), piece].astype(F32) + got_second[band(m), piece].astype(F32))
+            if which == 0:
+                middle[band(m), :] = value
+            mid[band(m), at] = value.astype(BF16)
+            share(m, which).start()
+        out_middle(m).start()
+
+    def compute(m):
+        share(m, 0).wait_recv()
+        share(m, 1).wait_recv()
+        out_mid(m).start()
+        slot = lax.rem(m, 2)
+
+        @pl.when(m >= 2)
+        def _():
+            out_normed(m - 2).wait()
+            for which in range(3):
+                out_act(m - 2, which).wait()
+
+        values = mid[band(m), :].astype(F32)
+        low = (values * lax.rsqrt(jnp.mean(values * values, axis=-1, keepdims=True) + EPS) * gain_ref[...]).astype(BF16)
+        normed[slot] = low
+        out_normed(m).start()
+        gate_pre = jnp.dot(low, wgu[0], preferred_element_type=F32)
+        up_pre = jnp.dot(low, wgu[1], preferred_element_type=F32)
+        gate = jax.nn.sigmoid(gate_pre)
+        silu = gate_pre * gate
+        grad = ghid[band(m), :]
+        acts[slot, 0] = (silu * up_pre).astype(BF16)
+        acts[slot, 1] = (grad * up_pre * (gate + silu * (1.0 - gate))).astype(BF16)
+        acts[slot, 2] = (grad * silu).astype(BF16)
+        for which in range(3):
+            out_act(m, which).start()
+
+    def both(m):
+        total(m)
+        compute(m - 1)
+
+    loads[0].wait()
+    loads[1].wait()
+    shares = [push(cot.at[:, at], cot.at[:, at], cot_send.at[i], cot_recv.at[i], near) for i, at in enumerate((mine, theirs))]
+    project_out(0)
+    loop(1, chunks, feed)
+    pair_sum(chunks - 1)
+    for copy in shares:
+        copy.start()
+    loads[2].wait()
+    loads[3].wait()
+    for copy in shares:
+        copy.wait_recv()
+    save = pltpu.make_async_copy(cot, cot_out, cot_sem)
+    save.start()
+    loop(0, chunks, grad_hidden)
+    loads[4].wait()
+    total(0)
+    loop(1, chunks, both)
+    compute(chunks - 1)
+
+    def finish(m):
+        send_first(m).wait_send()
+        send_second(m).wait_send()
+        share(m, 0).wait_send()
+        share(m, 1).wait_send()
+        out_middle(m).wait()
+        out_mid(m).wait()
+
+    for m in (chunks - 2, chunks - 1):
+        out_normed(m).wait()
+        for which in range(3):
+            out_act(m, which).wait()
+    for copy in shares:
+        copy.wait_send()
+    save.wait()
+    loop(0, chunks, finish)
+
+
+def middle_step(out_low, wout, gain, cot_own, cot_far, full_in, wdown, wgu):
+    tokens, width = cot_own.shape
+    wide, units = wgu.shape[1], wgu.shape[2]
+    chunks = tokens // ROWS_PER
+    dma = pltpu.SemaphoreType.DMA
+    half = (tokens, wide // 2)
+    return pl.pallas_call(
+        middle_kernel,
+        in_specs=[in_vmem(), in_vmem(), in_vmem()] + [in_hbm()] * 5,
+        out_specs=[in_hbm()] * 7,
+        out_shape=[
+            jax.ShapeDtypeStruct((tokens, width), F32),
+            jax.ShapeDtypeStruct((tokens, wide), BF16),
+            jax.ShapeDtypeStruct((tokens, wide), BF16),
+            jax.ShapeDtypeStruct((tokens, units), BF16),
+            jax.ShapeDtypeStruct((tokens, units), BF16),
+            jax.ShapeDtypeStruct((tokens, units), BF16),
+            jax.ShapeDtypeStruct((tokens, wide), BF16),
+        ],
+        scratch_shapes=[
+            pltpu.VMEM((tokens, wide), BF16),
+            pltpu.VMEM((tokens, wide), BF16),
+            pltpu.VMEM(wdown.shape, BF16),
+            pltpu.VMEM(wgu.shape, BF16),
+            pltpu.VMEM(half, F32),
+            pltpu.VMEM(half, BF16),
+            pltpu.VMEM(half, BF16),
+            pltpu.VMEM(half, BF16),
+            pltpu.VMEM(half, BF16),
+            pltpu.VMEM((tokens, wide), BF16),
+            pltpu.VMEM((tokens, width), F32),
+            pltpu.VMEM((tokens, units), F32),
+            pltpu.VMEM((2, ROWS_PER, wide), BF16),
+            pltpu.VMEM((2, 3, ROWS_PER, units), BF16),
+            dma((5,)), dma((2,)), dma((2,)),
+            dma((chunks,)), dma((chunks,)), dma((chunks,)), dma((chunks,)),
+            dma((chunks, 2)), dma((chunks, 2)),
+            dma((chunks,)), dma((chunks,)), dma((2,)), dma((2, 3)), dma,
+        ],
+        compiler_params=pltpu.CompilerParams(collective_id=1, has_side_effects=True, vmem_limit_bytes=62 << 20),
+        name="middle_step",
+    )(out_low, wout, gain.reshape(1, wide), cot_own, cot_far, full_in, wdown, wgu)
+
+
+def return_kernel(wout_ref, gain_ref, gate_ref, up_ref, mid_ref, cot_ref, wgu_ref,
+                  gmid_out, full_out, nout_out, sum_ref,
+                  gate, up, mid, cot, wgu, piece, keep, first, got_first, second, got_second, full, gmid, nout,
+                  load_sem, a_send, a_recv, b_send, b_recv, c_send, c_recv, gmid_sem, full_sem, nout_sem):
+    me, near, far = partners()
+    width = gmid.shape[1]
+    chunks = gmid.shape[0] // ROWS_PER
+    side, spot = lax.rem(me, 2), lax.div(me, 2)
+    mine, theirs = part_of(me, width), part_of(far, width)
+    loads = [
+        pltpu.make_async_copy(gate_ref, gate, load_sem.at[0]),
+        pltpu.make_async_copy(wgu_ref.at[0], wgu.at[0], load_sem.at[1]),
+        pltpu.make_async_copy(up_ref, up, load_sem.at[2]),
+        pltpu.make_async_copy(wgu_ref.at[1], wgu.at[1], load_sem.at[3]),
+        pltpu.make_async_copy(mid_ref, mid, load_sem.at[4]),
+        pltpu.make_async_copy(cot_ref, cot, load_sem.at[5]),
+    ]
+    for load in loads:
+        load.start()
+    greet(near, far)
+    sum_ref[...] = jnp.zeros_like(sum_ref)
+
+    def send_first(m):
+        return push(first.at[band(m)], got_first.at[band(m)], a_send.at[m], a_recv.at[m], near)
+
+    def send_second(m):
+        return push(second.at[band(m)], got_second.at[band(m)], b_send.at[m], b_recv.at[m], far)
+
+    def share(m, which):
+        at = (mine, theirs)[which]
+        return push(full.at[band(m), at], full.at[band(m), at], c_send.at[m, which], c_recv.at[m, which], near)
+
+    def outs(m):
+        return [
+            pltpu.make_async_copy(gmid.at[band(m)], gmid_out.at[band(m)], gmid_sem.at[m]),
+            pltpu.make_async_copy(full.at[band(m)], full_out.at[band(m)], full_sem.at[m]),
+            pltpu.make_async_copy(nout.at[band(m)], nout_out.at[band(m)], nout_sem.at[m]),
+        ]
+
+    def partial(m):
+        dims = (((1,), (1,)), ((), ()))
+        grad = lax.dot_general(gate[band(m), :], wgu[0], dims, preferred_element_type=F32)
+        grad = grad + lax.dot_general(up[band(m), :], wgu[1], dims, preferred_element_type=F32)
+        values = mid[band(m), :].astype(F32)
+        scale = lax.rsqrt(jnp.mean(values * values, axis=-1, keepdims=True) + EPS)
+        unit = values * scale
+        sum_ref[...] += jnp.sum(grad * unit, axis=0, keepdims=True)
+        scaled = grad * gain_ref[...]
+        piece[...] = scale * (scaled - unit * jnp.mean(scaled * unit, axis=-1, keepdims=True))
+        for j in range(2):
+            slot = slice(j * width, (j + 1) * width)
+            first[band(m), slot] = piece[:, part_of(2 * j + 1 - side, width)].astype(BF16)
+            keep[band(m), slot] = piece[:, part_of(2 * j + side, width)]
+        send_first(m).start()
+
+    def pair_sum(m):
+        send_first(m).wait_recv()
+        second[band(m), :] = (keep[band(m), :] + got_first[band(m), :].astype(F32)).astype(BF16)
+        send_second(m).start()
+
+    def feed(m):
+        partial(m)
+        pair_sum(m - 1)
+
+    def total(m):
+        send_second(m).wait_recv()
+        for which, at, slot in ((0, mine, spot), (1, theirs, 1 - spot)):
+            part = part_of(slot, width)
+            value = cot[band(m), at].astype(F32) + (second[band(m), part].astype(F32) + got_second[band(m), part].astype(F32))
+            if which == 0:
+                gmid[band(m), :] = value
+            full[band(m), at] = value.astype(BF16)
+            share(m, which).start()
+        outs(m)[0].start()
+
+    def compute(m):
+        share(m, 0).wait_recv()
+        share(m, 1).wait_recv()
+        outs(m)[1].start()
+        nout[band(m), :] = lax.dot_general(full[band(m), :], wout_ref[...], (((1,), (1,)), ((), ())), preferred_element_type=F32)
+        outs(m)[2].start()
+
+    def both(m):
+        total(m)
+        compute(m - 1)
+
+    def finish(m):
+        send_first(m).wait_send()
+        send_second(m).wait_send()
+        share(m, 0).wait_send()
+        share(m, 1).wait_send()
+        for copy in outs(m):
+            copy.wait()
+
+    for load in loads[:5]:
+        load.wait()
+    partial(0)
+    loop(1, chunks, feed)
+    pair_sum(chunks - 1)
+    loads[5].wait()
+    total(0)
+    loop(1, chunks, both)
+    compute(chunks - 1)
+    loop(0, chunks, finish)
+
+
+def return_step(wout, gain, grad_gate, grad_up, full_mid, full_cot, wgu):
+    tokens, wide = full_mid.shape
+    units = wgu.shape[2]
+    width = wide // 4
+    chunks = tokens // ROWS_PER
+    dma = pltpu.SemaphoreType.DMA
+    half = (tokens, wide // 2)
+    return pl.pallas_call(
+        return_kernel,
+        in_specs=[in_vmem(), in_vmem()] + [in_hbm()] * 5,
+        out_specs=[in_hbm()] * 3 + [in_vmem()],
+        out_shape=[
+            jax.ShapeDtypeStruct((tokens, width), F32),
+            jax.ShapeDtypeStruct((tokens, wide), BF16),
+            jax.ShapeDtypeStruct((tokens, wout.shape[0]), F32),
+            jax.ShapeDtypeStruct((1, wide), F32),
+        ],
+        scratch_shapes=[
+            pltpu.VMEM((tokens, units), BF16),
+            pltpu.VMEM((tokens, units), BF16),
+            pltpu.VMEM((tokens, wide), BF16),
+            pltpu.VMEM((tokens, wide), BF16),
+            pltpu.VMEM(wgu.shape, BF16),
+            pltpu.VMEM((ROWS_PER, wide), F32),
+            pltpu.VMEM(half, F32),
+            pltpu.VMEM(half, BF16),
+            pltpu.VMEM(half, BF16),
+            pltpu.VMEM(half, BF16),
+            pltpu.VMEM(half, BF16),
+            pltpu.VMEM((tokens, wide), BF16),
+            pltpu.VMEM((tokens, width), F32),
+            pltpu.VMEM((tokens, wout.shape[0]), F32),
+            dma((6,)),
+            dma((chunks,)), dma((chunks,)), dma((chunks,)), dma((chunks,)),
+            dma((chunks, 2)), dma((chunks, 2)),
+            dma((chunks,)), dma((chunks,)), dma((chunks,)),
+        ],
+        compiler_params=pltpu.CompilerParams(collective_id=2, has_side_effects=True, vmem_limit_bytes=62 << 20),
+        name="return_step",
+    )(wout, gain.reshape(1, wide), grad_gate, grad_up, full_mid, full_cot, wgu)
+
+
+PLAIN = (((1,), (0,)), ((), ()))
 ROWS = (((0,), (0,)), ((), ()))
-COLS = (((1,), (1,)), ((), ()))
 
 
 def rms_scale(values):
@@ -384,77 +867,166 @@
     return values
 
 
-def scatter_sum(values, axis, dim):
-    return lax.psum_scatter(values.astype(BF16), axis, scatter_dimension=dim, tiled=True).astype(F32)
+def row_major(values):
+    return with_layout_constraint(values, Layout(tuple(range(values.ndim))))
+
+
+def tie(value, token):
+    return value if token is None else lax.optimization_barrier((value, token))[0]
+
+
+class Timeline:
+    def __init__(self, size):
+        self.size = size
+        self.bits = size.bit_length() - 1
+        self.token = None
+        self.open = {}
+
+    def after(self, value):
+        return tie(value, self.token)
+
+    def swap(self, values, bit):
+        return lax.ppermute(values, "dp", [(i, i ^ (1 << bit)) for i in range(self.size)])
+
+    def scatter(self, name, grad, order=()):
+        order = list(order) + [bit for bit in range(self.bits) if bit not in order]
+        blocks = row_major(grad.astype(BF16)).reshape((2,) * self.bits + (grad.shape[0] // self.size, grad.shape[1]))
+        self.open[name] = ([blocks], list(range(self.bits))[::-1], order, 0)
+        self.move(name)
+
+    def move(self, name):
+        terms, axes, order, stage = self.open[name]
+        bit = order[stage]
+        own = lax.rem(lax.div(lax.axis_index("dp"), 1 << bit), 2)
+        axis = axes.index(bit)
+        if stage:
+            terms = terms[:-1] + [self.after(terms[-1])]
+
+        def pick(value, at):
+            return lax.dynamic_index_in_dim(value, at, axis, keepdims=False)
+
+        away = pick(terms[0], 1 - own) if stage == 0 else sum(pick(t, 1 - own).astype(F32) for t in terms).astype(BF16)
+        away = row_major(away)
+        self.token = away
+        came = self.swap(away, bit)
+        self.open[name] = ([pick(t, own) for t in terms] + [came], axes[:axis] + axes[axis + 1 :], order, stage + 1)
+
+    def close(self, name):
+        while self.open[name][3] < self.bits:
+            self.move(name)
+        terms = self.open.pop(name)[0]
+        terms = terms[:-1] + [self.after(terms[-1])]
+        return row_major(sum(t.astype(F32) for t in terms))
 
 
 def make_body(dp_size, tensor_size):
     def body(hidden_in, seg_ids, attn_gain, wqkv, conv_weight, wrate, onorm_gain, wout, mlp_gain, wgu, wdown, cotangent):
-        tokens = hidden_in.shape[0]
+        return step(hidden_in, seg_ids, attn_gain, wqkv, conv_weight, wrate, onorm_gain, wout, mlp_gain, wgu, wdown, cotangent)
+
+    def step(hidden_in, seg_ids, attn_gain, wqkv, conv_weight, wrate, onorm_gain, wout, mlp_gain, wgu, wdown, cotangent):
+        tokens, width = hidden_in.shape
         heads = wrate.shape[1]
-        dot = lambda a, b, dims: lax.dot_general(a, b, dims, preferred_element_type=F32)
+        me = lax.axis_index("tensor")
+        side, spot = lax.rem(me, 2), lax.div(me, 2)
+
+        def dot(a, b, dims):
+            return lax.dot_general(a, b, dims, preferred_element_type=F32)
+
+        def swap(values, step):
+            return lax.ppermute(values, "tensor", [(i, i ^ step) for i in range(tensor_size)])
+
+        def columns(values, q):
+            return lax.dynamic_slice_in_dim(values, q * width, width, 1)
+
+        def quarter_sum(pick):
+            away = jnp.concatenate([pick(2 * j + 1 - side).astype(BF16) for j in range(2)], axis=1)
+            came = swap(away, 1)
+            other = (pick(lax.rem(me + 2, 4)) + columns(came, 1 - spot).astype(F32)).astype(BF16)
+            far = swap(other, 2)
+            return pick(me) + columns(came, spot).astype(F32), far
+
         taps = conv_weight.astype(F32)
-        full_in = lax.all_gather(hidden_in, "tensor", axis=1, tiled=True).astype(F32)
+        rates = jnp.zeros((8, wrate.shape[0]), BF16).at[:heads].set(wrate.T)
+        full_low, normed_one, proj, logits = project(hidden_in, attn_gain, rates, wqkv)
+        cot_own, _ = lax.optimization_barrier((cotangent, logits))
+        cot_far = swap(cot_own, 2)
+        out_low, *kept = mixer_forward(proj, seg_ids, taps, logits, onorm_gain)
+        middle, mid_low, normed_two, hidden, grad_gate, grad_up, full_cot = middle_step(out_low, wout, mlp_gain, cotangent, cot_far, full_low, wdown, wgu)
+        line = Timeline(dp_size)
+        line.scatter("down", dot(full_cot, hidden, ROWS))
+        line.scatter("gate", dot(normed_two, line.after(grad_gate), ROWS), (1,))
+        line.scatter("up", dot(normed_two, line.after(grad_up), ROWS))
+        late_gate = line.after(grad_gate)
+        grad_middle, full_grad_mid, grad_nout, gain_two = return_step(wout, mlp_gain, late_gate, grad_up, mid_low, full_cot, wgu)
+        line.scatter("out", dot(full_grad_mid, out_low, ROWS))
+        line.move("gate")
+        line.move("down")
+        grad_proj, grad_logits, grad_conv, gain_onorm = mixer_backward(proj, seg_ids, taps, logits, onorm_gain, kept, line.after(grad_nout))
+        line.token = grad_logits
+        grad_logits = grad_logits.reshape(heads, tokens)
+        line.move("up")
+        line.move("down")
+        late_low, late_proj = line.after((full_low, grad_proj))
+        grad_nin = jnp.einsum("ctk,cdk->td", late_proj, wqkv, preferred_element_type=F32)
+        grad_nin = grad_nin + jnp.einsum("ht,dh->td", grad_logits, wrate, preferred_element_type=F32)
+        full_in = late_low.astype(F32)
         scale_one = rms_scale(full_in)
-        unit_one = full_in * scale_one
-        normed_one = (unit_one * attn_gain).astype(BF16)
-        proj = jnp.einsum("td,cdk->ctk", normed_one, wqkv, preferred_element_type=F32)
-        logits = jnp.einsum("td,dh->ht", normed_one, wrate, preferred_element_type=F32).reshape(heads, 1, tokens)
-        out_low, *kept = mixer_forward(proj, seg_ids, taps, logits, onorm_gain)
-        attn_part = jnp.dot(out_low, wout, preferred_element_type=F32)
-        middle = hidden_in.astype(F32) + scatter_sum(attn_part, "tensor", 1)
-        full_mid = lax.all_gather(middle.astype(BF16), "tensor", axis=1, tiled=True).astype(F32)
-        full_cot = lax.all_gather(cotangent, "tensor", axis=1, tiled=True)
-        scale_two = rms_scale(full_mid)
-        unit_two = full_mid * scale_two
-        normed_two = (unit_two * mlp_gain).astype(BF16)
-        gate_up = jnp.einsum("td,cdf->ctf", normed_two, wgu, preferred_element_type=F32)
-        gate_pre, up_pre = gate_up[0], gate_up[1]
-        gate_sig = jax.nn.sigmoid(gate_pre)
-        hidden = (gate_pre * gate_sig * up_pre).astype(BF16)
-        grad_hidden = dot(full_cot, wdown, COLS)
-        grad_up = grad_hidden * gate_pre * gate_sig
-        grad_gate = grad_hidden * up_pre * gate_sig * (1.0 + gate_pre * (1.0 - gate_sig))
-        grad_pair = jnp.stack([grad_gate, grad_up]).astype(BF16)
-        grad_nmid = jnp.einsum("ctf,cdf->td", grad_pair, wgu, preferred_element_type=F32)
-        part_two, gain_two = norm_back(grad_nmid, unit_two, scale_two, mlp_gain)
-        grad_middle = cotangent.astype(F32) + scatter_sum(part_two, "tensor", 1)
-        full_grad_mid = lax.all_gather(grad_middle.astype(BF16), "tensor", axis=1, tiled=True)
-        grad_down = dot(hidden, full_cot, ROWS)
-        grad_gate_up = jnp.einsum("td,ctf->cdf", normed_two, grad_pair, preferred_element_type=F32)
-        ffn_part = jnp.dot(hidden, wdown, preferred_element_type=F32)
-        layer_out = (middle + scatter_sum(ffn_part, "tensor", 1)).astype(BF16)
-        grad_nout = dot(full_grad_mid, wout, COLS)
-        grad_out = dot(out_low, full_grad_mid, ROWS)
-        grad_proj, grad_logits, grad_conv, gain_onorm = mixer_backward(proj, seg_ids, taps, logits, onorm_gain, kept, grad_nout)
-        grad_logits = grad_logits.reshape(heads, tokens)
-        grad_nin = jnp.einsum("ctk,cdk->td", grad_proj, wqkv, preferred_element_type=F32)
-        grad_nin = grad_nin + jnp.einsum("ht,dh->td", grad_logits, wrate, preferred_element_type=F32)
-        grad_qkv = jnp.einsum("td,ctk->cdk", normed_one, grad_proj, preferred_element_type=F32)
-        grad_beta = jnp.einsum("td,ht->dh", normed_one, grad_logits, preferred_element_type=F32)
-        part_one, gain_one = norm_back(grad_nin, unit_one, scale_one, attn_gain)
-        grad_in = (grad_middle + scatter_sum(part_one, "tensor", 1)).astype(BF16)
-        width = gain_one.shape[0]
-        flat = jnp.concatenate([gain_one, gain_two, gain_onorm.reshape(-1), grad_conv.reshape(-1), grad_beta.reshape(-1)])
-        shared = 2 * width + HEAD_DIM
-        flat = butterfly(flat, "dp", dp_size)
-        gains = butterfly(flat[:shared], "tensor", tensor_size)
-        grad_conv = flat[shared : shared + grad_conv.size].reshape(grad_conv.shape)
+        part_one, gain_one = norm_back(grad_nin, full_in * scale_one, scale_one, attn_gain)
+        part_one = part_one.astype(BF16)
+        line.token = (part_one, gain_one)
+        wide = gain_one.shape[0]
+        grad_beta = jnp.einsum("td,ht->dh", normed_one, line.after(grad_logits), preferred_element_type=F32)
+        gains = butterfly(jnp.concatenate([gain_one, gain_two.reshape(-1), gain_onorm.reshape(-1)]), "tensor", tensor_size)
+        shared = gains.shape[0]
+        line.move("gate")
+        line.scatter("k", dot(normed_one, line.after(grad_proj[1]), ROWS), (1,))
+        small = jnp.concatenate([gains, grad_conv.reshape(-1), grad_beta.reshape(-1)])
+        small_came = line.swap(small, 0)
+        line.scatter("v", dot(normed_one, line.after(grad_proj[2]), ROWS))
+        line.scatter("q", dot(normed_one, line.after(grad_proj[0]), ROWS))
+        one, one_far = quarter_sum(lambda q: columns(part_one, q).astype(F32))
+        line.move("up")
+        late_hidden = line.after(hidden)
+        ffn, ffn_far = quarter_sum(lambda q: dot(late_hidden, columns(wdown, q), PLAIN))
+        line.move("out")
+        grad_down = line.close("down").T
+        small = small + line.after(small_came)
+        small_came = line.swap(small, 1 % line.bits)
+        line.move("k")
+        line.move("out")
+        grad_gate_w = line.close("gate")
+        line.move("v")
+        grad_up_w = line.close("up")
+        small = small + line.after(small_came)
+        small_came = line.swap(small, 2 % line.bits)
+        grad_in = (grad_middle + one + line.after(one_far).astype(F32)).astype(BF16)
+        layer_out = (middle + ffn + line.after(ffn_far).astype(F32)).astype(BF16)
+        line.move("q")
+        line.move("v")
+        line.move("k")
+        line.move("q")
+        small = small + line.after(small_came)
+        for bit in range(3, line.bits):
+            small = small + line.swap(small, bit)
+        grad_out = line.close("out").T
+        grad_qkv = [line.close(n) for n in "qkv"]
+        gains = small[:shared]
+        grad_conv = small[shared : shared + grad_conv.size].reshape(grad_conv.shape)
         mine = grad_beta.shape[0] // dp_size
-        grad_beta = flat[shared + grad_conv.size :].reshape(grad_beta.shape)
+        grad_beta = small[shared + grad_conv.size :].reshape(grad_beta.shape)
         grad_beta = lax.dynamic_slice_in_dim(grad_beta, lax.axis_index("dp") * mine, mine, 0)
         return (
             layer_out,
             grad_in,
-            gains[:width],
-            scatter_sum(grad_qkv, "dp", 1),
+            gains[:wide],
+            jnp.stack(grad_qkv),
             grad_conv,
             grad_beta,
-            gains[2 * width :],
-            scatter_sum(grad_out, "dp", 1),
-            gains[width : 2 * width],
-            scatter_sum(grad_gate_up, "dp", 1),
-            scatter_sum(grad_down, "dp", 1),
+            gains[2 * wide :],
+            grad_out,
+            gains[wide : 2 * wide],
+            jnp.stack([grad_gate_w, grad_up_w]),
+            grad_down,
         )
 
     return body

time: 954 us -> 507 us (0.53)
  waiting for transfers between devices: 660 us -> 89.1 us
  Pallas kernels: 55.9 us -> 214 us
  matrix products: 155 us -> 59.7 us
  starting transfers between devices: 8.17 us -> 37 us
  other arithmetic: 32.6 us -> 60.5 us
  local copies, waits for them, and re-layouts: 18.1 us -> 35.8 us
  between operations: 15 us -> 1.56 us
    reduce_scatter x8 -> x0, waiting for transfers between devices: 551 us -> none  [scatter_sum(): lax.psum_scatter(values.astype(BF16), axis, scatter_dimension=dim, tiled=...]
    pallas_call x0 -> x3, Pallas kernels: none -> 158 us  [the longest x1 66.8 us: return_step(): pl.pallas_call(return_kernel, in_specs=[in_vmem(), in_vmem()] + [in_hbm()...]
    all_gather x4 -> x0, waiting for transfers between devices: 98 us -> none  [the longest x1 37.4 us: body(): lax.all_gather(hidden_in, 'tensor', axis=1, tiled=True).astype(F32)]
    dot_general x15 -> x14, matrix products: 155 us -> 59.7 us  [the longest x11 48.5 us: dot(): return lax.dot_general(a, b, dims, preferred_element_type=F32)]
    ppermute x0 -> x29, waiting for transfers between devices: none -> 88.7 us  [the longest x24 72.6 us: swap(): lax.ppermute(values, 'dp', [(i, i ^ 1 << bit) for i in range(self.size)])]
    ppermute x0 -> x29, starting transfers between devices: none -> 35.8 us  [the longest x24 31.9 us: swap(): lax.ppermute(values, 'dp', [(i, i ^ 1 << bit) for i in range(self.size)])]
    convert_element_type x9 -> x19, other arithmetic: 26.2 us -> 39.8 us  [the longest x14 29.3 us: move(): sum((pick(t, 1 - own).astype(F32) for t in terms)).astype(BF16)]
    squeeze x0 -> x8, local copies, waits for them, and re-layouts: none -> 11.2 us  [the longest x7 10.1 us: pick(): return lax.dynamic_index_in_dim(value, at, axis, keepdims=False)]
  transfers between devices with their start and end apart: 17 -> 31, of which waited for: 15 -> 10; matrix products, arithmetic and copies ran while one was open for 14% -> 24% of each run, Pallas kernels for 3% -> 25%
where the time goes in v2:
time: 507 us; the launch traced here: 498 us
  Pallas kernels  214 us (42%)
  waiting for transfers between devices  89.1 us (18%)
  other arithmetic  60.5 us (12%)
  matrix products  59.7 us (12%)
  starting transfers between devices  37 us (7%)
  local copies, waits for them, and re-layouts  35.8 us (7%)
    ppermute x24, waiting for transfers between devices, swap(): lax.ppermute(values, 'dp', [(i, i ^ 1 << bit) for i in range(self.size)])  72.6 us
    pallas_call x1, Pallas kernels, return_step(): pl.pallas_call(return_kernel, in_specs=[in_vmem(), in_vmem()] + [in_hbm()...  66.8 us
    pallas_call x1, Pallas kernels, middle_step(): pl.pallas_call(middle_kernel, in_specs=[in_vmem(), in_vmem(), in_vmem()]...  58.7 us
    dot_general x11, matrix products, dot(): return lax.dot_general(a, b, dims, preferred_element_type=F32)  48.5 us
    pallas_call x1, Pallas kernels, project(): pl.pallas_call(project_kernel, in_specs=[in_vmem(), in_vmem(), in_vmem(),...  32.8 us
    pallas_call x1, Pallas kernels, mixer_backward(): pl.pallas_call(backward_kernel, grid=(heads // PAIR, seqs), in_specs=[cub...  32.5 us
    ppermute x24, starting transfers between devices, swap(): lax.ppermute(values, 'dp', [(i, i ^ 1 << bit) for i in range(self.size)])  31.9 us
    convert_element_type x14, other arithmetic, move(): sum((pick(t, 1 - own).astype(F32) for t in terms)).astype(BF16)  29.3 us
  transfers between devices with their start and end apart: 31, of which 10 were waited for; matrix products, arithmetic and copies ran while one was open for 24% of the time, Pallas kernels for 25%

profile of v2, /device:TPU:0, one launch (start us, length us, event | category | flops | bytes accessed | tf_op | source)
XLA Modules:
  0.0 498.1 jit_solution(14502527747076040159)
XLA Ops:
  2.0 32.8 %project.1 = (bf16[1024,2048]{1,0:T(8,128)(2,1)}, bf16[1024,2048]{1,0:T(8,128)(2,1)}, f32[3,1024,512]{2,1,0:T(8,128)}, f32[8,1024]{1,0:T(8,128)}) custom-call(bf16[1024,512]{1,0:T(8,128)(2,1)} %x_ref.1, f32[1,2048]{1,0:T(1,128)} %bitcast.285, bf16[8,2048]{1,0:T(8,128)(2,1)} %scatter.4.rate_ref, bf16[3,2048,512]{2,1,0:T(8,128)(2,1)} %weight_ref.1), custom_call_target="tpu_custom_call" | custom-call | tf_op jit(solution)/shard_map/project/pallas_call | solution.py:487
  36.7 23.4 %mixer_forward.1 = (bf16[1024,512]{1,0:T(8,128)(2,1)S(1)}, f32[1024,512]{1,0:T(8,128)}, bf16[4,1024,128]{2,1,0:T(8,128)(2,1)S(1)}, bf16[4,1024,128]{2,1,0:T(8,12...) custom-call(f32[3,1024,512]{2,1,0:T(8,128)} %get-tuple-element.87.proj_ref,, ...), custom_call_target="tpu_custom_call" | custom-call | tf_op jit(solution)/shard_map/mixer_forward/pallas_call | solution.py:307
  64.1 58.7 %middle_step.1 = (f32[1024,512]{1,0:T(8,128)}, bf16[1024,2048]{1,0:T(8,128)(2,1)}, bf16[1024,2048]{1,0:T(8,128)(2,1)}, bf16[1024,1408]{1,0:T(8,128)(2,1)}, bf16[...) custom-call(bf16[1024,512]{1,0:T(8,128)(2,1)} %copy-done.7, ...), custom_call_target="tpu_custom_call" | custom-call | tf_op jit(solution)/shard_map/middle_step/pallas_call | solution.py:661
  122.9 9.6 %convolution_convert_fusion.2 = bf16[2048,1408]{1,0:T(8,128)(2,1)S(1)} fusion(bf16[1024,2048]{1,0:T(8,128)(2,1)} %get-tuple-element.97.cot_ref, bf16[1024,1408]{1,0:T(8,128)(2,1)} %get-tuple-element.125), kind=kOutput, calls=%fused_computation.14 | convolution fusion | flops 5908463616 | bytes 12845056 | tf_op jit(solution)/shard_map/dot_general | solution.py:933
  132.5 1.8 dynamic-slice_bitcast_fusion.2
  134.3 2.0 copy-done.15
  136.3 1.5 collective-permute-start.2
  137.8 7.1 %convolution_convert_fusion.1 = bf16[2048,1408]{1,0:T(8,128)(2,1)S(1)} fusion(bf16[1024,2048]{1,0:T(8,128)(2,1)S(1)} %copy-done.44, bf16[1024,1408]{1,0:T(8,128)(2,1)S(1)} %copy-done.18), kind=kOutput, calls=%fused_computation.13 | convolution fusion | flops 5908463616 | bytes 12845056 | tf_op jit(solution)/shard_map/dot_general | solution.py:933
  144.9 1.8 dynamic-slice_bitcast_fusion.1
  146.7 2.0 copy-done.14
  148.7 1.6 collective-permute-start.3
  150.3 7.2 %convolution_convert_fusion = bf16[2048,1408]{1,0:T(8,128)(2,1)S(1)} fusion(bf16[1024,2048]{1,0:T(8,128)(2,1)S(1)} %copy-done.44, bf16[1024,1408]{1,0:T(8,128)(2,1)S(1)} %copy-done.19), kind=kOutput, calls=%fused_computation.12 | convolution fusion | flops 5908463616 | bytes 12845056 | tf_op jit(solution)/shard_map/dot_general | solution.py:933
  157.6 2.1 dynamic-slice_bitcast_fusion
  161.5 66.8 %return_step.1 = (f32[1024,512]{1,0:T(8,128)}, bf16[1024,2048]{1,0:T(8,128)(2,1)}, f32[1024,512]{1,0:T(8,128)}, f32[1,2048]{1,0:T(1,128)}) custom-call(bf16[512,2048]{1,0:T(8,128)(2,1)} %wout_ref.3, f32[1,2048]{1,0:T(1,128)} %bitcast.290, bf16[1024,1408]{1,0:T(8,128)(2,1)} %get-tuple-element.106.gate_ref, bf16[1024,1408]{1,0:T(8,128)(2,1)} %get-tuple-element.99.up_ref, ...), custom_call_target="tpu_custom_call" | custom-call | tf_op jit(solution)/shard_map/return_step/pallas_call | solution.py:812
  228.3 4.9 convolution_convert_fusion.6
  234.3 3.2 fusion.11
  237.6 3.3 fusion.10
  247.1 32.5 %mixer_backward.1 = (bf16[3,1024,512]{2,1,0:T(8,128)(2,1)}, bf16[4,1,1024]{2,1,0:T(2,128)(2,1)S(1)}, f32[3,4,512]{2,1,0:T(4,128)S(1)}, f32[1,128]{1,0:T(1,128)S(1)}) custom-call(f32[3,1024,512]{2,1,0:T(8,128)} %get-tuple-element.87.proj_ref, s32[2,1,512]{2,1,0:T(1,128)S(1)} %reshape.321.seg_ref, f32[3,4,512]{2,1,0:T(4,128)S(1)} %convert_element_type.475.weight_ref, ...), custom_call_target="tpu_custom_call" | custom-call | tf_op jit(solution)/shard_map/mixer_backward/pallas_call | solution.py:344
  279.6 2.3 fusion.9
  281.9 1.6 collective-permute-start.4
  285.4 2.7 fusion.20
  288.0 2.6 collective-permute-start.30
  290.6 6.7 %fusion.52 = f32[1024,2048,1]{1,0,2:T(8,128)S(1)} fusion(bf16[3,1024,512]{2,1,0:T(8,128)(2,1)S(1)} %copy-done.17, bf16[3,2048,512]{2,1,0:T(8,128)(2,1)S(1)} %bitcast.252), kind=kOutput, calls=%fused_computation.123 | convolution fusion | flops 6442450944 | bytes 17825792 | tf_op jit(solution)/shard_map/ctk,cdk->td/dot_general | solution.py:970
  298.3 3.2 fusion.7
  301.5 2.2 fusion.6
  303.8 12.4 %collective-permute-done.5 = bf16[2,256,1408]{2,1,0:T(8,128)(2,1)} collective-permute-done((bf16[2,256,1408]{2,1,0:T(8,128)(2,1)}, bf16[2,256,1408]{2,1,0:T(8,128)(2,1)}, u32[]{:S(2)}, u32[]{:S(2)}) %collective-permute-start.5) | collective-permute-done | bytes 1441824 | tf_op jit(solution)/shard_map/ppermute | solution.py:889
  316.2 2.7 fusion.19
  318.9 2.6 collective-permute-start.28
  321.5 2.5 convolution_convert_fusion.5
  325.1 1.6 collective-permute-start.12
  326.7 2.5 convolution_convert_fusion.4
  331.6 2.5 convolution_convert_fusion.3
  335.2 1.5 collective-permute-start.9
  336.7 2.7 fusion.18
  339.4 2.0 fusion.30
  343.2 2.8 convolution_convert_fusion.8
  346.0 2.8 convolution_convert_fusion.7
  348.7 3.4 fusion.25
  353.5 1.7 pad_maximum_fusion.2
  357.0 3.1 pad_maximum_fusion.1
  362.5 2.1 fusion.13
  364.6 1.5 copy.46
  366.1 19.3 %collective-permute-done.12 = bf16[2,2,256,512]{3,2,1,0:T(8,128)(2,1)} collective-permute-done((bf16[2,2,256,512]{3,2,1,0:T(8,128)(2,1)}, bf16[2,2,256,512]{3,2,1,0:T(8,128)(2,1)}, u32[]{:S(2)}, u32[]{:S(2)}) %collective-permute-start.12) | collective-permute-done | bytes 1048608 | tf_op jit(solution)/shard_map/ppermute | solution.py:889
  385.4 1.5 collective-permute-start.20
  388.2 7.2 %collective-permute-done.11 = bf16[2,256,512]{2,1,0:T(8,128)(2,1)} collective-permute-done((bf16[2,256,512]{2,1,0:T(8,128)(2,1)}, bf16[2,256,512]{2,1,0:T(8,128)(2,1)}, u32[]{:S(2)}, u32[]{:S(2)}) %collective-permute-start.11) | collective-permute-done | bytes 524320 | tf_op jit(solution)/shard_map/ppermute | solution.py:889
  397.2 2.1 fusion.17
  400.7 2.1 collective-permute-start.23
  402.8 6.1 %collective-permute-done.20 = bf16[2,2,256,512]{3,2,1,0:T(8,128)(2,1)S(1)} collective-permute-done((bf16[2,2,256,512]{3,2,1,0:T(8,128)(2,1)}, bf16[2,2,256,512]{3,2,1,0:T(8,128)(2,1)S(1)}, u32[]{:S(2)}, u32[]{:S(2)}) %collective-permute-start.20) | collective-permute-done | bytes 1048608 | tf_op jit(solution)/shard_map/ppermute | solution.py:889
  410.4 2.1 fusion.15
  413.8 1.8 pad_maximum_fusion
  415.6 4.1 collective-permute-start.27
  419.7 1.8 fusion.41
  421.8 1.8 fusion.40
  423.6 9.9 %collective-permute-done.21 = bf16[2,256,512]{2,1,0:T(8,128)(2,1)S(1)} collective-permute-done((bf16[2,256,512]{2,1,0:T(8,128)(2,1)S(1)}, bf16[2,256,512]{2,1,0:T(8,128)(2,1)S(1)}, u32[]{:S(2)}, u32[]{:S(2)}) %collective-permute-start.21) | collective-permute-done | bytes 524320 | tf_op jit(solution)/shard_map/ppermute | solution.py:889
  433.5 1.7 collective-permute-start.25
  435.2 1.7 fusion.39
  438.7 1.7 collective-permute-start.26
  445.0 2.0 add_convert_fusion.1
  448.0 3.5 add_convert_fusion.3
  453.2 11.5 %collective-permute-done.24 = bf16[256,512]{1,0:T(8,128)(2,1)} collective-permute-done((bf16[256,512]{1,0:T(8,128)(2,1)}, bf16[256,512]{1,0:T(8,128)(2,1)}, u32[]{:S(2)}, u32[]{:S(2)}) %collective-permute-start.24) | collective-permute-done | bytes 262176 | tf_op jit(solution)/shard_map/ppermute | solution.py:889
  464.7 5.5 %collective-permute-done.26 = bf16[256,512]{1,0:T(8,128)(2,1)} collective-permute-done((bf16[256,512]{1,0:T(8,128)(2,1)}, bf16[256,512]{1,0:T(8,128)(2,1)}, u32[]{:S(2)}, u32[]{:S(2)}) %collective-permute-start.26) | collective-permute-done | bytes 262176 | tf_op jit(solution)/shard_map/ppermute | solution.py:889
  475.4 16.1 %collective-permute-done.8 = bf16[1024,512]{1,0:T(8,128)(2,1)S(1)} collective-permute-done((bf16[1024,512]{1,0:T(8,128)(2,1)S(1)}, bf16[1024,512]{1,0:T(8,128)(2,1)S(1)}, u32[]{:S(2)}, u32[]{:S(2)}) %collective-permute-start.8) | collective-permute-done | bytes 1048608 | tf_op jit(solution)/shard_map/ppermute | solution.py:936
  491.5 3.3 add_convert_fusion
  494.9 3.0 add_convert_fusion.2
  (185 shorter events, 52.9 us)
Async XLA Ops:
  2.0 32.8 %copy-start.28 = (bf16[1024,512]{1,0:T(8,128)(2,1)S(1)}, bf16[1024,512]{1,0:T(8,128)(2,1)}, u32[]{:S(2)}) copy-start(bf16[1024,512]{1,0:T(8,128)(2,1)} %own_ref.1) | copy-start | bytes 3145732
  2.0 34.0 %copy-start.42 = (bf16[3,4,512]{2,1,0:T(4,128)(2,1)S(1)}, bf16[3,4,512]{2,1,0:T(4,128)(2,1)}, u32[]{:S(2)}) copy-start(bf16[3,4,512]{2,1,0:T(4,128)(2,1)} %param.18) | copy-start | bytes 36868
  2.0 34.0 %copy-start.43 = (s32[2,512]{1,0:T(2,128)S(1)}, s32[2,512]{1,0:T(2,128)}, u32[]{:S(2)}) copy-start(s32[2,512]{1,0:T(2,128)} %param.15) | copy-start | bytes 12292
  2.0 34.0 %copy-start.10 = (f32[128]{0:T(128)S(1)}, f32[128]{0:T(128)}, u32[]{:S(2)}) copy-start(f32[128]{0:T(128)} %param.20) | copy-start | bytes 1540
  34.8 29.3 %collective-permute-start = (bf16[1024,512]{1,0:T(8,128)(2,1)S(1)}, bf16[1024,512]{1,0:T(8,128)(2,1)}, u32[]{:S(2)}, u32[]{:S(2)}) collective-permute-start(bf16[1024,512]{1,0:T(8,128)(2,1)S(1)} %copy-done.28), channel_id=1, source_target_pairs={{0,2},{1,3},{2,0},{3,1},{4,6},{5,7},{6,4},{7,5},{8,10},{9,11},{10,... | collective-permute-start | bytes 3145736 | tf_op jit(solution)/shard_map/ppermute | solution.py:936
  122.9 14.9 %copy-start.44 = (bf16[1024,2048]{1,0:T(8,128)(2,1)S(1)}, bf16[1024,2048]{1,0:T(8,128)(2,1)}, u32[]{:S(2)}) copy-start(bf16[1024,2048]{1,0:T(8,128)(2,1)} %get-tuple-element.94) | copy-start | bytes 12582916
  132.5 5.3 %copy-start.18 = (bf16[1024,1408]{1,0:T(8,128)(2,1)S(1)}, bf16[1024,1408]{1,0:T(8,128)(2,1)}, u32[]{:S(2)}) copy-start(bf16[1024,1408]{1,0:T(8,128)(2,1)} %get-tuple-element.106.gate_ref) | copy-start | bytes 8650756
  136.3 101.3 %collective-permute-start.2 = (bf16[2,2,256,1408]{3,2,1,0:T(8,128)(2,1)}, bf16[2,2,256,1408]{3,2,1,0:T(8,128)(2,1)}, u32[]{:S(2)}, u32[]{:S(2)}) collective-permute-start(bf16[2,2,256,1408]{3,2,1,0:T(8,128)(2,1)} %dynamic-slice_bitcast_fusion.2), channel_id=1, source_target_pairs={{0,4},{4,0},{8,12},{12,8},{16,20},{20,16},{24,28},{28,24},{1,5},{5... | collective-permute-start | bytes 8650760 | tf_op jit(solution)/shard_map/ppermute | solution.py:889
  144.9 3.8 copy-start.14
  144.9 5.4 %copy-start.19 = (bf16[1024,1408]{1,0:T(8,128)(2,1)S(1)}, bf16[1024,1408]{1,0:T(8,128)(2,1)}, u32[]{:S(2)}) copy-start(bf16[1024,1408]{1,0:T(8,128)(2,1)} %get-tuple-element.99.up_ref) | copy-start | bytes 8650756
  148.7 85.6 %collective-permute-start.3 = (bf16[2,2,256,1408]{3,2,1,0:T(8,128)(2,1)}, bf16[2,2,256,1408]{3,2,1,0:T(8,128)(2,1)}, u32[]{:S(2)}, u32[]{:S(2)}) collective-permute-start(bf16[2,2,256,1408]{3,2,1,0:T(8,128)(2,1)} %dynamic-slice_bitcast_fusion.1), channel_id=1, source_target_pairs={{0,8},{4,12},{8,0},{12,4},{16,24},{20,28},{24,16},{28,20},{1,9},{5... | collective-permute-start | bytes 8650760 | tf_op jit(solution)/shard_map/ppermute | solution.py:889
  161.0 118.7 %collective-permute-start.1 = (bf16[2,2,256,1408]{3,2,1,0:T(8,128)(2,1)}, bf16[2,2,256,1408]{3,2,1,0:T(8,128)(2,1)}, u32[]{:S(2)}, u32[]{:S(2)}) collective-permute-start(bf16[2,2,256,1408]{3,2,1,0:T(8,128)(2,1)} %dynamic-slice_bitcast_fusion), channel_id=1, source_target_pairs={{0,4},{4,0},{8,12},{12,8},{16,20},{20,16},{24,28},{28,24},{1,5},{5... | collective-permute-start | bytes 8650760 | tf_op jit(solution)/shard_map/ppermute | solution.py:889
  233.2 4.4 copy-start.20
  237.6 5.8 %copy-start.1 = (bf16[4,1024,128]{2,1,0:T(8,128)(2,1)S(1)}, bf16[4,1024,128]{2,1,0:T(8,128)(2,1)}, u32[]{:S(2)}) copy-start(bf16[4,1024,128]{2,1,0:T(8,128)(2,1)} %copy-done) | copy-start | bytes 3145732
  237.6 5.8 %copy-start.9 = (f32[8,1024]{1,0:T(8,128)S(1)}, f32[8,1024]{1,0:T(8,128)}, u32[]{:S(2)}) copy-start(f32[8,1024]{1,0:T(8,128)} %get-tuple-element.88.logit_ref) | copy-start | bytes 98308
  240.9 44.5 %collective-permute-start.6 = (bf16[2,256,1408]{2,1,0:T(8,128)(2,1)}, bf16[2,256,1408]{2,1,0:T(8,128)(2,1)}, u32[]{:S(2)}, u32[]{:S(2)}) collective-permute-start(bf16[2,256,1408]{2,1,0:T(8,128)(2,1)} %fusion.10), channel_id=1, source_target_pairs={{0,8},{4,12},{8,0},{12,4},{16,24},{20,28},{24,16},{28,20},{1,9},{5... | collective-permute-start | bytes 4325384 | tf_op jit(solution)/shard_map/ppermute | solution.py:889
  241.3 98.0 %collective-permute-start.10 = (bf16[2,2,256,512]{3,2,1,0:T(8,128)(2,1)}, bf16[2,2,256,512]{3,2,1,0:T(8,128)(2,1)}, u32[]{:S(2)}, u32[]{:S(2)}) collective-permute-start(bf16[2,2,256,512]{3,2,1,0:T(8,128)(2,1)} %dynamic-slice_bitcast_fusion.6), channel_id=1, source_target_pairs={{0,4},{4,0},{8,12},{12,8},{16,20},{20,16},{24,28},{28,24},{1,5},{5... | collective-permute-start | bytes 3145736 | tf_op jit(solution)/shard_map/ppermute | solution.py:889
  242.8 73.3 %collective-permute-start.5 = (bf16[2,256,1408]{2,1,0:T(8,128)(2,1)}, bf16[2,256,1408]{2,1,0:T(8,128)(2,1)}, u32[]{:S(2)}, u32[]{:S(2)}) collective-permute-start(bf16[2,256,1408]{2,1,0:T(8,128)(2,1)} %fusion.11), channel_id=1, source_target_pairs={{0,4},{4,0},{8,12},{12,8},{16,20},{20,16},{24,28},{28,24},{1,5},{5... | collective-permute-start | bytes 4325384 | tf_op jit(solution)/shard_map/ppermute | solution.py:889
  279.6 4.6 copy-start.17
  279.6 11.0 %slice-start = ((s8[6291456]{0:T(1024)(128)(4,1)}), s8[4194304]{0:T(1024)(128)(4,1)S(1)}, s32[]{:S(2)}) async-start(s8[6291456]{0:T(1024)(128)(4,1)} %bitcast.251), calls=%async_computation | async-start | bytes 8388608
  281.9 53.2 %collective-permute-start.4 = (bf16[2,256,1408]{2,1,0:T(8,128)(2,1)S(1)}, bf16[2,256,1408]{2,1,0:T(8,128)(2,1)}, u32[]{:S(2)}, u32[]{:S(2)}) collective-permute-start(bf16[2,256,1408]{2,1,0:T(8,128)(2,1)S(1)} %fusion.9), channel_id=1, source_target_pairs={{0,8},{4,12},{8,0},{12,4},{16,24},{20,28},{24,16},{28,20},{1,9},{5... | collective-permute-start | bytes 4325384 | tf_op jit(solution)/shard_map/ppermute | solution.py:889
  284.2 6.4 %slice-start.1 = ((s8[6291456]{0:T(1024)(128)(4,1)}), s8[2097152]{0:T(1024)(128)(4,1)S(1)}, s32[]{:S(2)}) async-start(s8[6291456]{0:T(1024)(128)(4,1)} %bitcast.251), calls=%async_computation.1 | async-start | bytes 4194304
  288.0 74.1 %collective-permute-start.30 = (bf16[256,1408]{1,0:T(8,128)(2,1)}, bf16[256,1408]{1,0:T(8,128)(2,1)}, u32[]{:S(2)}, u32[]{:S(2)}) collective-permute-start(bf16[256,1408]{1,0:T(8,128)(2,1)} %fusion.20), channel_id=1, source_target_pairs={{0,16},{4,20},{8,24},{12,28},{16,0},{20,4},{24,8},{28,12},{1,17},{... | collective-permute-start | bytes 2162696 | tf_op jit(solution)/shard_map/ppermute | solution.py:889
  290.6 6.7 %copy-start.11 = (bf16[1024,2048]{1,0:T(8,128)(2,1)S(1)}, bf16[1024,2048]{1,0:T(8,128)(2,1)}, u32[]{:S(2)}) copy-start(bf16[1024,2048]{1,0:T(8,128)(2,1)} %get-tuple-element.118.x_ref) | copy-start | bytes 12582916
  301.5 20.0 %copy-start.16 = (bf16[1024,2048]{1,0:T(8,128)(2,1)S(1)}, bf16[1024,2048]{1,0:T(8,128)(2,1)}, u32[]{:S(2)}) copy-start(bf16[1024,2048]{1,0:T(8,128)(2,1)} %get-tuple-element.115) | copy-start | bytes 12582916
  303.8 48.4 %copy-start.12 = (bf16[1024,2048]{1,0:T(8,128)(2,1)}, bf16[1024,2048]{1,0:T(8,128)(2,1)S(1)}, u32[]{:S(2)}) copy-start(bf16[1024,2048]{1,0:T(8,128)(2,1)S(1)} %fusion.6) | copy-start | bytes 12582916
  303.8 17.7 %copy-start.30 = (bf16[1024,512]{1,0:T(8,128)(2,1)S(1)}, bf16[1024,512]{1,0:T(8,128)(2,1)}, u32[]{:S(2)}) copy-start(bf16[1024,512]{1,0:T(8,128)(2,1)} %get-tuple-element.121) | copy-start | bytes 3145732
  318.9 77.7 %collective-permute-start.28 = (bf16[256,1408]{1,0:T(8,128)(2,1)}, bf16[256,1408]{1,0:T(8,128)(2,1)}, u32[]{:S(2)}, u32[]{:S(2)}) collective-permute-start(bf16[256,1408]{1,0:T(8,128)(2,1)} %fusion.19), channel_id=1, source_target_pairs={{0,16},{4,20},{8,24},{12,28},{16,0},{20,4},{24,8},{28,12},{1,17},{... | collective-permute-start | bytes 2162696 | tf_op jit(solution)/shard_map/ppermute | solution.py:889
  325.1 60.2 %collective-permute-start.12 = (bf16[2,2,256,512]{3,2,1,0:T(8,128)(2,1)}, bf16[2,2,256,512]{3,2,1,0:T(8,128)(2,1)}, u32[]{:S(2)}, u32[]{:S(2)}) collective-permute-start(bf16[2,2,256,512]{3,2,1,0:T(8,128)(2,1)} %dynamic-slice_bitcast_fusion.5), channel_id=1, source_target_pairs={{0,8},{4,12},{8,0},{12,4},{16,24},{20,28},{24,16},{28,20},{1,9},{5... | collective-permute-start | bytes 3145736 | tf_op jit(solution)/shard_map/ppermute | solution.py:889
  326.7 16.1 %slice-start.2 = ((s8[5767168]{0:T(1024)(128)(4,1)}), s8[4194304]{0:T(1024)(128)(4,1)S(1)}, s32[]{:S(2)}) async-start(s8[5767168]{0:T(1024)(128)(4,1)} %bitcast.265), calls=%async_computation.2 | async-start | bytes 8388608
  331.6 11.2 %slice-start.3 = ((s8[5767168]{0:T(1024)(128)(4,1)}), s8[1572864]{0:T(1024)(128)(4,1)S(1)}, s32[]{:S(2)}) async-start(s8[5767168]{0:T(1024)(128)(4,1)} %bitcast.265), calls=%async_computation.3 | async-start | bytes 3145728
  334.1 7.3 %copy-start.24 = (bf16[2048,512]{1,0:T(8,128)(2,1)}, bf16[2048,512]{1,0:T(8,128)(2,1)S(1)}, u32[]{:S(2)}) copy-start(bf16[2048,512]{1,0:T(8,128)(2,1)S(1)} %convolution_convert_fusion.3) | copy-start | bytes 6291460
  334.1 5.3 %copy-start.21 = (bf16[2048,512]{1,0:T(8,128)(2,1)S(1)}, bf16[2048,512]{1,0:T(8,128)(2,1)}, u32[]{:S(2)}) copy-start(bf16[2048,512]{1,0:T(8,128)(2,1)} %copy-done.20) | copy-start | bytes 6291460
  334.1 7.3 %copy-start.41 = (f32[1,2048]{1,0:T(1,128)S(1)}, f32[1,2048]{1,0:T(1,128)}, u32[]{:S(2)}) copy-start(f32[1,2048]{1,0:T(1,128)} %get-tuple-element.133) | copy-start | bytes 24580
  335.2 64.1 %collective-permute-start.9 = (bf16[2,2,256,512]{3,2,1,0:T(8,128)(2,1)}, bf16[2,2,256,512]{3,2,1,0:T(8,128)(2,1)}, u32[]{:S(2)}, u32[]{:S(2)}) collective-permute-start(bf16[2,2,256,512]{3,2,1,0:T(8,128)(2,1)} %dynamic-slice_bitcast_fusion.4), channel_id=1, source_target_pairs={{0,4},{4,0},{8,12},{12,8},{16,20},{20,16},{24,28},{28,24},{1,5},{5... | collective-permute-start | bytes 3145736 | tf_op jit(solution)/shard_map/ppermute | solution.py:889
  341.4 11.0 %collective-permute-start.15 = (f32[4224]{0:T(1024)S(1)}, f32[4224]{0:T(1024)S(1)}, u32[]{:S(2)}, u32[]{:S(2)}) collective-permute-start(f32[4224]{0:T(1024)S(1)} %pad_maximum_fusion.5), channel_id=1, source_target_pairs={{0,1},{1,0},{2,3},{3,2},{4,5},{5,4},{6,7},{7,6},{8,9},{9,8},{10,11... | collective-permute-start | bytes 50696 | tf_op jit(solution)/shard_map/ppermute | solution.py:865
  352.4 3.9 copy-start.38
  352.4 3.8 collective-permute-start.16
  356.3 4.5 collective-permute-start.17
  360.7 34.7 %collective-permute-start.11 = (bf16[2,256,512]{2,1,0:T(8,128)(2,1)}, bf16[2,256,512]{2,1,0:T(8,128)(2,1)}, u32[]{:S(2)}, u32[]{:S(2)}) collective-permute-start(bf16[2,256,512]{2,1,0:T(8,128)(2,1)} %fusion.30), channel_id=1, source_target_pairs={{0,8},{4,12},{8,0},{12,4},{16,24},{20,28},{24,16},{28,20},{1,9},{5... | collective-permute-start | bytes 1572872 | tf_op jit(solution)/shard_map/ppermute | solution.py:889
  362.1 38.6 %collective-permute-start.29 = (bf16[256,1408]{1,0:T(8,128)(2,1)}, bf16[256,1408]{1,0:T(8,128)(2,1)}, u32[]{:S(2)}, u32[]{:S(2)}) collective-permute-start(bf16[256,1408]{1,0:T(8,128)(2,1)} %fusion.18), channel_id=1, source_target_pairs={{0,16},{4,20},{8,24},{12,28},{16,0},{20,4},{24,8},{28,12},{1,17},{... | collective-permute-start | bytes 2162696 | tf_op jit(solution)/shard_map/ppermute | solution.py:889
  385.4 23.5 %collective-permute-start.20 = (bf16[2,2,256,512]{3,2,1,0:T(8,128)(2,1)}, bf16[2,2,256,512]{3,2,1,0:T(8,128)(2,1)S(1)}, u32[]{:S(2)}, u32[]{:S(2)}) collective-permute-start(bf16[2,2,256,512]{3,2,1,0:T(8,128)(2,1)} %dynamic-slice_bitcast_fusion.3), channel_id=1, source_target_pairs={{0,4},{4,0},{8,12},{12,8},{16,20},{20,16},{24,28},{28,24},{1,5},{5... | collective-permute-start | bytes 3145736 | tf_op jit(solution)/shard_map/ppermute | solution.py:889
  388.2 11.1 %copy-start.37 = (f32[18560]{0:T(1024)S(1)}, f32[18560]{0:T(1024)}, u32[]{:S(2)}) copy-start(f32[18560]{0:T(1024)} %fusion.50) | copy-start | bytes 222724
  395.5 49.5 %collective-permute-start.13 = (bf16[1024,1024]{1,0:T(8,128)(2,1)}, bf16[1024,1024]{1,0:T(8,128)(2,1)}, u32[]{:S(2)}, u32[]{:S(2)}) collective-permute-start(bf16[1024,1024]{1,0:T(8,128)(2,1)} %pad_maximum_fusion.2), channel_id=1, source_target_pairs={{0,1},{1,0},{2,3},{3,2},{4,5},{5,4},{6,7},{7,6},{8,9},{9,8},{10,11... | collective-permute-start | bytes 6291464 | tf_op jit(solution)/shard_map/ppermute | solution.py:936
  396.6 51.4 %collective-permute-start.7 = (bf16[1024,1024]{1,0:T(8,128)(2,1)}, bf16[1024,1024]{1,0:T(8,128)(2,1)}, u32[]{:S(2)}, u32[]{:S(2)}) collective-permute-start(bf16[1024,1024]{1,0:T(8,128)(2,1)} %pad_maximum_fusion.1), channel_id=1, source_target_pairs={{0,1},{1,0},{2,3},{3,2},{4,5},{5,4},{6,7},{7,6},{8,9},{9,8},{10,11... | collective-permute-start | bytes 6291464 | tf_op jit(solution)/shard_map/ppermute | solution.py:936
  399.3 14.4 %collective-permute-start.18 = (f32[18560]{0:T(1024)S(1)}, f32[18560]{0:T(1024)S(1)}, u32[]{:S(2)}, u32[]{:S(2)}) collective-permute-start(f32[18560]{0:T(1024)S(1)} %copy-done.37), channel_id=1, source_target_pairs={{0,8},{4,12},{8,0},{12,4},{16,24},{20,28},{24,16},{28,20},{1,9},{5... | collective-permute-start | bytes 222728 | tf_op jit(solution)/shard_map/ppermute | solution.py:889
  400.7 14.9 %collective-permute-start.23 = (bf16[2,256,512]{2,1,0:T(8,128)(2,1)S(1)}, bf16[2,256,512]{2,1,0:T(8,128)(2,1)S(1)}, u32[]{:S(2)}, u32[]{:S(2)}) collective-permute-start(bf16[2,256,512]{2,1,0:T(8,128)(2,1)S(1)} %fusion.28), channel_id=1, source_target_pairs={{0,8},{4,12},{8,0},{12,4},{16,24},{20,28},{24,16},{28,20},{1,9},{5... | collective-permute-start | bytes 1572872 | tf_op jit(solution)/shard_map/ppermute | solution.py:889
  408.9 26.3 %copy-start.29 = (bf16[2,2,256,512]{3,2,1,0:T(8,128)(2,1)}, bf16[2,2,256,512]{3,2,1,0:T(8,128)(2,1)S(1)}, u32[]{:S(2)}) copy-start(bf16[2,2,256,512]{3,2,1,0:T(8,128)(2,1)S(1)} %collective-permute-done.20) | copy-start | bytes 3145732
  408.9 12.6 %collective-permute-start.22 = (bf16[2,256,512]{2,1,0:T(8,128)(2,1)S(1)}, bf16[2,256,512]{2,1,0:T(8,128)(2,1)S(1)}, u32[]{:S(2)}, u32[]{:S(2)}) collective-permute-start(bf16[2,256,512]{2,1,0:T(8,128)(2,1)S(1)} %fusion.29), channel_id=1, source_target_pairs={{0,4},{4,0},{8,12},{12,8},{16,20},{20,16},{24,28},{28,24},{1,5},{5... | collective-permute-start | bytes 1572872 | tf_op jit(solution)/shard_map/ppermute | solution.py:889
  413.7 19.8 %collective-permute-start.21 = (bf16[2,256,512]{2,1,0:T(8,128)(2,1)S(1)}, bf16[2,256,512]{2,1,0:T(8,128)(2,1)S(1)}, u32[]{:S(2)}, u32[]{:S(2)}) collective-permute-start(bf16[2,256,512]{2,1,0:T(8,128)(2,1)S(1)} %fusion.27), channel_id=1, source_target_pairs={{0,8},{4,12},{8,0},{12,4},{16,24},{20,28},{24,16},{28,20},{1,9},{5... | collective-permute-start | bytes 1572872 | tf_op jit(solution)/shard_map/ppermute | solution.py:889
  415.6 23.2 %copy-start.31 = (bf16[2,256,512]{2,1,0:T(8,128)(2,1)}, bf16[2,256,512]{2,1,0:T(8,128)(2,1)S(1)}, u32[]{:S(2)}) copy-start(bf16[2,256,512]{2,1,0:T(8,128)(2,1)S(1)} %collective-permute-done.23) | copy-start | bytes 1572868
  415.6 23.1 %collective-permute-start.27 = (bf16[256,512]{1,0:T(8,128)(2,1)S(1)}, bf16[256,512]{1,0:T(8,128)(2,1)S(1)}, u32[]{:S(2)}, u32[]{:S(2)}) collective-permute-start(bf16[256,512]{1,0:T(8,128)(2,1)S(1)} %fusion.42), channel_id=1, source_target_pairs={{0,16},{4,20},{8,24},{12,28},{16,0},{20,4},{24,8},{28,12},{1,17},{... | collective-permute-start | bytes 786440 | tf_op jit(solution)/shard_map/ppermute | solution.py:889
  421.6 18.9 %copy-start.33 = (bf16[2,256,512]{2,1,0:T(8,128)(2,1)}, bf16[2,256,512]{2,1,0:T(8,128)(2,1)S(1)}, u32[]{:S(2)}) copy-start(bf16[2,256,512]{2,1,0:T(8,128)(2,1)S(1)} %collective-permute-done.22) | copy-start | bytes 1572868
  421.6 15.4 %collective-permute-start.19 = (f32[18560]{0:T(1024)S(1)}, f32[18560]{0:T(1024)S(1)}, u32[]{:S(2)}, u32[]{:S(2)}) collective-permute-start(f32[18560]{0:T(1024)S(1)} %add.557), channel_id=1, source_target_pairs={{0,16},{4,20},{8,24},{12,28},{16,0},{20,4},{24,8},{28,12},{1,17},{... | collective-permute-start | bytes 222728 | tf_op jit(solution)/shard_map/ppermute | solution.py:889
  433.5 6.9 %copy-start.35 = (bf16[2,256,512]{2,1,0:T(8,128)(2,1)}, bf16[2,256,512]{2,1,0:T(8,128)(2,1)S(1)}, u32[]{:S(2)}) copy-start(bf16[2,256,512]{2,1,0:T(8,128)(2,1)S(1)} %collective-permute-done.21) | copy-start | bytes 1572868
  433.5 31.2 %collective-permute-start.25 = (bf16[256,512]{1,0:T(8,128)(2,1)}, bf16[256,512]{1,0:T(8,128)(2,1)}, u32[]{:S(2)}, u32[]{:S(2)}) collective-permute-start(bf16[256,512]{1,0:T(8,128)(2,1)} %fusion.40), channel_id=1, source_target_pairs={{0,16},{4,20},{8,24},{12,28},{16,0},{20,4},{24,8},{28,12},{1,17},{... | collective-permute-start | bytes 786440 | tf_op jit(solution)/shard_map/ppermute | solution.py:889
  436.9 27.8 %collective-permute-start.24 = (bf16[256,512]{1,0:T(8,128)(2,1)}, bf16[256,512]{1,0:T(8,128)(2,1)}, u32[]{:S(2)}, u32[]{:S(2)}) collective-permute-start(bf16[256,512]{1,0:T(8,128)(2,1)} %fusion.39), channel_id=1, source_target_pairs={{0,16},{4,20},{8,24},{12,28},{16,0},{20,4},{24,8},{28,12},{1,17},{... | collective-permute-start | bytes 786440 | tf_op jit(solution)/shard_map/ppermute | solution.py:889
  438.7 31.5 %collective-permute-start.26 = (bf16[256,512]{1,0:T(8,128)(2,1)}, bf16[256,512]{1,0:T(8,128)(2,1)}, u32[]{:S(2)}, u32[]{:S(2)}) collective-permute-start(bf16[256,512]{1,0:T(8,128)(2,1)} %fusion.41), channel_id=1, source_target_pairs={{0,16},{4,20},{8,24},{12,28},{16,0},{20,4},{24,8},{28,12},{1,17},{... | collective-permute-start | bytes 786440 | tf_op jit(solution)/shard_map/ppermute | solution.py:889
  447.0 23.3 %copy-start.36 = (bf16[2,256,512]{2,1,0:T(8,128)(2,1)S(1)}, bf16[2,256,512]{2,1,0:T(8,128)(2,1)}, u32[]{:S(2)}) copy-start(bf16[2,256,512]{2,1,0:T(8,128)(2,1)} %copy-done.35) | copy-start | bytes 1572868
  447.0 24.5 %copy-start.34 = (bf16[2,256,512]{2,1,0:T(8,128)(2,1)S(1)}, bf16[2,256,512]{2,1,0:T(8,128)(2,1)}, u32[]{:S(2)}) copy-start(bf16[2,256,512]{2,1,0:T(8,128)(2,1)} %copy-done.33) | copy-start | bytes 1572868
  447.0 28.5 %collective-permute-start.14 = (bf16[1024,512]{1,0:T(8,128)(2,1)S(1)}, bf16[1024,512]{1,0:T(8,128)(2,1)S(1)}, u32[]{:S(2)}, u32[]{:S(2)}) collective-permute-start(bf16[1024,512]{1,0:T(8,128)(2,1)S(1)} %add_convert_fusion.1), channel_id=1, source_target_pairs={{0,2},{1,3},{2,0},{3,1},{4,6},{5,7},{6,4},{7,5},{8,10},{9,11},{10,... | collective-permute-start | bytes 3145736 | tf_op jit(solution)/shard_map/ppermute | solution.py:936
  451.5 21.5 %copy-start.32 = (bf16[2,256,512]{2,1,0:T(8,128)(2,1)S(1)}, bf16[2,256,512]{2,1,0:T(8,128)(2,1)}, u32[]{:S(2)}) copy-start(bf16[2,256,512]{2,1,0:T(8,128)(2,1)} %copy-done.31) | copy-start | bytes 1572868
  451.5 40.0 %collective-permute-start.8 = (bf16[1024,512]{1,0:T(8,128)(2,1)S(1)}, bf16[1024,512]{1,0:T(8,128)(2,1)S(1)}, u32[]{:S(2)}, u32[]{:S(2)}) collective-permute-start(bf16[1024,512]{1,0:T(8,128)(2,1)S(1)} %add_convert_fusion.3), channel_id=1, source_target_pairs={{0,2},{1,3},{2,0},{3,1},{4,6},{5,7},{6,4},{7,5},{8,10},{9,11},{10,... | collective-permute-start | bytes 3145736 | tf_op jit(solution)/shard_map/ppermute | solution.py:936
  471.5 20.0 %copy-start.25 = (f32[1024,512]{1,0:T(8,128)S(1)}, f32[1024,512]{1,0:T(8,128)}, u32[]{:S(2)}) copy-start(f32[1024,512]{1,0:T(8,128)} %get-tuple-element.131) | copy-start | bytes 6291460
  (18 other events, 33.2 us)

commit v3 on v2

--- a/solution.py
+++ b/solution.py
@@ -507,9 +507,9 @@
 
 
 def middle_kernel(low_ref, wout_ref, gain_ref, own_ref, other_ref, x_ref, wdown_ref, wgu_ref,
-                  middle_out, mid_out, normed_out, hidden_out, gate_out, up_out, cot_out,
-                  x_full, cot, wdown, wgu, keep, first, got_first, second, got_second, mid, middle, ghid, normed, acts,
-                  load_sem, cot_send, cot_recv, a_send, a_recv, b_send, b_recv, c_send, c_recv, middle_sem, mid_sem, normed_sem, act_sem, cot_sem):
+                  middle_out, mid_out, normed_out, hidden_out, gate_out, up_out, cot_out, ffn_out,
+                  x_full, cot, wdown, wgu, keep, first, got_first, second, got_second, mid, middle, ghid, normed, acts, ffn,
+                  load_sem, cot_send, cot_recv, a_send, a_recv, b_send, b_recv, c_send, c_recv, middle_sem, mid_sem, normed_sem, act_sem, cot_sem, ffn_sem):
     me, near, far = partners()
     width = own_ref.shape[1]
     chunks = low_ref.shape[0] // ROWS_PER
@@ -546,6 +546,10 @@
         slot = lax.rem(m, 2)
         return pltpu.make_async_copy(normed.at[slot], normed_out.at[band(m)], normed_sem.at[slot])
 
+    def out_ffn(m):
+        slot = lax.rem(m, 2)
+        return pltpu.make_async_copy(ffn.at[slot], ffn_out.at[band(m)], ffn_sem.at[slot])
+
     def out_act(m, which):
         slot = lax.rem(m, 2)
         return pltpu.make_async_copy(acts.at[slot, which], (hidden_out, gate_out, up_out)[which].at[band(m)], act_sem.at[slot, which])
@@ -592,6 +596,7 @@
         @pl.when(m >= 2)
         def _():
             out_normed(m - 2).wait()
+            out_ffn(m - 2).wait()
             for which in range(3):
                 out_act(m - 2, which).wait()
 
@@ -609,6 +614,8 @@
         acts[slot, 2] = (grad * silu).astype(BF16)
         for which in range(3):
             out_act(m, which).start()
+        ffn[slot] = jnp.dot(acts[slot, 0], wdown[...], preferred_element_type=F32).astype(BF16)
+        out_ffn(m).start()
 
     def both(m):
         total(m)
@@ -644,6 +651,7 @@
 
     for m in (chunks - 2, chunks - 1):
         out_normed(m).wait()
+        out_ffn(m).wait()
         for which in range(3):
             out_act(m, which).wait()
     for copy in shares:
@@ -661,7 +669,7 @@
     return pl.pallas_call(
         middle_kernel,
         in_specs=[in_vmem(), in_vmem(), in_vmem()] + [in_hbm()] * 5,
-        out_specs=[in_hbm()] * 7,
+        out_specs=[in_hbm()] * 8,
         out_shape=[
             jax.ShapeDtypeStruct((tokens, width), F32),
             jax.ShapeDtypeStruct((tokens, wide), BF16),
@@ -669,6 +677,7 @@
             jax.ShapeDtypeStruct((tokens, units), BF16),
             jax.ShapeDtypeStruct((tokens, units), BF16),
             jax.ShapeDtypeStruct((tokens, units), BF16),
+            jax.ShapeDtypeStruct((tokens, wide), BF16),
             jax.ShapeDtypeStruct((tokens, wide), BF16),
         ],
         scratch_shapes=[
@@ -686,10 +695,11 @@
             pltpu.VMEM((tokens, units), F32),
             pltpu.VMEM((2, ROWS_PER, wide), BF16),
             pltpu.VMEM((2, 3, ROWS_PER, units), BF16),
+            pltpu.VMEM((2, ROWS_PER, wide), BF16),
             dma((5,)), dma((2,)), dma((2,)),
             dma((chunks,)), dma((chunks,)), dma((chunks,)), dma((chunks,)),
             dma((chunks, 2)), dma((chunks, 2)),
-            dma((chunks,)), dma((chunks,)), dma((2,)), dma((2, 3)), dma,
+            dma((chunks,)), dma((chunks,)), dma((2,)), dma((2, 3)), dma, dma((2,)),
         ],
         compiler_params=pltpu.CompilerParams(collective_id=1, has_side_effects=True, vmem_limit_bytes=62 << 20),
         name="middle_step",
@@ -844,7 +854,6 @@
     )(wout, gain.reshape(1, wide), grad_gate, grad_up, full_mid, full_cot, wgu)
 
 
-PLAIN = (((1,), (0,)), ((), ()))
 ROWS = (((0,), (0,)), ((), ()))
 
 
@@ -881,6 +890,9 @@
         self.bits = size.bit_length() - 1
         self.token = None
         self.open = {}
+        self.later = {}
+        self.rider = None
+        self.rides = {}
 
     def after(self, value):
         return tie(value, self.token)
@@ -888,27 +900,59 @@
     def swap(self, values, bit):
         return lax.ppermute(values, "dp", [(i, i ^ (1 << bit)) for i in range(self.size)])
 
-    def scatter(self, name, grad, order=()):
-        order = list(order) + [bit for bit in range(self.bits) if bit not in order]
-        blocks = row_major(grad.astype(BF16)).reshape((2,) * self.bits + (grad.shape[0] // self.size, grad.shape[1]))
-        self.open[name] = ([blocks], list(range(self.bits))[::-1], order, 0)
-        self.move(name)
+    def send(self, away, bit, ride):
+        if not ride:
+            return self.swap(away, bit)
+        flat = away.reshape(-1, away.shape[-1])
+        rider = lax.reduce_precision(self.rider, 8, 7)
+        self.token = row_major(jnp.concatenate([flat, rider.astype(BF16)]))
+        came = self.swap(self.token, bit)
+        self.rider = rider + came[flat.shape[0] :].astype(F32)
+        return came[: flat.shape[0]].reshape(away.shape)
+
+    def half(self, values, bit, other):
+        own = lax.rem(lax.div(lax.axis_index("dp"), 1 << bit), 2)
+        side = 1 - own if other else own
+        run = values.shape[1] // self.size << bit
+        pieces = [lax.dynamic_slice_in_dim(values, (2 * i + side) * run, run, 1) for i in range(self.size // 2 >> bit)]
+        return pieces[0] if len(pieces) == 1 else jnp.concatenate(pieces, axis=1)
+
+    def product(self, rows, values):
+        grad = lax.dot_general(rows, values, ROWS, preferred_element_type=F32).astype(BF16)
+        return row_major(grad).reshape((2,) * (self.bits - 1) + (2 * rows.shape[1] // self.size, values.shape[1]))
+
+    def scatter(self, name, rows, values, bit, ride=False):
+        away = self.product(self.half(rows, bit, True), self.after(values))
+        self.token = away
+        came = self.send(away, bit, ride)
+        self.rides[name] = ride
+        order = [bit] + [i for i in range(self.bits) if i != bit]
+        axes = [i for i in range(self.bits)[::-1] if i != bit]
+        self.open[name] = ([came], axes, order, 1)
+        self.later[name] = (rows, values, bit)
+
+    def keep(self, name):
+        rows, values, bit = self.later.pop(name)
+        own = self.product(self.half(self.after(rows), bit, False), values)
+        self.token = own
+        terms, axes, order, stage = self.open[name]
+        self.open[name] = ([own] + terms, axes, order, stage)
 
     def move(self, name):
+        if name in self.later:
+            self.keep(name)
         terms, axes, order, stage = self.open[name]
         bit = order[stage]
         own = lax.rem(lax.div(lax.axis_index("dp"), 1 << bit), 2)
         axis = axes.index(bit)
-        if stage:
-            terms = terms[:-1] + [self.after(terms[-1])]
+        terms = terms[:-1] + [self.after(terms[-1])]
 
         def pick(value, at):
             return lax.dynamic_index_in_dim(value, at, axis, keepdims=False)
 
-        away = pick(terms[0], 1 - own) if stage == 0 else sum(pick(t, 1 - own).astype(F32) for t in terms).astype(BF16)
-        away = row_major(away)
+        away = row_major(sum(pick(t, 1 - own).astype(F32) for t in terms).astype(BF16))
         self.token = away
-        came = self.swap(away, bit)
+        came = self.send(away, bit, self.rides[name])
         self.open[name] = ([pick(t, own) for t in terms] + [came], axes[:axis] + axes[axis + 1 :], order, stage + 1)
 
     def close(self, name):
@@ -929,9 +973,6 @@
         me = lax.axis_index("tensor")
         side, spot = lax.rem(me, 2), lax.div(me, 2)
 
-        def dot(a, b, dims):
-            return lax.dot_general(a, b, dims, preferred_element_type=F32)
-
         def swap(values, step):
             return lax.ppermute(values, "tensor", [(i, i ^ step) for i in range(tensor_size)])
 
@@ -951,21 +992,26 @@
         cot_own, _ = lax.optimization_barrier((cotangent, logits))
         cot_far = swap(cot_own, 2)
         out_low, *kept = mixer_forward(proj, seg_ids, taps, logits, onorm_gain)
-        middle, mid_low, normed_two, hidden, grad_gate, grad_up, full_cot = middle_step(out_low, wout, mlp_gain, cotangent, cot_far, full_low, wdown, wgu)
+        middle, mid_low, normed_two, hidden, grad_gate, grad_up, full_cot, ffn_part = middle_step(out_low, wout, mlp_gain, cotangent, cot_far, full_low, wdown, wgu)
         line = Timeline(dp_size)
-        line.scatter("down", dot(full_cot, hidden, ROWS))
-        line.scatter("gate", dot(normed_two, line.after(grad_gate), ROWS), (1,))
-        line.scatter("up", dot(normed_two, line.after(grad_up), ROWS))
+        cut = grad_up.shape[1] // 11 * 4
+        line.scatter("down", full_cot, hidden, 0)
+        line.scatter("gate", normed_two, grad_gate, 1)
+        line.scatter("upx", normed_two, grad_up[:, cut:], 0)
+        line.scatter("upz", normed_two, grad_up[:, :cut], 1)
         late_gate = line.after(grad_gate)
         grad_middle, full_grad_mid, grad_nout, gain_two = return_step(wout, mlp_gain, late_gate, grad_up, mid_low, full_cot, wgu)
-        line.scatter("out", dot(full_grad_mid, out_low, ROWS))
+        line.token = grad_nout
+        line.move("down")
+        line.scatter("out", full_grad_mid, out_low, 0)
         line.move("gate")
-        line.move("down")
+        line.move("upx")
         grad_proj, grad_logits, grad_conv, gain_onorm = mixer_backward(proj, seg_ids, taps, logits, onorm_gain, kept, line.after(grad_nout))
         line.token = grad_logits
         grad_logits = grad_logits.reshape(heads, tokens)
-        line.move("up")
         line.move("down")
+        line.move("upz")
+        line.scatter("k", normed_one, grad_proj[1], 0)
         late_low, late_proj = line.after((full_low, grad_proj))
         grad_nin = jnp.einsum("ctk,cdk->td", late_proj, wqkv, preferred_element_type=F32)
         grad_nin = grad_nin + jnp.einsum("ht,dh->td", grad_logits, wrate, preferred_element_type=F32)
@@ -975,57 +1021,63 @@
         part_one = part_one.astype(BF16)
         line.token = (part_one, gain_one)
         wide = gain_one.shape[0]
-        grad_beta = jnp.einsum("td,ht->dh", normed_one, line.after(grad_logits), preferred_element_type=F32)
         gains = butterfly(jnp.concatenate([gain_one, gain_two.reshape(-1), gain_onorm.reshape(-1)]), "tensor", tensor_size)
         shared = gains.shape[0]
         line.move("gate")
-        line.scatter("k", dot(normed_one, line.after(grad_proj[1]), ROWS), (1,))
+        grad_beta = jnp.einsum("td,ht->dh", normed_one, line.after(grad_logits), preferred_element_type=F32)
+        line.move("out")
         small = jnp.concatenate([gains, grad_conv.reshape(-1), grad_beta.reshape(-1)])
-        small_came = line.swap(small, 0)
-        line.scatter("v", dot(normed_one, line.after(grad_proj[2]), ROWS))
-        line.scatter("q", dot(normed_one, line.after(grad_proj[0]), ROWS))
+        lanes = grad_proj.shape[2]
+        extra = -small.shape[0] % (16 * lanes)
+        line.rider = jnp.pad(small, (0, extra)).reshape(-1, lanes)
+        line.scatter("v", normed_one, grad_proj[2], 0, ride=True)
+        line.scatter("q", normed_one, grad_proj[0], 0)
+        line.move("upx")
+        line.move("k")
+        line.move("upz")
+        line.move("out")
         one, one_far = quarter_sum(lambda q: columns(part_one, q).astype(F32))
-        line.move("up")
-        late_hidden = line.after(hidden)
-        ffn, ffn_far = quarter_sum(lambda q: dot(late_hidden, columns(wdown, q), PLAIN))
-        line.move("out")
+        line.keep("v")
+        line.move("v")
+        late_ffn = line.after(ffn_part)
+        ffn, ffn_far = quarter_sum(lambda q: columns(late_ffn, q).astype(F32))
+        line.keep("q")
         grad_down = line.close("down").T
-        small = small + line.after(small_came)
-        small_came = line.swap(small, 1 % line.bits)
+        line.token = grad_down
         line.move("k")
-        line.move("out")
-        grad_gate_w = line.close("gate")
-        line.move("v")
-        grad_up_w = line.close("up")
-        small = small + line.after(small_came)
-        small_came = line.swap(small, 2 % line.bits)
-        grad_in = (grad_middle + one + line.after(one_far).astype(F32)).astype(BF16)
-        layer_out = (middle + ffn + line.after(ffn_far).astype(F32)).astype(BF16)
         line.move("q")
         line.move("v")
-        line.move("k")
+        grad_gate_w = line.close("gate")
+        grad_in = (grad_middle + one + line.after(one_far).astype(F32)).astype(BF16)
+        line.token = (grad_gate_w, grad_in)
+        grad_up_w = jnp.concatenate([line.close("upz"), line.close("upx")], axis=1)
+        grad_gate_up = jnp.stack([grad_gate_w, grad_up_w])
+        grad_out = line.close("out").T
+        layer_out = (middle + ffn + line.after(ffn_far).astype(F32)).astype(BF16)
+        line.token = (grad_gate_up, grad_out, layer_out)
         line.move("q")
-        small = small + line.after(small_came)
-        for bit in range(3, line.bits):
-            small = small + line.swap(small, bit)
-        grad_out = line.close("out").T
-        grad_qkv = [line.close(n) for n in "qkv"]
+        grad_k, grad_v = line.close("k"), line.close("v")
+        small = line.rider.reshape(-1)
+        grad_qkv = jnp.stack([grad_k, grad_k, grad_v])
+        line.token = (grad_qkv, small)
+        grad_qkv = lax.dynamic_update_slice(grad_qkv, line.close("q")[None], (0, 0, 0))
         gains = small[:shared]
+        mine = grad_beta.shape[0] // dp_size
+        rest = small[shared + grad_conv.size :]
         grad_conv = small[shared : shared + grad_conv.size].reshape(grad_conv.shape)
-        mine = grad_beta.shape[0] // dp_size
-        grad_beta = small[shared + grad_conv.size :].reshape(grad_beta.shape)
+        grad_beta = rest[: grad_beta.size].reshape(grad_beta.shape)
         grad_beta = lax.dynamic_slice_in_dim(grad_beta, lax.axis_index("dp") * mine, mine, 0)
         return (
             layer_out,
             grad_in,
             gains[:wide],
-            jnp.stack(grad_qkv),
+            grad_qkv,
             grad_conv,
             grad_beta,
             gains[2 * wide :],
             grad_out,
             gains[wide : 2 * wide],
-            jnp.stack([grad_gate_w, grad_up_w]),
+            grad_gate_up,
             grad_down,
         )
 

time: 507 us -> 535 us (1.055)
  waiting for transfers between devices: 89.1 us -> 104 us
  other arithmetic: 60.5 us -> 73.5 us
  local copies, waits for them, and re-layouts: 35.8 us -> 42.8 us
    ppermute x24, waiting for transfers between devices: 72.6 us -> 84.7 us  [swap(): lax.ppermute(values, 'dp', [(i, i ^ 1 << bit) for i in range(self.size)])]
    dynamic_slice x0 -> x12, local copies, waits for them, and re-layouts: none -> 9.22 us  [half(): lax.dynamic_slice_in_dim(values, (2 * i + side) * run, run, 1)]
    squeeze x8 -> x1, local copies, waits for them, and re-layouts: 11.2 us -> 3.19 us  [step(): line.scatter('q', normed_one, grad_proj[0], 0)]
    convert_element_type x14 -> x16, other arithmetic: 29.3 us -> 36.3 us  [move(): sum((pick(t, 1 - own).astype(F32) for t in terms)).astype(BF16)]
    another operation x7 -> x5, other arithmetic: 11.1 us -> 4.46 us  [the longest x3 2.59 us: step(): grad_qkv = jnp.stack([grad_k, grad_k, grad_v])]
    slice x3 -> x8, local copies, waits for them, and re-layouts: 1.68 us -> 7.6 us  [the longest x2 6.23 us: step(): grad_beta = rest[:grad_beta.size].reshape(grad_beta.shape)]
    dot_general x11 -> x16, matrix products: 48.5 us -> 44.8 us  [product(): lax.dot_general(rows, values, ROWS, preferred_element_type=F32).astype(BF16)]
    unnamed x107 -> x123, local copies, waits for them, and re-layouts: 19.5 us -> 18.5 us
  transfers between devices with their start and end apart: 31 -> 31, of which waited for: 10 -> 8; matrix products, arithmetic and copies ran while one was open for 24% -> 29% of each run, Pallas kernels for 25% -> 23%
where the time goes in v3:
time: 535 us; the launch traced here: 526 us
  Pallas kernels  215 us (40%)
  waiting for transfers between devices  104 us (19%)
  other arithmetic  73.5 us (14%)
  matrix products  56.1 us (10%)
  local copies, waits for them, and re-layouts  42.8 us (8%)
  starting transfers between devices  31.9 us (6%)
    ppermute x24, waiting for transfers between devices, swap(): lax.ppermute(values, 'dp', [(i, i ^ 1 << bit) for i in range(self.size)])  84.7 us
    pallas_call x1, Pallas kernels, return_step(): pl.pallas_call(return_kernel, in_specs=[in_vmem(), in_vmem()] + [in_hbm()...  67.1 us
    pallas_call x1, Pallas kernels, middle_step(): pl.pallas_call(middle_kernel, in_specs=[in_vmem(), in_vmem(), in_vmem()]...  59.8 us
    dot_general x16, matrix products, product(): lax.dot_general(rows, values, ROWS, preferred_element_type=F32).astype(BF16)  44.8 us
    convert_element_type x16, other arithmetic, move(): sum((pick(t, 1 - own).astype(F32) for t in terms)).astype(BF16)  36.3 us
    pallas_call x1, Pallas kernels, project(): pl.pallas_call(project_kernel, in_specs=[in_vmem(), in_vmem(), in_vmem(),...  32.8 us
    pallas_call x1, Pallas kernels, mixer_backward(): pl.pallas_call(backward_kernel, grid=(heads // PAIR, seqs), in_specs=[cub...  32.3 us
    ppermute x24, starting transfers between devices, swap(): lax.ppermute(values, 'dp', [(i, i ^ 1 << bit) for i in range(self.size)])  27.5 us
  transfers between devices with their start and end apart: 31, of which 8 were waited for; matrix products, arithmetic and copies ran while one was open for 29% of the time, Pallas kernels for 23%

profile of v3, /device:TPU:0, one launch (start us, length us, event | category | flops | bytes accessed | tf_op | source)
XLA Modules:
  0.0 525.7 jit_solution(4728836851992253438)
XLA Ops:
  2.0 32.8 %project.1 = (bf16[1024,2048]{1,0:T(8,128)(2,1)}, bf16[1024,2048]{1,0:T(8,128)(2,1)}, f32[3,1024,512]{2,1,0:T(8,128)}, f32[8,1024]{1,0:T(8,128)}) custom-call(bf16[1024,512]{1,0:T(8,128)(2,1)} %x_ref.1, f32[1,2048]{1,0:T(1,128)} %bitcast.218, bf16[8,2048]{1,0:T(8,128)(2,1)} %scatter.4.rate_ref, bf16[3,2048,512]{2,1,0:T(8,128)(2,1)} %weight_ref.1), custom_call_target="tpu_custom_call" | custom-call | tf_op jit(solution)/shard_map/project/pallas_call | solution.py:487
  36.8 23.4 %mixer_forward.1 = (bf16[1024,512]{1,0:T(8,128)(2,1)S(1)}, f32[1024,512]{1,0:T(8,128)}, bf16[4,1024,128]{2,1,0:T(8,128)(2,1)S(1)}, bf16[4,1024,128]{2,1,0:T(8,12...) custom-call(f32[3,1024,512]{2,1,0:T(8,128)} %get-tuple-element.98.proj_ref,, ...), custom_call_target="tpu_custom_call" | custom-call | tf_op jit(solution)/shard_map/mixer_forward/pallas_call | solution.py:307
  64.1 59.8 %middle_step.1 = (f32[1024,512]{1,0:T(8,128)}, bf16[1024,2048]{1,0:T(8,128)(2,1)}, bf16[1024,2048]{1,0:T(8,128)(2,1)}, bf16[1024,1408]{1,0:T(8,128)(2,1)}, bf16[...) custom-call(bf16[1024,512]{1,0:T(8,128)(2,1)} %copy-done, ...), custom_call_target="tpu_custom_call" | custom-call | tf_op jit(solution)/shard_map/middle_step/pallas_call | solution.py:669
  124.0 1.8 constant_dynamic-slice_fusion.44
  126.5 5.1 convolution_convert_fusion.3
  133.6 1.6 copy-done.25
  135.2 5.1 convolution_convert_fusion.2
  140.2 1.6 collective-permute-start.2
  142.2 3.6 fusion.89
  147.3 2.3 convolution_convert_fusion.7
  150.0 67.1 %return_step.1 = (f32[1024,512]{1,0:T(8,128)}, bf16[1024,2048]{1,0:T(8,128)(2,1)}, f32[1024,512]{1,0:T(8,128)}, f32[1,2048]{1,0:T(1,128)}) custom-call(bf16[512,2048]{1,0:T(8,128)(2,1)} %wout_ref.3, f32[1,2048]{1,0:T(1,128)} %bitcast.223, bf16[1024,1408]{1,0:T(8,128)(2,1)} %get-tuple-element.114.gate_ref, bf16[1024,1408]{1,0:T(8,128)(2,1)} %get-tuple-element.108.up_ref, ...), custom_call_target="tpu_custom_call" | custom-call | tf_op jit(solution)/shard_map/return_step/pallas_call | solution.py:822
  217.1 1.8 constant_dynamic-slice_fusion.36
  220.0 3.2 constant_dynamic-slice_fusion.24
  223.2 4.3 convolution_convert_fusion.1
  227.5 3.9 fusion.110
  233.0 2.2 fusion.107
  237.0 3.7 convolution_convert_fusion
  240.8 3.8 fusion.111
  247.0 2.4 fusion.86
  249.4 3.0 fusion.117
  252.9 32.3 %mixer_backward.1 = (bf16[3,1024,512]{2,1,0:T(8,128)(2,1)}, bf16[4,1,1024]{2,1,0:T(2,128)(2,1)S(1)}, f32[3,4,512]{2,1,0:T(4,128)S(1)}, f32[1,128]{1,0:T(1,128)S(1)}) custom-call(f32[3,1024,512]{2,1,0:T(8,128)} %get-tuple-element.98.proj_ref, s32[2,1,512]{2,1,0:T(1,128)S(1)} %reshape.335.seg_ref, f32[3,4,512]{2,1,0:T(4,128)S(1)} %convert_element_type.511.weight_ref, ...), custom_call_target="tpu_custom_call" | custom-call | tf_op jit(solution)/shard_map/mixer_backward/pallas_call | solution.py:344
  285.3 3.2 slice_bitcast_fusion.1
  288.5 2.7 fusion.116
  292.8 2.8 fusion.120
  295.7 2.3 convolution_convert_fusion.6
  298.6 6.7 %fusion.158 = f32[1024,2048,1]{1,0,2:T(8,128)S(1)} fusion(bf16[3,1024,512]{2,1,0:T(8,128)(2,1)S(1)} %copy-done.23, bf16[3,2048,512]{2,1,0:T(8,128)(2,1)S(1)} %bitcast.182), kind=kOutput, calls=%fused_computation.257 | convolution fusion | flops 6442450944 | bytes 17825792 | tf_op jit(solution)/shard_map/ctk,cdk->td/dot_general | solution.py:1016
  306.2 3.3 fusion.7
  309.5 2.3 fusion.6
  311.8 4.2 fusion.115
  319.6 2.3 fusion.121
  322.0 1.6 collective-permute-start.8
  323.6 2.2 convolution_convert_fusion.5
  328.5 1.6 pad_maximum_fusion.4
  331.4 2.6 collective-permute-start.21
  335.3 4.3 convolution_convert_fusion.4
  340.1 2.4 fusion.119
  345.8 7.8 %collective-permute-done.9 = bf16[2,256,512]{2,1,0:T(8,128)(2,1)} collective-permute-done((bf16[2,256,512]{2,1,0:T(8,128)(2,1)}, bf16[2,256,512]{2,1,0:T(8,128)(2,1)}, u32[]{:S(2)}, u32[]{:S(2)}) %collective-permute-start.9) | collective-permute-done | bytes 524320 | tf_op jit(solution)/shard_map/ppermute | solution.py:901
  353.6 1.9 fusion.138
  356.0 1.9 fusion.137
  359.5 17.5 %collective-permute-done.14 = bf16[1072,512]{1,0:T(8,128)(2,1)S(1)} collective-permute-done((bf16[1072,512]{1,0:T(8,128)(2,1)S(1)}, bf16[1072,512]{1,0:T(8,128)(2,1)S(1)}, u32[]{:S(2)}, u32[]{:S(2)}) %collective-permute-start.14) | collective-permute-done | bytes 1097760 | tf_op jit(solution)/shard_map/ppermute | solution.py:901
  380.0 2.3 fusion.92
  382.7 2.1 fusion.113
  385.3 1.6 pad_maximum_fusion.3
  386.9 1.8 copy.29
  388.7 19.3 %collective-permute-done.20 = bf16[2,256,512]{2,1,0:T(8,128)(2,1)} collective-permute-done((bf16[2,256,512]{2,1,0:T(8,128)(2,1)}, bf16[2,256,512]{2,1,0:T(8,128)(2,1)}, u32[]{:S(2)}, u32[]{:S(2)}) %collective-permute-start.20) | collective-permute-done | bytes 524320 | tf_op jit(solution)/shard_map/ppermute | solution.py:901
  408.6 1.9 fusion.136
  410.6 2.3 collective-permute-start.29
  412.9 2.2 fusion.123
  415.0 5.3 %collective-permute-done.18 = bf16[560,512]{1,0:T(8,128)(2,1)} collective-permute-done((bf16[560,512]{1,0:T(8,128)(2,1)}, bf16[560,512]{1,0:T(8,128)(2,1)}, u32[]{:S(2)}, u32[]{:S(2)}) %collective-permute-start.18) | collective-permute-done | bytes 573472 | tf_op jit(solution)/shard_map/ppermute | solution.py:901
  424.1 2.8 add_convert_fusion.4
  427.9 2.1 fusion.114
  430.0 25.8 %collective-permute-done.24 = bf16[304,512]{1,0:T(8,128)(2,1)S(1)} collective-permute-done((bf16[304,512]{1,0:T(8,128)(2,1)S(1)}, bf16[304,512]{1,0:T(8,128)(2,1)S(1)}, u32[]{:S(2)}, u32[]{:S(2)}) %collective-permute-start.24) | collective-permute-done | bytes 311328 | tf_op jit(solution)/shard_map/ppermute | solution.py:901
  456.7 4.9 slice.93
  467.6 2.1 collective-permute-start.26
  469.7 4.1 add_convert_fusion.3
  474.5 2.1 fusion.131
  476.7 2.0 copy.28
  478.7 1.8 add_convert_fusion.5
  482.9 1.7 fusion.118
  484.7 1.8 pad_maximum_fusion
  486.5 18.6 %collective-permute-done.16 = bf16[1024,512]{1,0:T(8,128)(2,1)S(1)} collective-permute-done((bf16[1024,512]{1,0:T(8,128)(2,1)S(1)}, bf16[1024,512]{1,0:T(8,128)(2,1)S(1)}, u32[]{:S(2)}, u32[]{:S(2)}) %collective-permute-start.16) | collective-permute-done | bytes 1048608 | tf_op jit(solution)/shard_map/ppermute | solution.py:977
  505.1 3.3 add_convert_fusion.2
  509.5 2.0 collective-permute-start.30
  514.1 8.8 %collective-permute-done.30 = bf16[256,512]{1,0:T(8,128)(2,1)S(1)} collective-permute-done((bf16[256,512]{1,0:T(8,128)(2,1)S(1)}, bf16[256,512]{1,0:T(8,128)(2,1)S(1)}, u32[]{:S(2)}, u32[]{:S(2)}) %collective-permute-start.30) | collective-permute-done | bytes 262176 | tf_op jit(solution)/shard_map/ppermute | solution.py:901
  (226 shorter events, 62.4 us)
Async XLA Ops:
  2.0 32.8 %copy-start.33 = (bf16[1024,512]{1,0:T(8,128)(2,1)S(1)}, bf16[1024,512]{1,0:T(8,128)(2,1)}, u32[]{:S(2)}) copy-start(bf16[1024,512]{1,0:T(8,128)(2,1)} %own_ref.1) | copy-start | bytes 3145732
  2.0 33.9 %copy-start.51 = (bf16[3,4,512]{2,1,0:T(4,128)(2,1)S(1)}, bf16[3,4,512]{2,1,0:T(4,128)(2,1)}, u32[]{:S(2)}) copy-start(bf16[3,4,512]{2,1,0:T(4,128)(2,1)} %param.18) | copy-start | bytes 36868
  2.0 33.9 %copy-start.52 = (s32[2,512]{1,0:T(2,128)S(1)}, s32[2,512]{1,0:T(2,128)}, u32[]{:S(2)}) copy-start(s32[2,512]{1,0:T(2,128)} %param.15) | copy-start | bytes 12292
  2.0 34.0 %copy-start.11 = (f32[128]{0:T(128)S(1)}, f32[128]{0:T(128)}, u32[]{:S(2)}) copy-start(f32[128]{0:T(128)} %param.20) | copy-start | bytes 1540
  34.8 29.3 %collective-permute-start = (bf16[1024,512]{1,0:T(8,128)(2,1)S(1)}, bf16[1024,512]{1,0:T(8,128)(2,1)}, u32[]{:S(2)}, u32[]{:S(2)}) collective-permute-start(bf16[1024,512]{1,0:T(8,128)(2,1)S(1)} %copy-done.33), channel_id=1, source_target_pairs={{0,2},{1,3},{2,0},{3,1},{4,6},{5,7},{6,4},{7,5},{8,10},{9,11},{10,... | collective-permute-start | bytes 3145736 | tf_op jit(solution)/shard_map/ppermute | solution.py:977
  126.5 6.6 %copy-start.15 = (bf16[1024,2048]{1,0:T(8,128)(2,1)S(1)}, bf16[1024,2048]{1,0:T(8,128)(2,1)}, u32[]{:S(2)}) copy-start(bf16[1024,2048]{1,0:T(8,128)(2,1)} %get-tuple-element.135) | copy-start | bytes 12582916
  131.5 96.0 %collective-permute-start.1 = (bf16[2,2,256,1408]{3,2,1,0:T(8,128)(2,1)}, bf16[2,2,256,1408]{3,2,1,0:T(8,128)(2,1)}, u32[]{:S(2)}, u32[]{:S(2)}) collective-permute-start(bf16[2,2,256,1408]{3,2,1,0:T(8,128)(2,1)} %bitcast.4), channel_id=1, source_target_pairs={{0,4},{4,0},{8,12},{12,8},{16,20},{20,16},{24,28},{28,24},{1,5},{5... | collective-permute-start | bytes 8650760 | tf_op jit(solution)/shard_map/ppermute | solution.py:901
  140.2 100.6 %collective-permute-start.2 = (bf16[2,2,256,1408]{3,2,1,0:T(8,128)(2,1)}, bf16[2,2,256,1408]{3,2,1,0:T(8,128)(2,1)}, u32[]{:S(2)}, u32[]{:S(2)}) collective-permute-start(bf16[2,2,256,1408]{3,2,1,0:T(8,128)(2,1)} %bitcast.5), channel_id=1, source_target_pairs={{0,8},{4,12},{8,0},{12,4},{16,24},{20,28},{24,16},{28,20},{1,9},{5... | collective-permute-start | bytes 8650760 | tf_op jit(solution)/shard_map/ppermute | solution.py:901
  145.8 103.7 %collective-permute-start.4 = (bf16[2,2,256,896]{3,2,1,0:T(8,128)(2,1)}, bf16[2,2,256,896]{3,2,1,0:T(8,128)(2,1)}, u32[]{:S(2)}, u32[]{:S(2)}) collective-permute-start(bf16[2,2,256,896]{3,2,1,0:T(8,128)(2,1)} %bitcast.6), channel_id=1, source_target_pairs={{0,4},{4,0},{8,12},{12,8},{16,20},{20,16},{24,28},{28,24},{1,5},{5... | collective-permute-start | bytes 5505032 | tf_op jit(solution)/shard_map/ppermute | solution.py:901
  149.5 143.3 %collective-permute-start.6 = (bf16[2,2,256,512]{3,2,1,0:T(8,128)(2,1)}, bf16[2,2,256,512]{3,2,1,0:T(8,128)(2,1)}, u32[]{:S(2)}, u32[]{:S(2)}) collective-permute-start(bf16[2,2,256,512]{3,2,1,0:T(8,128)(2,1)} %bitcast.7), channel_id=1, source_target_pairs={{0,8},{4,12},{8,0},{12,4},{16,24},{20,28},{24,16},{28,20},{1,9},{5... | collective-permute-start | bytes 3145736 | tf_op jit(solution)/shard_map/ppermute | solution.py:901
  227.5 5.5 %copy-start.28 = (bf16[1024,1408]{1,0:T(8,128)(2,1)}, bf16[1024,1408]{1,0:T(8,128)(2,1)S(1)}, u32[]{:S(2)}) copy-start(bf16[1024,1408]{1,0:T(8,128)(2,1)S(1)} %convolution_convert_fusion.1) | copy-start | bytes 8650756
  227.5 5.5 %copy-start.1 = (bf16[1024,512]{1,0:T(8,128)(2,1)S(1)}, bf16[1024,512]{1,0:T(8,128)(2,1)}, u32[]{:S(2)}) copy-start(bf16[1024,512]{1,0:T(8,128)(2,1)} %copy-done) | copy-start | bytes 3145732
  231.4 57.1 %collective-permute-start.5 = (bf16[2,256,1408]{2,1,0:T(8,128)(2,1)}, bf16[2,256,1408]{2,1,0:T(8,128)(2,1)}, u32[]{:S(2)}, u32[]{:S(2)}) collective-permute-start(bf16[2,256,1408]{2,1,0:T(8,128)(2,1)} %fusion.110), channel_id=1, source_target_pairs={{0,8},{4,12},{8,0},{12,4},{16,24},{20,28},{24,16},{28,20},{1,9},{5... | collective-permute-start | bytes 4325384 | tf_op jit(solution)/shard_map/ppermute | solution.py:901
  240.8 6.2 %copy-start.27 = (bf16[1024,1408]{1,0:T(8,128)(2,1)}, bf16[1024,1408]{1,0:T(8,128)(2,1)S(1)}, u32[]{:S(2)}) copy-start(bf16[1024,1408]{1,0:T(8,128)(2,1)S(1)} %convolution_convert_fusion) | copy-start | bytes 8650756
  244.6 67.2 %collective-permute-start.3 = (bf16[2,256,1408]{2,1,0:T(8,128)(2,1)}, bf16[2,256,1408]{2,1,0:T(8,128)(2,1)}, u32[]{:S(2)}, u32[]{:S(2)}) collective-permute-start(bf16[2,256,1408]{2,1,0:T(8,128)(2,1)} %fusion.111), channel_id=1, source_target_pairs={{0,4},{4,0},{8,12},{12,8},{16,20},{20,16},{24,28},{28,24},{1,5},{5... | collective-permute-start | bytes 4325384 | tf_op jit(solution)/shard_map/ppermute | solution.py:901
  245.2 74.5 %collective-permute-start.7 = (bf16[2,2,256,512]{3,2,1,0:T(8,128)(2,1)}, bf16[2,2,256,512]{3,2,1,0:T(8,128)(2,1)}, u32[]{:S(2)}, u32[]{:S(2)}) collective-permute-start(bf16[2,2,256,512]{3,2,1,0:T(8,128)(2,1)} %bitcast.10), channel_id=1, source_target_pairs={{0,4},{4,0},{8,12},{12,8},{16,20},{20,16},{24,28},{28,24},{1,5},{5... | collective-permute-start | bytes 3145736 | tf_op jit(solution)/shard_map/ppermute | solution.py:901
  247.0 5.9 %copy-start.7 = (bf16[1024,512]{1,0:T(8,128)(2,1)S(1)}, bf16[1024,512]{1,0:T(8,128)(2,1)}, u32[]{:S(2)}) copy-start(bf16[1024,512]{1,0:T(8,128)(2,1)} %copy-done.6) | copy-start | bytes 3145732
  247.0 5.9 %copy-start.8 = (bf16[1024,512]{1,0:T(8,128)(2,1)S(1)}, bf16[1024,512]{1,0:T(8,128)(2,1)}, u32[]{:S(2)}) copy-start(bf16[1024,512]{1,0:T(8,128)(2,1)} %get-tuple-element.128.err_ref) | copy-start | bytes 3145732
  247.0 5.9 %copy-start.10 = (f32[8,1024]{1,0:T(8,128)S(1)}, f32[8,1024]{1,0:T(8,128)}, u32[]{:S(2)}) copy-start(f32[8,1024]{1,0:T(8,128)} %get-tuple-element.99.logit_ref) | copy-start | bytes 98308
  249.4 35.9 %copy-start.30 = (bf16[1024,896]{1,0:T(8,128)(2,1)}, bf16[1024,896]{1,0:T(8,128)(2,1)S(1)}, u32[]{:S(2)}) copy-start(bf16[1024,896]{1,0:T(8,128)(2,1)S(1)} %fusion.86) | copy-start | bytes 5505028
  252.5 87.1 %collective-permute-start.10 = (bf16[2,256,896]{2,1,0:T(8,128)(2,1)}, bf16[2,256,896]{2,1,0:T(8,128)(2,1)}, u32[]{:S(2)}, u32[]{:S(2)}) collective-permute-start(bf16[2,256,896]{2,1,0:T(8,128)(2,1)} %fusion.117), channel_id=1, source_target_pairs={{0,8},{4,12},{8,0},{12,4},{16,24},{20,28},{24,16},{28,20},{1,9},{5... | collective-permute-start | bytes 2752520 | tf_op jit(solution)/shard_map/ppermute | solution.py:901
  285.3 5.9 %copy-start.17 = (bf16[1024,2048]{1,0:T(8,128)(2,1)S(1)}, bf16[1024,2048]{1,0:T(8,128)(2,1)}, u32[]{:S(2)}) copy-start(bf16[1024,2048]{1,0:T(8,128)(2,1)} %get-tuple-element.135) | copy-start | bytes 12582916
  291.4 4.2 copy-start.41
  291.4 4.2 copy-start.42
  291.5 4.2 copy-start.43
  291.5 4.2 copy-start.45
  291.5 6.5 %slice-start = ((s8[6291456]{0:T(1024)(128)(4,1)}), s8[4194304]{0:T(1024)(128)(4,1)S(1)}, s32[]{:S(2)}) async-start(s8[6291456]{0:T(1024)(128)(4,1)} %bitcast.181), calls=%async_computation | async-start | bytes 8388608
  292.8 5.2 copy-start.35
  298.6 6.7 %copy-start.12 = (bf16[1024,2048]{1,0:T(8,128)(2,1)S(1)}, bf16[1024,2048]{1,0:T(8,128)(2,1)}, u32[]{:S(2)}) copy-start(bf16[1024,2048]{1,0:T(8,128)(2,1)} %get-tuple-element.138.x_ref) | copy-start | bytes 12582916
  309.5 8.6 %copy-start.21 = (bf16[1024,2048]{1,0:T(8,128)(2,1)S(1)}, bf16[1024,2048]{1,0:T(8,128)(2,1)}, u32[]{:S(2)}) copy-start(bf16[1024,2048]{1,0:T(8,128)(2,1)} %get-tuple-element.141) | copy-start | bytes 12582916
  311.8 15.4 %copy-start.18 = (bf16[1024,2048]{1,0:T(8,128)(2,1)}, bf16[1024,2048]{1,0:T(8,128)(2,1)S(1)}, u32[]{:S(2)}) copy-start(bf16[1024,2048]{1,0:T(8,128)(2,1)S(1)} %fusion.6) | copy-start | bytes 12582916
  316.0 28.1 %collective-permute-start.13 = (bf16[2,2,256,512]{3,2,1,0:T(8,128)(2,1)}, bf16[2,2,256,512]{3,2,1,0:T(8,128)(2,1)S(1)}, u32[]{:S(2)}, u32[]{:S(2)}) collective-permute-start(bf16[2,2,256,512]{3,2,1,0:T(8,128)(2,1)} %bitcast.21), channel_id=1, source_target_pairs={{0,4},{4,0},{8,12},{12,8},{16,20},{20,16},{24,28},{28,24},{1,5},{5... | collective-permute-start | bytes 3145736 | tf_op jit(solution)/shard_map/ppermute | solution.py:901
  316.6 37.1 %collective-permute-start.9 = (bf16[2,256,512]{2,1,0:T(8,128)(2,1)}, bf16[2,256,512]{2,1,0:T(8,128)(2,1)}, u32[]{:S(2)}, u32[]{:S(2)}) collective-permute-start(bf16[2,256,512]{2,1,0:T(8,128)(2,1)} %fusion.120), channel_id=1, source_target_pairs={{0,4},{4,0},{8,12},{12,8},{16,20},{20,16},{24,28},{28,24},{1,5},{5... | collective-permute-start | bytes 1572872 | tf_op jit(solution)/shard_map/ppermute | solution.py:901
  318.3 5.3 copy-start.44
  318.3 5.2 copy-start.46
  319.6 6.2 %copy-start.36 = (bf16[1024,512]{1,0:T(8,128)(2,1)}, bf16[1024,512]{1,0:T(8,128)(2,1)S(1)}, u32[]{:S(2)}) copy-start(bf16[1024,512]{1,0:T(8,128)(2,1)S(1)} %fusion.101) | copy-start | bytes 3145732
  322.0 33.5 %collective-permute-start.8 = (bf16[2,256,512]{2,1,0:T(8,128)(2,1)}, bf16[2,256,512]{2,1,0:T(8,128)(2,1)}, u32[]{:S(2)}, u32[]{:S(2)}) collective-permute-start(bf16[2,256,512]{2,1,0:T(8,128)(2,1)} %fusion.121), channel_id=1, source_target_pairs={{0,8},{4,12},{8,0},{12,4},{16,24},{20,28},{24,16},{28,20},{1,9},{5... | collective-permute-start | bytes 1572872 | tf_op jit(solution)/shard_map/ppermute | solution.py:901
  325.8 1.6 collective-permute-start.11
  327.5 3.8 collective-permute-start.12
  331.4 50.9 %collective-permute-start.21 = (bf16[256,1408]{1,0:T(8,128)(2,1)}, bf16[256,1408]{1,0:T(8,128)(2,1)S(1)}, u32[]{:S(2)}, u32[]{:S(2)}) collective-permute-start(bf16[256,1408]{1,0:T(8,128)(2,1)} %fusion.116), channel_id=1, source_target_pairs={{0,16},{4,20},{8,24},{12,28},{16,0},{20,4},{24,8},{28,12},{1,17},{... | collective-permute-start | bytes 2162696 | tf_op jit(solution)/shard_map/ppermute | solution.py:901
  335.3 7.2 %copy-start.14 = (bf16[1024,2048]{1,0:T(8,128)(2,1)S(1)}, bf16[1024,2048]{1,0:T(8,128)(2,1)}, u32[]{:S(2)}) copy-start(bf16[1024,2048]{1,0:T(8,128)(2,1)} %get-tuple-element.157) | copy-start | bytes 12582916
  339.6 37.4 %collective-permute-start.14 = (bf16[1072,512]{1,0:T(8,128)(2,1)S(1)}, bf16[1072,512]{1,0:T(8,128)(2,1)S(1)}, u32[]{:S(2)}, u32[]{:S(2)}) collective-permute-start(bf16[1072,512]{1,0:T(8,128)(2,1)S(1)} %pad_maximum_fusion.8), channel_id=1, source_target_pairs={{0,4},{4,0},{8,12},{12,8},{16,20},{20,16},{24,28},{28,24},{1,5},{5... | collective-permute-start | bytes 3293192 | tf_op jit(solution)/shard_map/ppermute | solution.py:901
  344.1 14.1 %copy-start.37 = (bf16[1024,512]{1,0:T(8,128)(2,1)}, bf16[1024,512]{1,0:T(8,128)(2,1)S(1)}, u32[]{:S(2)}) copy-start(bf16[1024,512]{1,0:T(8,128)(2,1)S(1)} %fusion.98) | copy-start | bytes 3145732
  344.1 14.1 %copy-start.34 = (bf16[2,2,256,512]{3,2,1,0:T(8,128)(2,1)}, bf16[2,2,256,512]{3,2,1,0:T(8,128)(2,1)S(1)}, u32[]{:S(2)}) copy-start(bf16[2,2,256,512]{3,2,1,0:T(8,128)(2,1)S(1)} %collective-permute-done.13) | copy-start | bytes 3145732
  344.1 79.3 %collective-permute-start.17 = (bf16[256,1408]{1,0:T(8,128)(2,1)}, bf16[256,1408]{1,0:T(8,128)(2,1)}, u32[]{:S(2)}, u32[]{:S(2)}) collective-permute-start(bf16[256,1408]{1,0:T(8,128)(2,1)} %fusion.115), channel_id=1, source_target_pairs={{0,16},{4,20},{8,24},{12,28},{16,0},{20,4},{24,8},{28,12},{1,17},{... | collective-permute-start | bytes 2162696 | tf_op jit(solution)/shard_map/ppermute | solution.py:901
  353.6 70.5 %collective-permute-start.22 = (bf16[1024,1024]{1,0:T(8,128)(2,1)}, bf16[1024,1024]{1,0:T(8,128)(2,1)}, u32[]{:S(2)}, u32[]{:S(2)}) collective-permute-start(bf16[1024,1024]{1,0:T(8,128)(2,1)} %pad_maximum_fusion.4), channel_id=1, source_target_pairs={{0,1},{1,0},{2,3},{3,2},{4,5},{5,4},{6,7},{7,6},{8,9},{9,8},{10,11... | collective-permute-start | bytes 6291464 | tf_op jit(solution)/shard_map/ppermute | solution.py:977
  355.5 55.0 %collective-permute-start.19 = (bf16[2,2,256,512]{3,2,1,0:T(8,128)(2,1)}, bf16[2,2,256,512]{3,2,1,0:T(8,128)(2,1)}, u32[]{:S(2)}, u32[]{:S(2)}) collective-permute-start(bf16[2,2,256,512]{3,2,1,0:T(8,128)(2,1)} %bitcast.33), channel_id=1, source_target_pairs={{0,4},{4,0},{8,12},{12,8},{16,20},{20,16},{24,28},{28,24},{1,5},{5... | collective-permute-start | bytes 3145736 | tf_op jit(solution)/shard_map/ppermute | solution.py:901
  359.5 20.5 %copy-start.38 = (bf16[1024,512]{1,0:T(8,128)(2,1)}, bf16[1024,512]{1,0:T(8,128)(2,1)S(1)}, u32[]{:S(2)}) copy-start(bf16[1024,512]{1,0:T(8,128)(2,1)S(1)} %fusion.95) | copy-start | bytes 3145732
  377.0 31.0 %collective-permute-start.20 = (bf16[2,256,512]{2,1,0:T(8,128)(2,1)}, bf16[2,256,512]{2,1,0:T(8,128)(2,1)}, u32[]{:S(2)}, u32[]{:S(2)}) collective-permute-start(bf16[2,256,512]{2,1,0:T(8,128)(2,1)} %fusion.122), channel_id=1, source_target_pairs={{0,8},{4,12},{8,0},{12,4},{16,24},{20,28},{24,16},{28,20},{1,9},{5... | collective-permute-start | bytes 1572872 | tf_op jit(solution)/shard_map/ppermute | solution.py:901
  382.3 38.1 %collective-permute-start.18 = (bf16[560,512]{1,0:T(8,128)(2,1)}, bf16[560,512]{1,0:T(8,128)(2,1)}, u32[]{:S(2)}, u32[]{:S(2)}) collective-permute-start(bf16[560,512]{1,0:T(8,128)(2,1)} %pad_maximum_fusion.9), channel_id=1, source_target_pairs={{0,8},{4,12},{8,0},{12,4},{16,24},{20,28},{24,16},{28,20},{1,9},{5... | collective-permute-start | bytes 1720328 | tf_op jit(solution)/shard_map/ppermute | solution.py:901
  408.0 66.5 %collective-permute-start.28 = (bf16[256,896]{1,0:T(8,128)(2,1)}, bf16[256,896]{1,0:T(8,128)(2,1)}, u32[]{:S(2)}, u32[]{:S(2)}) collective-permute-start(bf16[256,896]{1,0:T(8,128)(2,1)} %fusion.119), channel_id=1, source_target_pairs={{0,16},{4,20},{8,24},{12,28},{16,0},{20,4},{24,8},{28,12},{1,17},{... | collective-permute-start | bytes 1376264 | tf_op jit(solution)/shard_map/ppermute | solution.py:901
  410.6 63.2 %collective-permute-start.29 = (bf16[256,512]{1,0:T(8,128)(2,1)}, bf16[256,512]{1,0:T(8,128)(2,1)}, u32[]{:S(2)}, u32[]{:S(2)}) collective-permute-start(bf16[256,512]{1,0:T(8,128)(2,1)} %fusion.137), channel_id=1, source_target_pairs={{0,16},{4,20},{8,24},{12,28},{16,0},{20,4},{24,8},{28,12},{1,17},{... | collective-permute-start | bytes 786440 | tf_op jit(solution)/shard_map/ppermute | solution.py:901
  420.3 58.4 %collective-permute-start.15 = (bf16[1024,1024]{1,0:T(8,128)(2,1)}, bf16[1024,1024]{1,0:T(8,128)(2,1)}, u32[]{:S(2)}, u32[]{:S(2)}) collective-permute-start(bf16[1024,1024]{1,0:T(8,128)(2,1)} %pad_maximum_fusion.3), channel_id=1, source_target_pairs={{0,1},{1,0},{2,3},{3,2},{4,5},{5,4},{6,7},{7,6},{8,9},{9,8},{10,11... | collective-permute-start | bytes 6291464 | tf_op jit(solution)/shard_map/ppermute | solution.py:977
  423.4 32.4 %collective-permute-start.24 = (bf16[304,512]{1,0:T(8,128)(2,1)S(1)}, bf16[304,512]{1,0:T(8,128)(2,1)S(1)}, u32[]{:S(2)}, u32[]{:S(2)}) collective-permute-start(bf16[304,512]{1,0:T(8,128)(2,1)S(1)} %pad_maximum_fusion.10), channel_id=1, source_target_pairs={{0,16},{4,20},{8,24},{12,28},{16,0},{20,4},{24,8},{28,12},{1,17},{... | collective-permute-start | bytes 933896 | tf_op jit(solution)/shard_map/ppermute | solution.py:901
  426.9 40.8 %collective-permute-start.23 = (bf16[1024,512]{1,0:T(8,128)(2,1)}, bf16[1024,512]{1,0:T(8,128)(2,1)}, u32[]{:S(2)}, u32[]{:S(2)}) collective-permute-start(bf16[1024,512]{1,0:T(8,128)(2,1)} %add_convert_fusion.4), channel_id=1, source_target_pairs={{0,2},{1,3},{2,0},{3,1},{4,6},{5,7},{6,4},{7,5},{8,10},{9,11},{10,... | collective-permute-start | bytes 3145736 | tf_op jit(solution)/shard_map/ppermute | solution.py:977
  455.8 11.8 %copy-start.40 = (bf16[304,512]{1,0:T(8,128)(2,1)}, bf16[304,512]{1,0:T(8,128)(2,1)S(1)}, u32[]{:S(2)}) copy-start(bf16[304,512]{1,0:T(8,128)(2,1)S(1)} %collective-permute-done.24) | copy-start | bytes 933892
  455.8 18.8 %collective-permute-start.27 = (bf16[256,512]{1,0:T(8,128)(2,1)}, bf16[256,512]{1,0:T(8,128)(2,1)}, u32[]{:S(2)}, u32[]{:S(2)}) collective-permute-start(bf16[256,512]{1,0:T(8,128)(2,1)} %fusion.138), channel_id=1, source_target_pairs={{0,16},{4,20},{8,24},{12,28},{16,0},{20,4},{24,8},{28,12},{1,17},{... | collective-permute-start | bytes 786440 | tf_op jit(solution)/shard_map/ppermute | solution.py:901
  467.6 40.8 %collective-permute-start.26 = (bf16[2,256,512]{2,1,0:T(8,128)(2,1)}, bf16[2,256,512]{2,1,0:T(8,128)(2,1)}, u32[]{:S(2)}, u32[]{:S(2)}) collective-permute-start(bf16[2,256,512]{2,1,0:T(8,128)(2,1)} %fusion.123), channel_id=1, source_target_pairs={{0,8},{4,12},{8,0},{12,4},{16,24},{20,28},{24,16},{28,20},{1,9},{5... | collective-permute-start | bytes 1572872 | tf_op jit(solution)/shard_map/ppermute | solution.py:901
  469.7 4.1 copy-start.47
  473.8 37.7 %collective-permute-start.25 = (bf16[256,512]{1,0:T(8,128)(2,1)S(1)}, bf16[256,512]{1,0:T(8,128)(2,1)}, u32[]{:S(2)}, u32[]{:S(2)}) collective-permute-start(bf16[256,512]{1,0:T(8,128)(2,1)S(1)} %copy-done.47), channel_id=1, source_target_pairs={{0,16},{4,20},{8,24},{12,28},{16,0},{20,4},{24,8},{28,12},{1,17},{... | collective-permute-start | bytes 786440 | tf_op jit(solution)/shard_map/ppermute | solution.py:901
  480.5 24.6 %collective-permute-start.16 = (bf16[1024,512]{1,0:T(8,128)(2,1)S(1)}, bf16[1024,512]{1,0:T(8,128)(2,1)S(1)}, u32[]{:S(2)}, u32[]{:S(2)}) collective-permute-start(bf16[1024,512]{1,0:T(8,128)(2,1)S(1)} %add_convert_fusion.5), channel_id=1, source_target_pairs={{0,2},{1,3},{2,0},{3,1},{4,6},{5,7},{6,4},{7,5},{8,10},{9,11},{10,... | collective-permute-start | bytes 3145736 | tf_op jit(solution)/shard_map/ppermute | solution.py:977
  484.7 20.4 %copy-start.29 = (f32[1024,512]{1,0:T(8,128)S(1)}, f32[1024,512]{1,0:T(8,128)}, u32[]{:S(2)}) copy-start(f32[1024,512]{1,0:T(8,128)} %get-tuple-element.103) | copy-start | bytes 6291460
  505.1 7.7 %slice-start.2 = ((bf16[304,512]{1,0:T(8,128)(2,1)}), bf16[256,512]{1,0:T(8,128)(2,1)S(1)}, s32[]{:S(2)}) async-start(bf16[304,512]{1,0:T(8,128)(2,1)} %copy-done.40), calls=%async_computation.2 | async-start | bytes 524288 | tf_op jit(solution)/shard_map/slice | solution.py:911
  509.5 13.4 %collective-permute-start.30 = (bf16[256,512]{1,0:T(8,128)(2,1)S(1)}, bf16[256,512]{1,0:T(8,128)(2,1)S(1)}, u32[]{:S(2)}, u32[]{:S(2)}) collective-permute-start(bf16[256,512]{1,0:T(8,128)(2,1)S(1)} %fusion.129), channel_id=1, source_target_pairs={{0,16},{4,20},{8,24},{12,28},{16,0},{20,4},{24,8},{28,12},{1,17},{... | collective-permute-start | bytes 786440 | tf_op jit(solution)/shard_map/ppermute | solution.py:901
  (25 other events, 52.5 us)

commit v4 on v3

--- a/solution.py
+++ b/solution.py
@@ -452,8 +452,8 @@
         onward(m).start()
 
     def both(m):
-        relay(m)
-        compute(m - 1)
+        pl.when(m < chunks)(lambda: relay(m))
+        pl.when(m > 0)(lambda: compute(m - 1))
 
     def finish(m):
         to_far(m).wait_send()
@@ -464,10 +464,8 @@
         out_proj(m).wait()
 
     loop(0, chunks, begin)
-    relay(0)
     load.wait()
-    loop(1, chunks, both)
-    compute(chunks - 1)
+    loop(0, chunks + 1, both)
     loop(0, chunks, finish)
 
 
@@ -570,8 +568,8 @@
         send_second(m).start()
 
     def feed(m):
-        project_out(m)
-        pair_sum(m - 1)
+        pl.when(m < chunks)(lambda: project_out(m))
+        pl.when(m > 0)(lambda: pair_sum(m - 1))
 
     def grad_hidden(m):
         ghid[band(m), :] = lax.dot_general(cot[band(m), :], wdown[...], (((1,), (1,)), ((), ())), preferred_element_type=F32)
@@ -618,15 +616,13 @@
         out_ffn(m).start()
 
     def both(m):
-        total(m)
-        compute(m - 1)
-
+        pl.when(m < chunks)(lambda: total(m))
+        pl.when(m > 0)(lambda: compute(m - 1))
+
+    shares = [push(cot.at[:, at], cot.at[:, at], cot_send.at[i], cot_recv.at[i], near) for i, at in enumerate((mine, theirs))]
+    loop(0, chunks + 1, feed)
     loads[0].wait()
     loads[1].wait()
-    shares = [push(cot.at[:, at], cot.at[:, at], cot_send.at[i], cot_recv.at[i], near) for i, at in enumerate((mine, theirs))]
-    project_out(0)
-    loop(1, chunks, feed)
-    pair_sum(chunks - 1)
     for copy in shares:
         copy.start()
     loads[2].wait()
@@ -637,9 +633,7 @@
     save.start()
     loop(0, chunks, grad_hidden)
     loads[4].wait()
-    total(0)
-    loop(1, chunks, both)
-    compute(chunks - 1)
+    loop(0, chunks + 1, both)
 
     def finish(m):
         send_first(m).wait_send()
@@ -767,8 +761,8 @@
         send_second(m).start()
 
     def feed(m):
-        partial(m)
-        pair_sum(m - 1)
+        pl.when(m < chunks)(lambda: partial(m))
+        pl.when(m > 0)(lambda: pair_sum(m - 1))
 
     def total(m):
         send_second(m).wait_recv()
@@ -789,8 +783,8 @@
         outs(m)[2].start()
 
     def both(m):
-        total(m)
-        compute(m - 1)
+        pl.when(m < chunks)(lambda: total(m))
+        pl.when(m > 0)(lambda: compute(m - 1))
 
     def finish(m):
         send_first(m).wait_send()
@@ -802,13 +796,9 @@
 
     for load in loads[:5]:
         load.wait()
-    partial(0)
-    loop(1, chunks, feed)
-    pair_sum(chunks - 1)
+    loop(0, chunks + 1, feed)
     loads[5].wait()
-    total(0)
-    loop(1, chunks, both)
-    compute(chunks - 1)
+    loop(0, chunks + 1, both)
     loop(0, chunks, finish)
 
 
@@ -922,14 +912,24 @@
         return row_major(grad).reshape((2,) * (self.bits - 1) + (2 * rows.shape[1] // self.size, values.shape[1]))
 
     def scatter(self, name, rows, values, bit, ride=False):
-        away = self.product(self.half(rows, bit, True), self.after(values))
+        whole = bit == 0 and values.shape[1] * 4 <= rows.shape[1]
+        if whole:
+            own = lax.rem(lax.div(lax.axis_index("dp"), 1 << bit), 2)
+            grad = lax.dot_general(rows, self.after(values), ROWS, preferred_element_type=F32).astype(BF16)
+            blocks = row_major(grad).reshape((2,) * self.bits + (rows.shape[1] // self.size, values.shape[1]))
+            away = row_major(lax.dynamic_index_in_dim(blocks, 1 - own, self.bits - 1 - bit, keepdims=False))
+        else:
+            away = self.product(self.half(rows, bit, True), self.after(values))
         self.token = away
         came = self.send(away, bit, ride)
         self.rides[name] = ride
         order = [bit] + [i for i in range(self.bits) if i != bit]
         axes = [i for i in range(self.bits)[::-1] if i != bit]
         self.open[name] = ([came], axes, order, 1)
-        self.later[name] = (rows, values, bit)
+        if whole:
+            self.open[name] = ([lax.dynamic_index_in_dim(blocks, own, self.bits - 1 - bit, keepdims=False), came], axes, order, 1)
+        else:
+            self.later[name] = (rows, values, bit)
 
     def keep(self, name):
         rows, values, bit = self.later.pop(name)
@@ -1037,11 +1037,9 @@
         line.move("upz")
         line.move("out")
         one, one_far = quarter_sum(lambda q: columns(part_one, q).astype(F32))
-        line.keep("v")
         line.move("v")
         late_ffn = line.after(ffn_part)
         ffn, ffn_far = quarter_sum(lambda q: columns(late_ffn, q).astype(F32))
-        line.keep("q")
         grad_down = line.close("down").T
         line.token = grad_down
         line.move("k")

time: 535 us -> 539 us (level)
  local copies, waits for them, and re-layouts: 42.8 us -> 49.5 us
    dot_general x16 -> x8, matrix products: 44.8 us -> 27.7 us  [product(): lax.dot_general(rows, values, ROWS, preferred_element_type=F32).astype(BF16)]
    dot_general x0 -> x4, matrix products: none -> 11.9 us  [scatter(): lax.dot_general(rows, self.after(values), ROWS, preferred_element_type=F32)]
    unnamed x123 -> x115, local copies, waits for them, and re-layouts: 18.5 us -> 22 us
  transfers between devices with their start and end apart: 31 -> 31, of which waited for: 8 -> 7; matrix products, arithmetic and copies ran while one was open for 29% -> 28% of each run, Pallas kernels for 23% -> 23%
where the time goes in v4:
time: 539 us; the launch traced here: 529 us
  Pallas kernels  214 us (40%)
  waiting for transfers between devices  109 us (20%)
  other arithmetic  74.1 us (14%)
  matrix products  50.9 us (9%)
  local copies, waits for them, and re-layouts  49.5 us (9%)
  starting transfers between devices  29.4 us (5%)
    ppermute x24, waiting for transfers between devices, swap(): lax.ppermute(values, 'dp', [(i, i ^ 1 << bit) for i in range(self.size)])  89.4 us
    pallas_call x1, Pallas kernels, return_step(): pl.pallas_call(return_kernel, in_specs=[in_vmem(), in_vmem()] + [in_hbm()...  66.4 us
    pallas_call x1, Pallas kernels, middle_step(): pl.pallas_call(middle_kernel, in_specs=[in_vmem(), in_vmem(), in_vmem()]...  59.2 us
    convert_element_type x16, other arithmetic, move(): sum((pick(t, 1 - own).astype(F32) for t in terms)).astype(BF16)  37.4 us
    pallas_call x1, Pallas kernels, project(): pl.pallas_call(project_kernel, in_specs=[in_vmem(), in_vmem(), in_vmem(),...  32.8 us
    pallas_call x1, Pallas kernels, mixer_backward(): pl.pallas_call(backward_kernel, grid=(heads // PAIR, seqs), in_specs=[cub...  32.3 us
    dot_general x8, matrix products, product(): lax.dot_general(rows, values, ROWS, preferred_element_type=F32).astype(BF16)  27.7 us
    ppermute x24, starting transfers between devices, swap(): lax.ppermute(values, 'dp', [(i, i ^ 1 << bit) for i in range(self.size)])  24.8 us
  transfers between devices with their start and end apart: 31, of which 7 were waited for; matrix products, arithmetic and copies ran while one was open for 28% of the time, Pallas kernels for 23%

profile of v4, /device:TPU:0, one launch (start us, length us, event | category | flops | bytes accessed | tf_op | source)
XLA Modules:
  0.0 528.9 jit_solution(17302544776870693557)
XLA Ops:
  2.0 32.8 %project.1 = (bf16[1024,2048]{1,0:T(8,128)(2,1)}, bf16[1024,2048]{1,0:T(8,128)(2,1)}, f32[3,1024,512]{2,1,0:T(8,128)}, f32[8,1024]{1,0:T(8,128)}) custom-call(bf16[1024,512]{1,0:T(8,128)(2,1)} %x_ref.1, f32[1,2048]{1,0:T(1,128)} %bitcast.277, bf16[8,2048]{1,0:T(8,128)(2,1)} %scatter.4.rate_ref, bf16[3,2048,512]{2,1,0:T(8,128)(2,1)} %weight_ref.1), custom_call_target="tpu_custom_call" | custom-call | tf_op jit(solution)/shard_map/project/pallas_call | solution.py:485
  36.8 23.4 %mixer_forward.1 = (bf16[1024,512]{1,0:T(8,128)(2,1)S(1)}, f32[1024,512]{1,0:T(8,128)}, bf16[4,1024,128]{2,1,0:T(8,128)(2,1)S(1)}, bf16[4,1024,128]{2,1,0:T(8,12...) custom-call(f32[3,1024,512]{2,1,0:T(8,128)} %get-tuple-element.94.proj_ref,, ...), custom_call_target="tpu_custom_call" | custom-call | tf_op jit(solution)/shard_map/mixer_forward/pallas_call | solution.py:307
  64.1 59.2 %middle_step.1 = (f32[1024,512]{1,0:T(8,128)}, bf16[1024,2048]{1,0:T(8,128)(2,1)}, bf16[1024,2048]{1,0:T(8,128)(2,1)}, bf16[1024,1408]{1,0:T(8,128)(2,1)}, bf16[...) custom-call(bf16[1024,512]{1,0:T(8,128)(2,1)} %copy-done.7, ...), custom_call_target="tpu_custom_call" | custom-call | tf_op jit(solution)/shard_map/middle_step/pallas_call | solution.py:663
  123.3 1.8 constant_dynamic-slice_fusion.21
  125.8 5.2 convolution_convert_fusion.3
  131.0 1.6 collective-permute-start.1
  134.0 1.8 slice.80
  137.6 4.8 convolution_convert_fusion.2
  142.5 1.6 collective-permute-start.2
  144.3 3.6 fusion.49
  148.5 2.3 convolution_convert_fusion.8
  151.2 66.4 %return_step.1 = (f32[1024,512]{1,0:T(8,128)}, bf16[1024,2048]{1,0:T(8,128)(2,1)}, f32[1024,512]{1,0:T(8,128)}, f32[1,2048]{1,0:T(1,128)}) custom-call(bf16[512,2048]{1,0:T(8,128)(2,1)} %wout_ref.3, f32[1,2048]{1,0:T(1,128)} %bitcast.282, bf16[1024,1408]{1,0:T(8,128)(2,1)} %get-tuple-element.116.gate_ref, bf16[1024,1408]{1,0:T(8,128)(2,1)} %get-tuple-element.110.up_ref, ...), custom_call_target="tpu_custom_call" | custom-call | tf_op jit(solution)/shard_map/return_step/pallas_call | solution.py:812
  217.7 1.8 constant_dynamic-slice_fusion.17
  220.1 4.3 convolution_convert_fusion.1
  224.5 3.9 fusion.55
  228.4 1.6 collective-permute-start.6
  230.0 2.5 convolution_convert_fusion.7
  235.1 1.6 copy-done.21
  236.7 3.8 convolution_convert_fusion
  240.5 1.6 copy-done.22
  242.1 2.8 fusion.56
  247.2 2.4 fusion.46
  249.7 3.0 fusion.66
  253.2 32.3 %mixer_backward.1 = (bf16[3,1024,512]{2,1,0:T(8,128)(2,1)}, bf16[4,1,1024]{2,1,0:T(2,128)(2,1)S(1)}, f32[3,4,512]{2,1,0:T(4,128)S(1)}, f32[1,128]{1,0:T(1,128)S(1)}) custom-call(f32[3,1024,512]{2,1,0:T(8,128)} %get-tuple-element.94.proj_ref, s32[2,1,512]{2,1,0:T(1,128)S(1)} %reshape.353.seg_ref, f32[3,4,512]{2,1,0:T(4,128)S(1)} %convert_element_type.535.weight_ref, ...), custom_call_target="tpu_custom_call" | custom-call | tf_op jit(solution)/shard_map/mixer_backward/pallas_call | solution.py:344
  285.6 3.4 slice_bitcast_fusion
  289.0 2.5 fusion.61
  293.0 3.0 fusion.69
  297.5 2.5 convolution_convert_fusion.6
  304.2 6.7 %fusion.99 = f32[1024,2048,1]{1,0,2:T(8,128)S(1)} fusion(bf16[3,1024,512]{2,1,0:T(8,128)(2,1)S(1)} %copy-done.19, bf16[3,2048,512]{2,1,0:T(8,128)(2,1)S(1)} %bitcast.236), kind=kOutput, calls=%fused_computation.196 | convolution fusion | flops 6442450944 | bytes 17825792 | tf_op jit(solution)/shard_map/ctk,cdk->td/dot_general | solution.py:1016
  310.9 3.3 fusion.7
  314.2 2.3 fusion.6
  316.5 4.2 fusion.60
  322.2 2.1 fusion.65
  324.3 1.6 collective-permute-start.11
  325.9 2.5 convolution_convert_fusion.5
  328.6 1.7 pad_maximum_fusion.3
  332.2 2.0 collective-permute-done.9
  335.5 4.6 convolution_convert_fusion.4
  341.1 2.6 collective-permute-start.17
  343.7 2.2 fusion.68
  346.3 2.1 fusion.64
  348.5 1.9 fusion.84
  351.3 1.9 fusion.83
  353.2 8.3 %collective-permute-done.10 = bf16[1072,512]{1,0:T(8,128)(2,1)S(1)} collective-permute-done((bf16[1072,512]{1,0:T(8,128)(2,1)S(1)}, bf16[1072,512]{1,0:T(8,128)(2,1)S(1)}, u32[]{:S(2)}, u32[]{:S(2)}) %collective-permute-start.10) | collective-permute-done | bytes 1097760 | tf_op jit(solution)/shard_map/ppermute | solution.py:891
  364.1 41.6 %collective-permute-done.21 = bf16[256,1408]{1,0:T(8,128)(2,1)S(1)} collective-permute-done((bf16[256,1408]{1,0:T(8,128)(2,1)S(1)}, bf16[256,1408]{1,0:T(8,128)(2,1)S(1)}, u32[]{:S(2)}, u32[]{:S(2)}) %collective-permute-start.21) | collective-permute-done | bytes 720928 | tf_op jit(solution)/shard_map/ppermute | solution.py:891
  405.7 1.9 fusion.58
  410.4 2.8 pad_maximum_fusion.2
  413.2 3.2 collective-permute-start.28
  416.3 1.9 fusion.82
  418.3 2.1 fusion.62
  420.5 4.2 collective-permute-done.18
  428.3 2.8 add_convert_fusion.4
  432.2 2.3 fusion.59
  434.5 26.7 %collective-permute-done.24 = bf16[304,512]{1,0:T(8,128)(2,1)S(1)} collective-permute-done((bf16[304,512]{1,0:T(8,128)(2,1)S(1)}, bf16[304,512]{1,0:T(8,128)(2,1)S(1)}, u32[]{:S(2)}, u32[]{:S(2)}) %collective-permute-start.24) | collective-permute-done | bytes 311328 | tf_op jit(solution)/shard_map/ppermute | solution.py:891
  462.8 4.9 slice.93
  472.5 1.6 copy.35
  474.7 2.0 collective-permute-start.26
  476.7 4.0 add_convert_fusion.3
  483.9 1.8 add_convert_fusion.5
  488.1 1.7 fusion.67
  489.9 1.8 pad_maximum_fusion
  491.7 17.6 %collective-permute-done.16 = bf16[1024,512]{1,0:T(8,128)(2,1)S(1)} collective-permute-done((bf16[1024,512]{1,0:T(8,128)(2,1)S(1)}, bf16[1024,512]{1,0:T(8,128)(2,1)S(1)}, u32[]{:S(2)}, u32[]{:S(2)}) %collective-permute-start.16) | collective-permute-done | bytes 1048608 | tf_op jit(solution)/shard_map/ppermute | solution.py:977
  509.2 3.3 add_convert_fusion.2
  517.5 8.6 %collective-permute-done.30 = bf16[256,512]{1,0:T(8,128)(2,1)S(1)} collective-permute-done((bf16[256,512]{1,0:T(8,128)(2,1)S(1)}, bf16[256,512]{1,0:T(8,128)(2,1)S(1)}, u32[]{:S(2)}, u32[]{:S(2)}) %collective-permute-start.30) | collective-permute-done | bytes 262176 | tf_op jit(solution)/shard_map/ppermute | solution.py:891
  (214 shorter events, 62.8 us)
Async XLA Ops:
  2.0 32.8 %copy-start.36 = (bf16[1024,512]{1,0:T(8,128)(2,1)S(1)}, bf16[1024,512]{1,0:T(8,128)(2,1)}, u32[]{:S(2)}) copy-start(bf16[1024,512]{1,0:T(8,128)(2,1)} %own_ref.1) | copy-start | bytes 3145732
  2.0 34.0 %copy-start.47 = (s32[2,512]{1,0:T(2,128)S(1)}, s32[2,512]{1,0:T(2,128)}, u32[]{:S(2)}) copy-start(s32[2,512]{1,0:T(2,128)} %param.15) | copy-start | bytes 12292
  2.0 34.0 %copy-start.46 = (bf16[3,4,512]{2,1,0:T(4,128)(2,1)S(1)}, bf16[3,4,512]{2,1,0:T(4,128)(2,1)}, u32[]{:S(2)}) copy-start(bf16[3,4,512]{2,1,0:T(4,128)(2,1)} %param.18) | copy-start | bytes 36868
  2.0 34.0 %copy-start.11 = (f32[128]{0:T(128)S(1)}, f32[128]{0:T(128)}, u32[]{:S(2)}) copy-start(f32[128]{0:T(128)} %param.20) | copy-start | bytes 1540
  34.8 29.3 %collective-permute-start = (bf16[1024,512]{1,0:T(8,128)(2,1)S(1)}, bf16[1024,512]{1,0:T(8,128)(2,1)}, u32[]{:S(2)}, u32[]{:S(2)}) collective-permute-start(bf16[1024,512]{1,0:T(8,128)(2,1)S(1)} %copy-done.36), channel_id=1, source_target_pairs={{0,2},{1,3},{2,0},{3,1},{4,6},{5,7},{6,4},{7,5},{8,10},{9,11},{10,... | collective-permute-start | bytes 3145736 | tf_op jit(solution)/shard_map/ppermute | solution.py:977
  131.0 93.5 %collective-permute-start.1 = (bf16[2,2,256,1408]{3,2,1,0:T(8,128)(2,1)}, bf16[2,2,256,1408]{3,2,1,0:T(8,128)(2,1)}, u32[]{:S(2)}, u32[]{:S(2)}) collective-permute-start(bf16[2,2,256,1408]{3,2,1,0:T(8,128)(2,1)} %bitcast.4), channel_id=1, source_target_pairs={{0,4},{4,0},{8,12},{12,8},{16,20},{20,16},{24,28},{28,24},{1,5},{5... | collective-permute-start | bytes 8650760 | tf_op jit(solution)/shard_map/ppermute | solution.py:891
  142.5 98.0 %collective-permute-start.2 = (bf16[2,2,256,1408]{3,2,1,0:T(8,128)(2,1)}, bf16[2,2,256,1408]{3,2,1,0:T(8,128)(2,1)}, u32[]{:S(2)}, u32[]{:S(2)}) collective-permute-start(bf16[2,2,256,1408]{3,2,1,0:T(8,128)(2,1)} %bitcast.5), channel_id=1, source_target_pairs={{0,8},{4,12},{8,0},{12,4},{16,24},{20,28},{24,16},{28,20},{1,9},{5... | collective-permute-start | bytes 8650760 | tf_op jit(solution)/shard_map/ppermute | solution.py:891
  147.9 101.8 %collective-permute-start.3 = (bf16[2,2,256,896]{3,2,1,0:T(8,128)(2,1)}, bf16[2,2,256,896]{3,2,1,0:T(8,128)(2,1)}, u32[]{:S(2)}, u32[]{:S(2)}) collective-permute-start(bf16[2,2,256,896]{3,2,1,0:T(8,128)(2,1)} %bitcast.6), channel_id=1, source_target_pairs={{0,4},{4,0},{8,12},{12,8},{16,20},{20,16},{24,28},{28,24},{1,5},{5... | collective-permute-start | bytes 5505032 | tf_op jit(solution)/shard_map/ppermute | solution.py:891
  150.8 142.2 %collective-permute-start.7 = (bf16[2,2,256,512]{3,2,1,0:T(8,128)(2,1)}, bf16[2,2,256,512]{3,2,1,0:T(8,128)(2,1)}, u32[]{:S(2)}, u32[]{:S(2)}) collective-permute-start(bf16[2,2,256,512]{3,2,1,0:T(8,128)(2,1)} %bitcast.7), channel_id=1, source_target_pairs={{0,8},{4,12},{8,0},{12,4},{16,24},{20,28},{24,16},{28,20},{1,9},{5... | collective-permute-start | bytes 3145736 | tf_op jit(solution)/shard_map/ppermute | solution.py:891
  220.1 9.8 %copy-start.48 = (bf16[1024,2048]{1,0:T(8,128)(2,1)S(1)}, bf16[1024,2048]{1,0:T(8,128)(2,1)}, u32[]{:S(2)}) copy-start(bf16[1024,2048]{1,0:T(8,128)(2,1)} %get-tuple-element.119) | copy-start | bytes 12582916
  224.5 64.5 %copy-start.23 = (bf16[1024,1408]{1,0:T(8,128)(2,1)}, bf16[1024,1408]{1,0:T(8,128)(2,1)S(1)}, u32[]{:S(2)}) copy-start(bf16[1024,1408]{1,0:T(8,128)(2,1)S(1)} %convolution_convert_fusion.1) | copy-start | bytes 8650756
  224.5 5.5 %copy-start.8 = (bf16[1024,512]{1,0:T(8,128)(2,1)S(1)}, bf16[1024,512]{1,0:T(8,128)(2,1)}, u32[]{:S(2)}) copy-start(bf16[1024,512]{1,0:T(8,128)(2,1)} %copy-done.7) | copy-start | bytes 3145732
  228.4 60.6 %collective-permute-start.6 = (bf16[2,256,1408]{2,1,0:T(8,128)(2,1)}, bf16[2,256,1408]{2,1,0:T(8,128)(2,1)}, u32[]{:S(2)}, u32[]{:S(2)}) collective-permute-start(bf16[2,256,1408]{2,1,0:T(8,128)(2,1)} %fusion.55), channel_id=1, source_target_pairs={{0,8},{4,12},{8,0},{12,4},{16,24},{20,28},{24,16},{28,20},{1,9},{5... | collective-permute-start | bytes 4325384 | tf_op jit(solution)/shard_map/ppermute | solution.py:891
  230.0 4.9 copy-start.14
  244.9 71.6 %collective-permute-start.5 = (bf16[2,256,1408]{2,1,0:T(8,128)(2,1)}, bf16[2,256,1408]{2,1,0:T(8,128)(2,1)}, u32[]{:S(2)}, u32[]{:S(2)}) collective-permute-start(bf16[2,256,1408]{2,1,0:T(8,128)(2,1)} %fusion.56), channel_id=1, source_target_pairs={{0,4},{4,0},{8,12},{12,8},{16,20},{20,16},{24,28},{28,24},{1,5},{5... | collective-permute-start | bytes 4325384 | tf_op jit(solution)/shard_map/ppermute | solution.py:891
  246.4 75.7 %collective-permute-start.4 = (bf16[2,2,256,512]{3,2,1,0:T(8,128)(2,1)}, bf16[2,2,256,512]{3,2,1,0:T(8,128)(2,1)}, u32[]{:S(2)}, u32[]{:S(2)}) collective-permute-start(bf16[2,2,256,512]{3,2,1,0:T(8,128)(2,1)} %dynamic-slice_bitcast_fusion.2), channel_id=1, source_target_pairs={{0,4},{4,0},{8,12},{12,8},{16,20},{20,16},{24,28},{28,24},{1,5},{5... | collective-permute-start | bytes 3145736 | tf_op jit(solution)/shard_map/ppermute | solution.py:891
  247.2 6.0 %copy-start.5 = (bf16[1024,512]{1,0:T(8,128)(2,1)S(1)}, bf16[1024,512]{1,0:T(8,128)(2,1)}, u32[]{:S(2)}) copy-start(bf16[1024,512]{1,0:T(8,128)(2,1)} %copy-done.4) | copy-start | bytes 3145732
  247.2 6.0 %copy-start.6 = (bf16[1024,512]{1,0:T(8,128)(2,1)S(1)}, bf16[1024,512]{1,0:T(8,128)(2,1)}, u32[]{:S(2)}) copy-start(bf16[1024,512]{1,0:T(8,128)(2,1)} %get-tuple-element.107.err_ref) | copy-start | bytes 3145732
  249.7 3.5 copy-start.33
  249.7 3.5 copy-start.1
  249.7 3.5 copy-start.3
  252.7 88.4 %collective-permute-start.14 = (bf16[2,256,896]{2,1,0:T(8,128)(2,1)}, bf16[2,256,896]{2,1,0:T(8,128)(2,1)}, u32[]{:S(2)}, u32[]{:S(2)}) collective-permute-start(bf16[2,256,896]{2,1,0:T(8,128)(2,1)} %fusion.66), channel_id=1, source_target_pairs={{0,8},{4,12},{8,0},{12,4},{16,24},{20,28},{24,16},{28,20},{1,9},{5... | collective-permute-start | bytes 2752520 | tf_op jit(solution)/shard_map/ppermute | solution.py:891
  291.7 5.8 %copy-start.17 = (bf16[1024,2048]{1,0:T(8,128)(2,1)S(1)}, bf16[1024,2048]{1,0:T(8,128)(2,1)}, u32[]{:S(2)}) copy-start(bf16[1024,2048]{1,0:T(8,128)(2,1)} %get-tuple-element.101) | copy-start | bytes 12582916
  291.7 12.1 %slice-start = ((s8[6291456]{0:T(1024)(128)(4,1)}), s8[4194304]{0:T(1024)(128)(4,1)S(1)}, s32[]{:S(2)}) async-start(s8[6291456]{0:T(1024)(128)(4,1)} %bitcast.235), calls=%async_computation | async-start | bytes 8388608
  293.0 7.0 %copy-start.37 = (bf16[1024,512]{1,0:T(8,128)(2,1)}, bf16[1024,512]{1,0:T(8,128)(2,1)S(1)}, u32[]{:S(2)}) copy-start(bf16[1024,512]{1,0:T(8,128)(2,1)S(1)} %fusion.52) | copy-start | bytes 3145732
  296.0 52.5 %collective-permute-start.12 = (bf16[2,256,512]{2,1,0:T(8,128)(2,1)}, bf16[2,256,512]{2,1,0:T(8,128)(2,1)}, u32[]{:S(2)}, u32[]{:S(2)}) collective-permute-start(bf16[2,256,512]{2,1,0:T(8,128)(2,1)} %fusion.69), channel_id=1, source_target_pairs={{0,4},{4,0},{8,12},{12,8},{16,20},{20,16},{24,28},{28,24},{1,5},{5... | collective-permute-start | bytes 1572872 | tf_op jit(solution)/shard_map/ppermute | solution.py:891
  297.5 5.4 %copy-start.12 = (bf16[1024,2048]{1,0:T(8,128)(2,1)S(1)}, bf16[1024,2048]{1,0:T(8,128)(2,1)}, u32[]{:S(2)}) copy-start(bf16[1024,2048]{1,0:T(8,128)(2,1)} %get-tuple-element.134.x_ref) | copy-start | bytes 12582916
  297.5 6.3 %slice-start.1 = ((s8[6291456]{0:T(1024)(128)(4,1)}), s8[2097152]{0:T(1024)(128)(4,1)S(1)}, s32[]{:S(2)}) async-start(s8[6291456]{0:T(1024)(128)(4,1)} %bitcast.235), calls=%async_computation.1 | async-start | bytes 4194304
  302.3 43.6 %collective-permute-start.13 = (bf16[2,2,256,512]{3,2,1,0:T(8,128)(2,1)}, bf16[2,2,256,512]{3,2,1,0:T(8,128)(2,1)}, u32[]{:S(2)}, u32[]{:S(2)}) collective-permute-start(bf16[2,2,256,512]{3,2,1,0:T(8,128)(2,1)} %dynamic-slice_bitcast_fusion.1), channel_id=1, source_target_pairs={{0,4},{4,0},{8,12},{12,8},{16,20},{20,16},{24,28},{28,24},{1,5},{5... | collective-permute-start | bytes 3145736 | tf_op jit(solution)/shard_map/ppermute | solution.py:891
  304.2 6.7 %copy-start.43 = (f32[2048]{0:T(1024)S(1)}, f32[2048]{0:T(1024)}, u32[]{:S(2)}) copy-start(f32[2048]{0:T(1024)} %param.16) | copy-start | bytes 24580
  304.2 6.7 %copy-start.44 = (bf16[2048,4]{0,1:T(4,128)(2,1)S(1)}, bf16[2048,4]{0,1:T(4,128)(2,1)}, u32[]{:S(2)}) copy-start(bf16[2048,4]{0,1:T(4,128)(2,1)} %param.19) | copy-start | bytes 49156
  316.5 11.8 %copy-start.15 = (bf16[1024,2048]{1,0:T(8,128)(2,1)}, bf16[1024,2048]{1,0:T(8,128)(2,1)S(1)}, u32[]{:S(2)}) copy-start(bf16[1024,2048]{1,0:T(8,128)(2,1)S(1)} %fusion.6) | copy-start | bytes 12582916
  316.5 4.2 copy-start.45
  320.7 5.1 copy-start.40
  320.8 9.6 %collective-permute-start.8 = (f32[4224]{0:T(1024)S(1)}, f32[4224]{0:T(1024)S(1)}, u32[]{:S(2)}, u32[]{:S(2)}) collective-permute-start(f32[4224]{0:T(1024)S(1)} %pad_maximum_fusion.10), channel_id=1, source_target_pairs={{0,1},{1,0},{2,3},{3,2},{4,5},{5,4},{6,7},{7,6},{8,9},{9,8},{10,11... | collective-permute-start | bytes 50696 | tf_op jit(solution)/shard_map/ppermute | solution.py:864
  324.3 26.1 %collective-permute-start.11 = (bf16[2,256,512]{2,1,0:T(8,128)(2,1)}, bf16[2,256,512]{2,1,0:T(8,128)(2,1)}, u32[]{:S(2)}, u32[]{:S(2)}) collective-permute-start(bf16[2,256,512]{2,1,0:T(8,128)(2,1)} %fusion.65), channel_id=1, source_target_pairs={{0,8},{4,12},{8,0},{12,4},{16,24},{20,28},{24,16},{28,20},{1,9},{5... | collective-permute-start | bytes 1572872 | tf_op jit(solution)/shard_map/ppermute | solution.py:891
  330.3 3.8 collective-permute-start.9
  334.2 27.7 %copy-start.24 = (f32[48,512]{1,0:T(8,128)}, f32[48,512]{1,0:T(8,128)S(1)}, u32[]{:S(2)}) copy-start(f32[48,512]{1,0:T(8,128)S(1)} %reduce_precision.13) | copy-start | bytes 294916
  334.3 27.2 %collective-permute-start.10 = (bf16[1072,512]{1,0:T(8,128)(2,1)S(1)}, bf16[1072,512]{1,0:T(8,128)(2,1)S(1)}, u32[]{:S(2)}, u32[]{:S(2)}) collective-permute-start(bf16[1072,512]{1,0:T(8,128)(2,1)S(1)} %pad_maximum_fusion.7), channel_id=1, source_target_pairs={{0,4},{4,0},{8,12},{12,8},{16,20},{20,16},{24,28},{28,24},{1,5},{5... | collective-permute-start | bytes 3293192 | tf_op jit(solution)/shard_map/ppermute | solution.py:891
  340.1 8.4 %copy-start.29 = (bf16[2048,512]{1,0:T(8,128)(2,1)}, bf16[2048,512]{1,0:T(8,128)(2,1)S(1)}, u32[]{:S(2)}) copy-start(bf16[2048,512]{1,0:T(8,128)(2,1)S(1)} %convolution_convert_fusion.4) | copy-start | bytes 6291460
  340.1 5.9 %copy-start.42 = (bf16[256,1408]{1,0:T(8,128)(2,1)S(1)}, bf16[256,1408]{1,0:T(8,128)(2,1)}, u32[]{:S(2)}) copy-start(bf16[256,1408]{1,0:T(8,128)(2,1)} %fusion.61) | copy-start | bytes 2162692
  341.1 86.8 %collective-permute-start.17 = (bf16[256,1408]{1,0:T(8,128)(2,1)}, bf16[256,1408]{1,0:T(8,128)(2,1)}, u32[]{:S(2)}, u32[]{:S(2)}) collective-permute-start(bf16[256,1408]{1,0:T(8,128)(2,1)} %fusion.60), channel_id=1, source_target_pairs={{0,16},{4,20},{8,24},{12,28},{16,0},{20,4},{24,8},{28,12},{1,17},{... | collective-permute-start | bytes 2162696 | tf_op jit(solution)/shard_map/ppermute | solution.py:891
  346.0 59.7 %collective-permute-start.21 = (bf16[256,1408]{1,0:T(8,128)(2,1)S(1)}, bf16[256,1408]{1,0:T(8,128)(2,1)S(1)}, u32[]{:S(2)}, u32[]{:S(2)}) collective-permute-start(bf16[256,1408]{1,0:T(8,128)(2,1)S(1)} %copy-done.42), channel_id=1, source_target_pairs={{0,16},{4,20},{8,24},{12,28},{16,0},{20,4},{24,8},{28,12},{1,17},{... | collective-permute-start | bytes 2162696 | tf_op jit(solution)/shard_map/ppermute | solution.py:891
  348.4 79.9 %collective-permute-start.22 = (bf16[1024,1024]{1,0:T(8,128)(2,1)}, bf16[1024,1024]{1,0:T(8,128)(2,1)}, u32[]{:S(2)}, u32[]{:S(2)}) collective-permute-start(bf16[1024,1024]{1,0:T(8,128)(2,1)} %pad_maximum_fusion.3), channel_id=1, source_target_pairs={{0,1},{1,0},{2,3},{3,2},{4,5},{5,4},{6,7},{7,6},{8,9},{9,8},{10,11... | collective-permute-start | bytes 6291464 | tf_op jit(solution)/shard_map/ppermute | solution.py:977
  350.4 67.9 %collective-permute-start.19 = (bf16[2,2,256,512]{3,2,1,0:T(8,128)(2,1)}, bf16[2,2,256,512]{3,2,1,0:T(8,128)(2,1)}, u32[]{:S(2)}, u32[]{:S(2)}) collective-permute-start(bf16[2,2,256,512]{3,2,1,0:T(8,128)(2,1)} %dynamic-slice_bitcast_fusion), channel_id=1, source_target_pairs={{0,4},{4,0},{8,12},{12,8},{16,20},{20,16},{24,28},{28,24},{1,5},{5... | collective-permute-start | bytes 3145736 | tf_op jit(solution)/shard_map/ppermute | solution.py:891
  361.5 51.7 %collective-permute-start.20 = (bf16[2,256,512]{2,1,0:T(8,128)(2,1)}, bf16[2,256,512]{2,1,0:T(8,128)(2,1)}, u32[]{:S(2)}, u32[]{:S(2)}) collective-permute-start(bf16[2,256,512]{2,1,0:T(8,128)(2,1)} %fusion.64), channel_id=1, source_target_pairs={{0,8},{4,12},{8,0},{12,4},{16,24},{20,28},{24,16},{28,20},{1,9},{5... | collective-permute-start | bytes 1572872 | tf_op jit(solution)/shard_map/ppermute | solution.py:891
  364.1 43.5 %copy-start.18 = (bf16[1024,2048]{1,0:T(8,128)(2,1)S(1)}, bf16[1024,2048]{1,0:T(8,128)(2,1)}, u32[]{:S(2)}) copy-start(bf16[1024,2048]{1,0:T(8,128)(2,1)} %get-tuple-element.149) | copy-start | bytes 12582916
  405.7 19.0 %collective-permute-start.18 = (bf16[560,512]{1,0:T(8,128)(2,1)}, bf16[560,512]{1,0:T(8,128)(2,1)}, u32[]{:S(2)}, u32[]{:S(2)}) collective-permute-start(bf16[560,512]{1,0:T(8,128)(2,1)} %pad_maximum_fusion.8), channel_id=1, source_target_pairs={{0,8},{4,12},{8,0},{12,4},{16,24},{20,28},{24,16},{28,20},{1,9},{5... | collective-permute-start | bytes 1720328 | tf_op jit(solution)/shard_map/ppermute | solution.py:891
  413.2 11.5 %copy-start.25 = (f32[48,512]{1,0:T(8,128)S(1)}, f32[48,512]{1,0:T(8,128)}, u32[]{:S(2)}) copy-start(f32[48,512]{1,0:T(8,128)} %copy-done.24) | copy-start | bytes 294916
  413.2 67.5 %collective-permute-start.28 = (bf16[256,896]{1,0:T(8,128)(2,1)}, bf16[256,896]{1,0:T(8,128)(2,1)}, u32[]{:S(2)}, u32[]{:S(2)}) collective-permute-start(bf16[256,896]{1,0:T(8,128)(2,1)} %fusion.68), channel_id=1, source_target_pairs={{0,16},{4,20},{8,24},{12,28},{16,0},{20,4},{24,8},{28,12},{1,17},{... | collective-permute-start | bytes 1376264 | tf_op jit(solution)/shard_map/ppermute | solution.py:891
  418.3 63.3 %collective-permute-start.27 = (bf16[256,512]{1,0:T(8,128)(2,1)}, bf16[256,512]{1,0:T(8,128)(2,1)}, u32[]{:S(2)}, u32[]{:S(2)}) collective-permute-start(bf16[256,512]{1,0:T(8,128)(2,1)} %fusion.84), channel_id=1, source_target_pairs={{0,16},{4,20},{8,24},{12,28},{16,0},{20,4},{24,8},{28,12},{1,17},{... | collective-permute-start | bytes 786440 | tf_op jit(solution)/shard_map/ppermute | solution.py:891
  424.7 59.2 %collective-permute-start.15 = (bf16[1024,1024]{1,0:T(8,128)(2,1)}, bf16[1024,1024]{1,0:T(8,128)(2,1)}, u32[]{:S(2)}, u32[]{:S(2)}) collective-permute-start(bf16[1024,1024]{1,0:T(8,128)(2,1)} %pad_maximum_fusion.2), channel_id=1, source_target_pairs={{0,1},{1,0},{2,3},{3,2},{4,5},{5,4},{6,7},{7,6},{8,9},{9,8},{10,11... | collective-permute-start | bytes 6291464 | tf_op jit(solution)/shard_map/ppermute | solution.py:977
  426.6 35.6 %copy-start.31 = (bf16[512,512]{1,0:T(8,128)(2,1)}, bf16[512,512]{1,0:T(8,128)(2,1)S(1)}, u32[]{:S(2)}) copy-start(bf16[512,512]{1,0:T(8,128)(2,1)S(1)} %slice.100) | copy-start | bytes 1572868
  427.9 33.3 %collective-permute-start.24 = (bf16[304,512]{1,0:T(8,128)(2,1)S(1)}, bf16[304,512]{1,0:T(8,128)(2,1)S(1)}, u32[]{:S(2)}, u32[]{:S(2)}) collective-permute-start(bf16[304,512]{1,0:T(8,128)(2,1)S(1)} %pad_maximum_fusion.9), channel_id=1, source_target_pairs={{0,16},{4,20},{8,24},{12,28},{16,0},{20,4},{24,8},{28,12},{1,17},{... | collective-permute-start | bytes 933896 | tf_op jit(solution)/shard_map/ppermute | solution.py:891
  431.1 43.5 %collective-permute-start.23 = (bf16[1024,512]{1,0:T(8,128)(2,1)}, bf16[1024,512]{1,0:T(8,128)(2,1)}, u32[]{:S(2)}, u32[]{:S(2)}) collective-permute-start(bf16[1024,512]{1,0:T(8,128)(2,1)} %add_convert_fusion.4), channel_id=1, source_target_pairs={{0,2},{1,3},{2,0},{3,1},{4,6},{5,7},{6,4},{7,5},{8,10},{9,11},{10,... | collective-permute-start | bytes 3145736 | tf_op jit(solution)/shard_map/ppermute | solution.py:977
  461.2 20.3 %collective-permute-start.29 = (bf16[256,512]{1,0:T(8,128)(2,1)}, bf16[256,512]{1,0:T(8,128)(2,1)}, u32[]{:S(2)}, u32[]{:S(2)}) collective-permute-start(bf16[256,512]{1,0:T(8,128)(2,1)} %fusion.83), channel_id=1, source_target_pairs={{0,16},{4,20},{8,24},{12,28},{16,0},{20,4},{24,8},{28,12},{1,17},{... | collective-permute-start | bytes 786440 | tf_op jit(solution)/shard_map/ppermute | solution.py:891
  467.7 4.1 slice-start.2
  474.7 37.8 %collective-permute-start.26 = (bf16[2,256,512]{2,1,0:T(8,128)(2,1)}, bf16[2,256,512]{2,1,0:T(8,128)(2,1)}, u32[]{:S(2)}, u32[]{:S(2)}) collective-permute-start(bf16[2,256,512]{2,1,0:T(8,128)(2,1)} %fusion.62), channel_id=1, source_target_pairs={{0,8},{4,12},{8,0},{12,4},{16,24},{20,28},{24,16},{28,20},{1,9},{5... | collective-permute-start | bytes 1572872 | tf_op jit(solution)/shard_map/ppermute | solution.py:891
  480.7 35.2 %collective-permute-start.25 = (bf16[256,512]{1,0:T(8,128)(2,1)}, bf16[256,512]{1,0:T(8,128)(2,1)}, u32[]{:S(2)}, u32[]{:S(2)}) collective-permute-start(bf16[256,512]{1,0:T(8,128)(2,1)} %fusion.82), channel_id=1, source_target_pairs={{0,16},{4,20},{8,24},{12,28},{16,0},{20,4},{24,8},{28,12},{1,17},{... | collective-permute-start | bytes 786440 | tf_op jit(solution)/shard_map/ppermute | solution.py:891
  485.7 23.5 %collective-permute-start.16 = (bf16[1024,512]{1,0:T(8,128)(2,1)S(1)}, bf16[1024,512]{1,0:T(8,128)(2,1)S(1)}, u32[]{:S(2)}, u32[]{:S(2)}) collective-permute-start(bf16[1024,512]{1,0:T(8,128)(2,1)S(1)} %add_convert_fusion.5), channel_id=1, source_target_pairs={{0,2},{1,3},{2,0},{3,1},{4,6},{5,7},{6,4},{7,5},{8,10},{9,11},{10,... | collective-permute-start | bytes 3145736 | tf_op jit(solution)/shard_map/ppermute | solution.py:977
  489.9 19.3 %copy-start.30 = (f32[1024,512]{1,0:T(8,128)S(1)}, f32[1024,512]{1,0:T(8,128)}, u32[]{:S(2)}) copy-start(f32[1024,512]{1,0:T(8,128)} %get-tuple-element.99) | copy-start | bytes 6291460
  509.2 5.6 %copy-start.32 = (bf16[512,512]{1,0:T(8,128)(2,1)S(1)}, bf16[512,512]{1,0:T(8,128)(2,1)}, u32[]{:S(2)}) copy-start(bf16[512,512]{1,0:T(8,128)(2,1)} %copy-done.31) | copy-start | bytes 1572868
  509.2 5.6 %slice-start.3 = ((bf16[304,512]{1,0:T(8,128)(2,1)}), bf16[256,512]{1,0:T(8,128)(2,1)S(1)}, s32[]{:S(2)}) async-start(bf16[304,512]{1,0:T(8,128)(2,1)} %copy-done.38), calls=%async_computation.3 | async-start | bytes 524288 | tf_op jit(solution)/shard_map/slice | solution.py:901
  513.7 12.4 %collective-permute-start.30 = (bf16[256,512]{1,0:T(8,128)(2,1)S(1)}, bf16[256,512]{1,0:T(8,128)(2,1)S(1)}, u32[]{:S(2)}, u32[]{:S(2)}) collective-permute-start(bf16[256,512]{1,0:T(8,128)(2,1)S(1)} %fusion.75), channel_id=1, source_target_pairs={{0,16},{4,20},{8,24},{12,28},{16,0},{20,4},{24,8},{28,12},{1,17},{... | collective-permute-start | bytes 786440 | tf_op jit(solution)/shard_map/ppermute | solution.py:891
  (22 other events, 40.4 us)

commit v5 on v4

--- a/solution.py
+++ b/solution.py
@@ -325,7 +325,7 @@
             jax.ShapeDtypeStruct((tokens, heads * HEAD_DIM), BF16),
         ],
         scratch_shapes=[pltpu.VMEM((length + 2 * HALO, CHUNK), F32)],
-        compiler_params=pltpu.CompilerParams(vmem_limit_bytes=48 << 20),
+        compiler_params=pltpu.CompilerParams(vmem_limit_bytes=62 << 20),
         name="mixer_forward",
     )(proj, seg.reshape(seqs, 1, length), weight, logits, gain.reshape(1, HEAD_DIM))
 
@@ -362,7 +362,7 @@
             pltpu.VMEM((PAIR, length, HEAD_DIM), F32),
             pltpu.VMEM((PAIR, length, HEAD_DIM), F32),
         ],
-        compiler_params=pltpu.CompilerParams(vmem_limit_bytes=48 << 20),
+        compiler_params=pltpu.CompilerParams(vmem_limit_bytes=62 << 20),
         name="mixer_backward",
     )(proj, seg.reshape(seqs, 1, length), weight, logits, gain.reshape(1, HEAD_DIM), mixed, inverse, scores, states, delta, err, grad_nout)
 
@@ -741,8 +741,20 @@
 
     def partial(m):
         dims = (((1,), (1,)), ((), ()))
-        grad = lax.dot_general(gate[band(m), :], wgu[0], dims, preferred_element_type=F32)
-        grad = grad + lax.dot_general(up[band(m), :], wgu[1], dims, preferred_element_type=F32)
+
+        @pl.when(m == 0)
+        def _():
+            loads[0].wait()
+            loads[1].wait()
+
+        piece[...] = lax.dot_general(gate[band(m), :], wgu[0], dims, preferred_element_type=F32)
+
+        @pl.when(m == 0)
+        def _():
+            for load in loads[2:5]:
+                load.wait()
+
+        grad = piece[...] + lax.dot_general(up[band(m), :], wgu[1], dims, preferred_element_type=F32)
         values = mid[band(m), :].astype(F32)
         scale = lax.rsqrt(jnp.mean(values * values, axis=-1, keepdims=True) + EPS)
         unit = values * scale
@@ -794,8 +806,6 @@
         for copy in outs(m):
             copy.wait()
 
-    for load in loads[:5]:
-        load.wait()
     loop(0, chunks + 1, feed)
     loads[5].wait()
     loop(0, chunks + 1, both)
@@ -984,21 +994,20 @@
             came = swap(away, 1)
             other = (pick(lax.rem(me + 2, 4)) + columns(came, 1 - spot).astype(F32)).astype(BF16)
             far = swap(other, 2)
-            return pick(me) + columns(came, spot).astype(F32), far
+            return pick(me) + columns(came, spot).astype(F32), far, other
 
         taps = conv_weight.astype(F32)
-        rates = jnp.zeros((8, wrate.shape[0]), BF16).at[:heads].set(wrate.T)
-        full_low, normed_one, proj, logits = project(hidden_in, attn_gain, rates, wqkv)
+        full_low, normed_one, proj, logits = project(hidden_in, attn_gain, wrate.T, wqkv)
         cot_own, _ = lax.optimization_barrier((cotangent, logits))
         cot_far = swap(cot_own, 2)
         out_low, *kept = mixer_forward(proj, seg_ids, taps, logits, onorm_gain)
         middle, mid_low, normed_two, hidden, grad_gate, grad_up, full_cot, ffn_part = middle_step(out_low, wout, mlp_gain, cotangent, cot_far, full_low, wdown, wgu)
         line = Timeline(dp_size)
         cut = grad_up.shape[1] // 11 * 4
+        line.scatter("gate", normed_two, grad_gate, 1)
         line.scatter("down", full_cot, hidden, 0)
-        line.scatter("gate", normed_two, grad_gate, 1)
+        line.scatter("upz", normed_two, grad_up[:, :cut], 1)
         line.scatter("upx", normed_two, grad_up[:, cut:], 0)
-        line.scatter("upz", normed_two, grad_up[:, :cut], 1)
         late_gate = line.after(grad_gate)
         grad_middle, full_grad_mid, grad_nout, gain_two = return_step(wout, mlp_gain, late_gate, grad_up, mid_low, full_cot, wgu)
         line.token = grad_nout
@@ -1021,60 +1030,59 @@
         part_one = part_one.astype(BF16)
         line.token = (part_one, gain_one)
         wide = gain_one.shape[0]
-        gains = butterfly(jnp.concatenate([gain_one, gain_two.reshape(-1), gain_onorm.reshape(-1)]), "tensor", tensor_size)
-        shared = gains.shape[0]
+        lanes = grad_proj.shape[2]
+        thin = jnp.concatenate([gain_one.reshape(-1, lanes), gain_two.reshape(-1, lanes), jnp.pad(gain_onorm, ((0, 0), (0, lanes - HEAD_DIM)))])
+        gains = butterfly(thin, "tensor", tensor_size)
         line.move("gate")
-        grad_beta = jnp.einsum("td,ht->dh", normed_one, line.after(grad_logits), preferred_element_type=F32)
+        grad_beta = jnp.einsum("ht,td->hd", line.after(grad_logits), normed_one, preferred_element_type=F32)
         line.move("out")
-        small = jnp.concatenate([gains, grad_conv.reshape(-1), grad_beta.reshape(-1)])
-        lanes = grad_proj.shape[2]
-        extra = -small.shape[0] % (16 * lanes)
-        line.rider = jnp.pad(small, (0, extra)).reshape(-1, lanes)
+        small = jnp.concatenate([grad_conv.reshape(-1, lanes), grad_beta.reshape(-1, lanes), gains])
+        line.rider = jnp.pad(small, ((0, -small.shape[0] % 16), (0, 0)))
         line.scatter("v", normed_one, grad_proj[2], 0, ride=True)
         line.scatter("q", normed_one, grad_proj[0], 0)
         line.move("upx")
         line.move("k")
         line.move("upz")
+        late_ffn, late_one = line.after((ffn_part, part_one))
+        one, one_far, _ = quarter_sum(lambda q: columns(late_one, q).astype(F32))
+        ffn, ffn_far, ffn_sent = quarter_sum(lambda q: columns(late_ffn, q).astype(F32))
+        line.move("v")
         line.move("out")
-        one, one_far = quarter_sum(lambda q: columns(part_one, q).astype(F32))
-        line.move("v")
-        late_ffn = line.after(ffn_part)
-        ffn, ffn_far = quarter_sum(lambda q: columns(late_ffn, q).astype(F32))
         grad_down = line.close("down").T
-        line.token = grad_down
+        line.token = (grad_down, ffn_sent)
         line.move("k")
         line.move("q")
+        grad_in = (grad_middle + one + line.after(one_far).astype(F32)).astype(BF16)
+        line.token = (line.token, grad_in)
         line.move("v")
         grad_gate_w = line.close("gate")
-        grad_in = (grad_middle + one + line.after(one_far).astype(F32)).astype(BF16)
-        line.token = (grad_gate_w, grad_in)
         grad_up_w = jnp.concatenate([line.close("upz"), line.close("upx")], axis=1)
-        grad_gate_up = jnp.stack([grad_gate_w, grad_up_w])
+        line.token = (grad_gate_w, grad_up_w)
+        line.move("q")
+        grad_gate_up = jnp.stack([line.after(grad_gate_w), grad_up_w])
         grad_out = line.close("out").T
         layer_out = (middle + ffn + line.after(ffn_far).astype(F32)).astype(BF16)
-        line.token = (grad_gate_up, grad_out, layer_out)
-        line.move("q")
         grad_k, grad_v = line.close("k"), line.close("v")
-        small = line.rider.reshape(-1)
+        small = line.rider
         grad_qkv = jnp.stack([grad_k, grad_k, grad_v])
-        line.token = (grad_qkv, small)
+        line.token = (grad_gate_up, grad_out, layer_out, grad_qkv, small)
         grad_qkv = lax.dynamic_update_slice(grad_qkv, line.close("q")[None], (0, 0, 0))
-        gains = small[:shared]
-        mine = grad_beta.shape[0] // dp_size
-        rest = small[shared + grad_conv.size :]
-        grad_conv = small[shared : shared + grad_conv.size].reshape(grad_conv.shape)
-        grad_beta = rest[: grad_beta.size].reshape(grad_beta.shape)
-        grad_beta = lax.dynamic_slice_in_dim(grad_beta, lax.axis_index("dp") * mine, mine, 0)
+        conv_rows, beta_rows, gain_rows = grad_conv.size // lanes, grad_beta.size // lanes, wide // lanes
+        grad_conv = small[:conv_rows].reshape(grad_conv.shape)
+        grad_beta = small[conv_rows : conv_rows + beta_rows].reshape(grad_beta.shape)
+        gains = small[conv_rows + beta_rows :]
+        mine = wide // dp_size
+        grad_beta = lax.dynamic_slice_in_dim(grad_beta, lax.axis_index("dp") * mine, mine, 1).T
         return (
             layer_out,
             grad_in,
-            gains[:wide],
+            gains[:gain_rows].reshape(-1),
             grad_qkv,
             grad_conv,
             grad_beta,
-            gains[2 * wide :],
+            gains[2 * gain_rows, :HEAD_DIM],
             grad_out,
-            gains[wide : 2 * wide],
+            gains[gain_rows : 2 * gain_rows].reshape(-1),
             grad_gate_up,
             grad_down,
         )

time: 539 us -> 538 us (level)
  local copies, waits for them, and re-layouts: 49.5 us -> 36 us
  starting transfers between devices: 29.4 us -> 35.4 us
  other arithmetic: 74.1 us -> 79.7 us
    ppermute x5, waiting for transfers between devices: 17.6 us -> 0.01 us  [swap(): lax.ppermute(values, 'tensor', [(i, i ^ step) for i in range(tensor_size)])]
    ppermute x24, waiting for transfers between devices: 89.4 us -> 105 us  [swap(): lax.ppermute(values, 'dp', [(i, i ^ 1 << bit) for i in range(self.size)])]
    ppermute x24, starting transfers between devices: 24.8 us -> 30.9 us  [swap(): lax.ppermute(values, 'dp', [(i, i ^ 1 << bit) for i in range(self.size)])]
    slice x5 -> x2, local copies, waits for them, and re-layouts: 6.05 us -> 0.01 us  [the longest x1 0.01 us: step(): grad_beta = small[conv_rows:conv_rows + beta_rows].reshape(grad_beta.shape)]
    unnamed x115 -> x142, local copies, waits for them, and re-layouts: 22 us -> 16.9 us
  transfers between devices with their start and end apart: 31 -> 31, of which waited for: 7 -> 8; matrix products, arithmetic and copies ran while one was open for 28% -> 26% of each run, Pallas kernels for 23% -> 23%
where the time goes in v5:
time: 538 us; the launch traced here: 528 us
  Pallas kernels  213 us (40%)
  waiting for transfers between devices  108 us (20%)
  other arithmetic  79.7 us (15%)
  matrix products  53.7 us (10%)
  local copies, waits for them, and re-layouts  36 us (7%)
  starting transfers between devices  35.4 us (7%)
    ppermute x24, waiting for transfers between devices, swap(): lax.ppermute(values, 'dp', [(i, i ^ 1 << bit) for i in range(self.size)])  105 us
    pallas_call x1, Pallas kernels, return_step(): pl.pallas_call(return_kernel, in_specs=[in_vmem(), in_vmem()] + [in_hbm()...  65 us
    pallas_call x1, Pallas kernels, middle_step(): pl.pallas_call(middle_kernel, in_specs=[in_vmem(), in_vmem(), in_vmem()]...  59.3 us
    convert_element_type x16, other arithmetic, move(): sum((pick(t, 1 - own).astype(F32) for t in terms)).astype(BF16)  33.6 us
    pallas_call x1, Pallas kernels, project(): pl.pallas_call(project_kernel, in_specs=[in_vmem(), in_vmem(), in_vmem(),...  32.8 us
    pallas_call x1, Pallas kernels, mixer_backward(): pl.pallas_call(backward_kernel, grid=(heads // PAIR, seqs), in_specs=[cub...  32.7 us
    ppermute x24, starting transfers between devices, swap(): lax.ppermute(values, 'dp', [(i, i ^ 1 << bit) for i in range(self.size)])  30.9 us
    dot_general x8, matrix products, product(): lax.dot_general(rows, values, ROWS, preferred_element_type=F32).astype(BF16)  28.9 us
  transfers between devices with their start and end apart: 31, of which 8 were waited for; matrix products, arithmetic and copies ran while one was open for 26% of the time, Pallas kernels for 23%

profile of v5, /device:TPU:0, one launch (start us, length us, event | category | flops | bytes accessed | tf_op | source)
XLA Modules:
  0.0 528.4 jit_solution(17174980119791833592)
XLA Ops:
  0.7 32.8 %project.1 = (bf16[1024,2048]{1,0:T(8,128)(2,1)}, bf16[1024,2048]{1,0:T(8,128)(2,1)}, f32[3,1024,512]{2,1,0:T(8,128)}, f32[4,1024]{1,0:T(4,128)}) custom-call(bf16[1024,512]{1,0:T(8,128)(2,1)} %x_ref.1, f32[1,2048]{1,0:T(1,128)} %bitcast.266, bf16[4,2048]{1,0:T(4,128)(2,1)} %bitcast.269, bf16[3,2048,512]{2,1,0:T(8,128)(2,1)} %weight_ref.1), custom_call_target="tpu_custom_call" | custom-call | tf_op jit(solution)/shard_map/project/pallas_call | solution.py:485
  35.9 23.5 %mixer_forward.1 = (bf16[1024,512]{1,0:T(8,128)(2,1)}, f32[1024,512]{1,0:T(8,128)}, bf16[4,1024,128]{2,1,0:T(8,128)(2,1)}, bf16[4,1024,128]{2,1,0:T(8,128)(2,1)}...) custom-call(f32[3,1024,512]{2,1,0:T(8,128)} %get-tuple-element.84.proj_ref, ...), custom_call_target="tpu_custom_call" | custom-call | tf_op jit(solution)/shard_map/mixer_forward/pallas_call | solution.py:307
  59.4 59.3 %middle_step.1 = (f32[1024,512]{1,0:T(8,128)}, bf16[1024,2048]{1,0:T(8,128)(2,1)}, bf16[1024,2048]{1,0:T(8,128)(2,1)}, bf16[1024,1408]{1,0:T(8,128)(2,1)}, bf16[...) custom-call(bf16[1024,512]{1,0:T(8,128)(2,1)} %get-tuple-element.111, ...), custom_call_target="tpu_custom_call" | custom-call | tf_op jit(solution)/shard_map/middle_step/pallas_call | solution.py:663
  118.7 1.8 constant_dynamic-slice_fusion.23
  121.2 5.0 convolution_convert_fusion.3
  126.2 1.5 constant_dynamic-slice_fusion.21
  128.6 5.0 convolution_convert_fusion.2
  135.3 1.6 collective-permute-start.2
  137.0 2.2 convolution_convert_fusion.8
  139.2 3.6 fusion.49
  144.6 65.0 %return_step.1 = (f32[1024,512]{1,0:T(8,128)}, bf16[1024,2048]{1,0:T(8,128)(2,1)}, f32[1024,512]{1,0:T(8,128)}, f32[1,2048]{1,0:T(1,128)}) custom-call(bf16[512,2048]{1,0:T(8,128)(2,1)} %wout_ref.3, f32[1,2048]{1,0:T(1,128)} %bitcast.271, bf16[1024,1408]{1,0:T(8,128)(2,1)} %get-tuple-element.105.gate_ref, bf16[1024,1408]{1,0:T(8,128)(2,1)} %get-tuple-element.99.up_ref, ...), custom_call_target="tpu_custom_call" | custom-call | tf_op jit(solution)/shard_map/return_step/pallas_call | solution.py:822
  211.5 1.8 constant_dynamic-slice_fusion.17
  213.9 4.3 convolution_convert_fusion.1
  218.3 3.9 fusion.55
  222.7 2.5 convolution_convert_fusion.7
  228.2 3.7 convolution_convert_fusion
  231.9 3.8 fusion.56
  236.1 1.5 copy-done.7
  237.6 2.4 fusion.46
  245.9 32.7 %mixer_backward.1 = (bf16[3,1024,512]{2,1,0:T(8,128)(2,1)}, bf16[4,1,1024]{2,1,0:T(2,128)(2,1)}, f32[3,4,512]{2,1,0:T(4,128)}, f32[1,128]{1,0:T(1,128)}) custom-call(f32[3,1024,512]{2,1,0:T(8,128)} %get-tuple-element.84.proj_ref, s32[2,1,512]{2,1,0:T(1,128)} %reshape.326.seg_ref, f32[3,4,512]{2,1,0:T(4,128)} %convert_element_type.537.weight_ref, ...), custom_call_target="tpu_custom_call" | custom-call | tf_op jit(solution)/shard_map/mixer_backward/pallas_call | solution.py:344
  280.1 3.3 slice_bitcast_fusion
  283.3 2.7 fusion.61
  286.3 2.6 fusion.52
  288.9 2.4 fusion.69
  292.9 2.5 convolution_convert_fusion.6
  298.4 6.7 %fusion.102 = f32[1024,2048,1]{1,0,2:T(8,128)S(1)} fusion(bf16[3,1024,512]{2,1,0:T(8,128)(2,1)S(1)} %copy-done.11, bf16[3,2048,512]{2,1,0:T(8,128)(2,1)S(1)} %bitcast.229), kind=kOutput, calls=%fused_computation.201 | convolution fusion | flops 6442450944 | bytes 17825792 | tf_op jit(solution)/shard_map/ctk,cdk->td/dot_general | solution.py:1025
  305.1 5.5 %fusion.7 = (f32[2048]{0:T(1024)S(1)}, f32[1024]{0:T(1024)S(1)}, f32[1024,2048]{1,0:T(8,128)}) fusion(bf16[1024,2048]{1,0:T(8,128)(2,1)S(1)} %copy-done, f32[1024]{0:T(1024)S(1)} %add_rsqrt_fusion, f32[2048]{0:T(1024)S(1)} %copy-done.58, bf16[4,1024]{1,0:T(4,128)(2,1)S(1)} %bitcast.267, bf16[2048,4]{0,1:T(4,128)(2,1)S(1)} %copy-done.59, ...), kind=kOutput, calls=%fused_computation.9 | convolution fusion | flops 33551360 | bytes 21020672 | tf_op jit(solution)/shard_map/ht,dh->td/dot_general | solution.py:1026
  310.6 7.1 %fusion.6 = bf16[1024,2048]{1,0:T(8,128)(2,1)} fusion(bf16[1024,2048]{1,0:T(8,128)(2,1)} %get-tuple-element.124.x_ref, f32[1024,2048]{1,0:T(8,128)} %get-tuple-element.212, f32[1024]{0:T(1024)S(1)} %broadcast_multiply_fusion, f32[2048]{0:T(1024)S(1)} %copy-done.58, f32[1024]{0:T(1024)S(1)} %add_rsqrt_fusion), kind=kLoop, calls=%fused_computation.8 | loop fusion | flops 14680064 | bytes 16793600 | tf_op jit(solution)/shard_map/convert_element_type | solution.py:1030
  317.8 2.8 fusion.60
  320.7 2.1 fusion.65
  322.8 2.5 convolution_convert_fusion.5
  327.2 2.7 collective-permute-done.12
  331.6 4.6 convolution_convert_fusion.4
  338.7 2.4 fusion.68
  341.1 2.0 fusion.64
  343.1 1.9 fusion.84
  345.2 1.6 pad_maximum_fusion.3
  348.4 1.6 pad_maximum_fusion.2
  350.0 2.6 collective-permute-start.17
  353.2 20.4 %collective-permute-done.19 = bf16[1072,512]{1,0:T(8,128)(2,1)S(1)} collective-permute-done((bf16[1072,512]{1,0:T(8,128)(2,1)}, bf16[1072,512]{1,0:T(8,128)(2,1)S(1)}, u32[]{:S(2)}, u32[]{:S(2)}) %collective-permute-start.19) | collective-permute-done | bytes 1097760 | tf_op jit(solution)/shard_map/ppermute | solution.py:901
  376.9 3.3 collective-permute-done.18
  380.2 2.4 collective-permute-start.16
  382.6 1.8 fusion.83
  385.2 2.8 add_convert_fusion.4
  389.1 1.9 fusion.59
  391.0 1.5 copy.34
  392.5 16.2 %collective-permute-done.22 = bf16[560,512]{1,0:T(8,128)(2,1)} collective-permute-done((bf16[560,512]{1,0:T(8,128)(2,1)}, bf16[560,512]{1,0:T(8,128)(2,1)}, u32[]{:S(2)}, u32[]{:S(2)}) %collective-permute-start.22) | collective-permute-done | bytes 573472 | tf_op jit(solution)/shard_map/ppermute | solution.py:901
  411.5 2.3 collective-permute-start.26
  413.9 1.8 add_convert_fusion.5
  420.2 2.5 collective-permute-start.20
  422.7 3.5 add_convert_fusion.3
  428.0 30.8 %collective-permute-done.21 = bf16[256,1408]{1,0:T(8,128)(2,1)S(1)} collective-permute-done((bf16[256,1408]{1,0:T(8,128)(2,1)}, bf16[256,1408]{1,0:T(8,128)(2,1)S(1)}, u32[]{:S(2)}, u32[]{:S(2)}) %collective-permute-start.21) | collective-permute-done | bytes 720928 | tf_op jit(solution)/shard_map/ppermute | solution.py:901
  458.8 1.9 fusion.57
  461.0 3.0 collective-permute-start.30
  464.0 1.8 fusion.79
  465.8 25.3 %collective-permute-done.28 = bf16[256,512]{1,0:T(8,128)(2,1)S(1)} collective-permute-done((bf16[256,512]{1,0:T(8,128)(2,1)S(1)}, bf16[256,512]{1,0:T(8,128)(2,1)S(1)}, u32[]{:S(2)}, u32[]{:S(2)}) %collective-permute-start.28) | collective-permute-done | bytes 262176 | tf_op jit(solution)/shard_map/ppermute | solution.py:901
  491.1 2.9 collective-permute-start.29
  494.0 2.0 fusion.78
  496.1 2.1 fusion.80
  500.7 8.4 %collective-permute-done.30 = bf16[256,512]{1,0:T(8,128)(2,1)S(1)} collective-permute-done((bf16[256,512]{1,0:T(8,128)(2,1)S(1)}, bf16[256,512]{1,0:T(8,128)(2,1)S(1)}, u32[]{:S(2)}, u32[]{:S(2)}) %collective-permute-start.30) | collective-permute-done | bytes 262176 | tf_op jit(solution)/shard_map/ppermute | solution.py:901
  509.0 1.9 fusion.71
  511.0 2.0 copy.33
  514.2 1.8 pad_maximum_fusion
  517.0 3.3 add_convert_fusion.2
  (240 shorter events, 60.6 us)
Async XLA Ops:
  0.6 32.9 %copy-start.29 = (bf16[1024,512]{1,0:T(8,128)(2,1)S(1)}, bf16[1024,512]{1,0:T(8,128)(2,1)}, u32[]{:S(2)}) copy-start(bf16[1024,512]{1,0:T(8,128)(2,1)} %own_ref.1) | copy-start | bytes 3145732
  0.7 34.0 %copy-start.61 = (s32[2,512]{1,0:T(2,128)S(1)}, s32[2,512]{1,0:T(2,128)}, u32[]{:S(2)}) copy-start(s32[2,512]{1,0:T(2,128)} %param.13) | copy-start | bytes 12292
  0.7 34.6 %copy-start.60 = (bf16[3,4,512]{2,1,0:T(4,128)(2,1)S(1)}, bf16[3,4,512]{2,1,0:T(4,128)(2,1)}, u32[]{:S(2)}) copy-start(bf16[3,4,512]{2,1,0:T(4,128)(2,1)} %param.16) | copy-start | bytes 36868
  33.5 25.9 %collective-permute-start = (bf16[1024,512]{1,0:T(8,128)(2,1)S(1)}, bf16[1024,512]{1,0:T(8,128)(2,1)}, u32[]{:S(2)}, u32[]{:S(2)}) collective-permute-start(bf16[1024,512]{1,0:T(8,128)(2,1)S(1)} %copy-done.29), channel_id=1, source_target_pairs={{0,2},{1,3},{2,0},{3,1},{4,6},{5,7},{6,4},{7,5},{8,10},{9,11},{10,... | collective-permute-start | bytes 3145736 | tf_op jit(solution)/shard_map/ppermute | solution.py:987
  120.6 5.6 %copy-start.31 = (bf16[1024,512]{1,0:T(8,128)(2,1)}, bf16[1024,512]{1,0:T(8,128)(2,1)S(1)}, u32[]{:S(2)}) copy-start(bf16[1024,512]{1,0:T(8,128)(2,1)S(1)} %get-tuple-element.205) | copy-start | bytes 3145732
  120.6 5.6 %copy-start.33 = (bf16[1024,512]{1,0:T(8,128)(2,1)}, bf16[1024,512]{1,0:T(8,128)(2,1)S(1)}, u32[]{:S(2)}) copy-start(bf16[1024,512]{1,0:T(8,128)(2,1)S(1)} %get-tuple-element.206) | copy-start | bytes 3145732
  121.2 5.0 copy-start.5
  128.6 6.5 %copy-start.6 = (bf16[1024,1408]{1,0:T(8,128)(2,1)S(1)}, bf16[1024,1408]{1,0:T(8,128)(2,1)}, u32[]{:S(2)}) copy-start(bf16[1024,1408]{1,0:T(8,128)(2,1)} %get-tuple-element.99.up_ref) | copy-start | bytes 8650756
  133.5 84.7 %collective-permute-start.1 = (bf16[2,2,256,1408]{3,2,1,0:T(8,128)(2,1)}, bf16[2,2,256,1408]{3,2,1,0:T(8,128)(2,1)}, u32[]{:S(2)}, u32[]{:S(2)}) collective-permute-start(bf16[2,2,256,1408]{3,2,1,0:T(8,128)(2,1)} %bitcast.5), channel_id=1, source_target_pairs={{0,4},{4,0},{8,12},{12,8},{16,20},{20,16},{24,28},{28,24},{1,5},{5... | collective-permute-start | bytes 8650760 | tf_op jit(solution)/shard_map/ppermute | solution.py:901
  135.3 96.6 %collective-permute-start.2 = (bf16[2,2,256,1408]{3,2,1,0:T(8,128)(2,1)}, bf16[2,2,256,1408]{3,2,1,0:T(8,128)(2,1)}, u32[]{:S(2)}, u32[]{:S(2)}) collective-permute-start(bf16[2,2,256,1408]{3,2,1,0:T(8,128)(2,1)} %bitcast.4), channel_id=1, source_target_pairs={{0,8},{4,12},{8,0},{12,4},{16,24},{20,28},{24,16},{28,20},{1,9},{5... | collective-permute-start | bytes 8650760 | tf_op jit(solution)/shard_map/ppermute | solution.py:901
  142.8 97.2 %collective-permute-start.3 = (bf16[2,2,256,896]{3,2,1,0:T(8,128)(2,1)}, bf16[2,2,256,896]{3,2,1,0:T(8,128)(2,1)S(1)}, u32[]{:S(2)}, u32[]{:S(2)}) collective-permute-start(bf16[2,2,256,896]{3,2,1,0:T(8,128)(2,1)} %bitcast.7), channel_id=1, source_target_pairs={{0,4},{4,0},{8,12},{12,8},{16,20},{20,16},{24,28},{28,24},{1,5},{5... | collective-permute-start | bytes 5505032 | tf_op jit(solution)/shard_map/ppermute | solution.py:901
  143.4 145.5 %collective-permute-start.5 = (bf16[2,2,256,512]{3,2,1,0:T(8,128)(2,1)}, bf16[2,2,256,512]{3,2,1,0:T(8,128)(2,1)}, u32[]{:S(2)}, u32[]{:S(2)}) collective-permute-start(bf16[2,2,256,512]{3,2,1,0:T(8,128)(2,1)} %bitcast.6), channel_id=1, source_target_pairs={{0,8},{4,12},{8,0},{12,4},{16,24},{20,28},{24,16},{28,20},{1,9},{5... | collective-permute-start | bytes 3145736 | tf_op jit(solution)/shard_map/ppermute | solution.py:901
  213.9 8.8 %copy-start.63 = (bf16[1024,2048]{1,0:T(8,128)(2,1)S(1)}, bf16[1024,2048]{1,0:T(8,128)(2,1)}, u32[]{:S(2)}) copy-start(bf16[1024,2048]{1,0:T(8,128)(2,1)} %get-tuple-element.108) | copy-start | bytes 12582916
  222.2 61.2 %collective-permute-start.4 = (bf16[2,256,1408]{2,1,0:T(8,128)(2,1)}, bf16[2,256,1408]{2,1,0:T(8,128)(2,1)}, u32[]{:S(2)}, u32[]{:S(2)}) collective-permute-start(bf16[2,256,1408]{2,1,0:T(8,128)(2,1)} %fusion.55), channel_id=1, source_target_pairs={{0,8},{4,12},{8,0},{12,4},{16,24},{20,28},{24,16},{28,20},{1,9},{5... | collective-permute-start | bytes 4325384 | tf_op jit(solution)/shard_map/ppermute | solution.py:901
  240.0 38.6 %copy-start.25 = (bf16[2,2,256,896]{3,2,1,0:T(8,128)(2,1)}, bf16[2,2,256,896]{3,2,1,0:T(8,128)(2,1)S(1)}, u32[]{:S(2)}) copy-start(bf16[2,2,256,896]{3,2,1,0:T(8,128)(2,1)S(1)} %collective-permute-done.3) | copy-start | bytes 5505028
  242.3 96.3 %collective-permute-start.8 = (bf16[2,256,896]{2,1,0:T(8,128)(2,1)}, bf16[2,256,896]{2,1,0:T(8,128)(2,1)}, u32[]{:S(2)}, u32[]{:S(2)}) collective-permute-start(bf16[2,256,896]{2,1,0:T(8,128)(2,1)} %fusion.66), channel_id=1, source_target_pairs={{0,8},{4,12},{8,0},{12,4},{16,24},{20,28},{24,16},{28,20},{1,9},{5... | collective-permute-start | bytes 2752520 | tf_op jit(solution)/shard_map/ppermute | solution.py:901
  243.8 73.9 %collective-permute-start.10 = (bf16[2,256,1408]{2,1,0:T(8,128)(2,1)}, bf16[2,256,1408]{2,1,0:T(8,128)(2,1)}, u32[]{:S(2)}, u32[]{:S(2)}) collective-permute-start(bf16[2,256,1408]{2,1,0:T(8,128)(2,1)} %fusion.56), channel_id=1, source_target_pairs={{0,4},{4,0},{8,12},{12,8},{16,20},{20,16},{24,28},{28,24},{1,5},{5... | collective-permute-start | bytes 4325384 | tf_op jit(solution)/shard_map/ppermute | solution.py:901
  245.3 75.4 %collective-permute-start.9 = (bf16[2,2,256,512]{3,2,1,0:T(8,128)(2,1)}, bf16[2,2,256,512]{3,2,1,0:T(8,128)(2,1)}, u32[]{:S(2)}, u32[]{:S(2)}) collective-permute-start(bf16[2,2,256,512]{3,2,1,0:T(8,128)(2,1)} %dynamic-slice_bitcast_fusion.2), channel_id=1, source_target_pairs={{0,4},{4,0},{8,12},{12,8},{16,20},{20,16},{24,28},{28,24},{1,5},{5... | collective-permute-start | bytes 3145736 | tf_op jit(solution)/shard_map/ppermute | solution.py:901
  280.1 49.9 %copy-start.40 = (f32[12,512]{1,0:T(8,128)}, f32[12,512]{1,0:T(8,128)S(1)}, u32[]{:S(2)}) copy-start(f32[12,512]{1,0:T(8,128)S(1)} %reshape.342) | copy-start | bytes 73732
  280.1 5.9 %copy-start.3 = (bf16[1024,2048]{1,0:T(8,128)(2,1)S(1)}, bf16[1024,2048]{1,0:T(8,128)(2,1)}, u32[]{:S(2)}) copy-start(bf16[1024,2048]{1,0:T(8,128)(2,1)} %get-tuple-element.121) | copy-start | bytes 12582916
  286.2 6.6 %copy-start.9 = (bf16[1024,2048]{1,0:T(8,128)(2,1)S(1)}, bf16[1024,2048]{1,0:T(8,128)(2,1)}, u32[]{:S(2)}) copy-start(bf16[1024,2048]{1,0:T(8,128)(2,1)} %get-tuple-element.118) | copy-start | bytes 12582916
  286.2 11.7 %slice-start = ((s8[6291456]{0:T(1024)(128)(4,1)}), s8[4194304]{0:T(1024)(128)(4,1)S(1)}, s32[]{:S(2)}) async-start(s8[6291456]{0:T(1024)(128)(4,1)} %bitcast.228), calls=%async_computation | async-start | bytes 8388608
  288.9 6.4 %copy-start.35 = (bf16[1024,512]{1,0:T(8,128)(2,1)}, bf16[1024,512]{1,0:T(8,128)(2,1)S(1)}, u32[]{:S(2)}) copy-start(bf16[1024,512]{1,0:T(8,128)(2,1)S(1)} %fusion.52) | copy-start | bytes 3145732
  291.4 51.7 %collective-permute-start.6 = (bf16[2,256,512]{2,1,0:T(8,128)(2,1)}, bf16[2,256,512]{2,1,0:T(8,128)(2,1)}, u32[]{:S(2)}, u32[]{:S(2)}) collective-permute-start(bf16[2,256,512]{2,1,0:T(8,128)(2,1)} %fusion.69), channel_id=1, source_target_pairs={{0,4},{4,0},{8,12},{12,8},{16,20},{20,16},{24,28},{28,24},{1,5},{5... | collective-permute-start | bytes 1572872 | tf_op jit(solution)/shard_map/ppermute | solution.py:901
  292.9 5.1 slice-start.1
  295.3 45.8 %copy-start.20 = (bf16[2048,512]{1,0:T(8,128)(2,1)}, bf16[2048,512]{1,0:T(8,128)(2,1)S(1)}, u32[]{:S(2)}) copy-start(bf16[2048,512]{1,0:T(8,128)(2,1)S(1)} %convolution_convert_fusion.6) | copy-start | bytes 6291460
  296.5 44.6 %collective-permute-start.7 = (bf16[2,2,256,512]{3,2,1,0:T(8,128)(2,1)}, bf16[2,2,256,512]{3,2,1,0:T(8,128)(2,1)}, u32[]{:S(2)}, u32[]{:S(2)}) collective-permute-start(bf16[2,2,256,512]{3,2,1,0:T(8,128)(2,1)} %dynamic-slice_bitcast_fusion.1), channel_id=1, source_target_pairs={{0,4},{4,0},{8,12},{12,8},{16,20},{20,16},{24,28},{28,24},{1,5},{5... | collective-permute-start | bytes 3145736 | tf_op jit(solution)/shard_map/ppermute | solution.py:901
  298.4 6.7 %copy-start.58 = (f32[2048]{0:T(1024)S(1)}, f32[2048]{0:T(1024)}, u32[]{:S(2)}) copy-start(f32[2048]{0:T(1024)} %param.14) | copy-start | bytes 24580
  298.4 6.7 %copy-start.59 = (bf16[2048,4]{0,1:T(4,128)(2,1)S(1)}, bf16[2048,4]{0,1:T(4,128)(2,1)}, u32[]{:S(2)}) copy-start(bf16[2048,4]{0,1:T(4,128)(2,1)} %param.17) | copy-start | bytes 49156
  305.1 5.5 %copy-start.62 = (f32[1,128]{1,0:T(1,128)S(1)}, f32[1,128]{1,0:T(1,128)}, u32[]{:S(2)}) copy-start(f32[1,128]{1,0:T(1,128)} %get-tuple-element.132) | copy-start | bytes 1540
  317.7 5.1 copy-start.10
  317.8 8.2 %collective-permute-start.11 = (f32[9,512]{1,0:T(8,128)S(1)}, f32[9,512]{1,0:T(8,128)S(1)}, u32[]{:S(2)}, u32[]{:S(2)}) collective-permute-start(f32[9,512]{1,0:T(8,128)S(1)} %select_maximum_fusion.2), channel_id=1, source_target_pairs={{0,1},{1,0},{2,3},{3,2},{4,5},{5,4},{6,7},{7,6},{8,9},{9,8},{10,11... | collective-permute-start | bytes 55304 | tf_op jit(solution)/shard_map/ppermute | solution.py:874
  326.0 4.0 collective-permute-start.12
  327.2 9.0 %copy-start.43 = (f32[16,512]{1,0:T(8,128)}, f32[16,512]{1,0:T(8,128)S(1)}, u32[]{:S(2)}) copy-start(f32[16,512]{1,0:T(8,128)S(1)} %reshape.343) | copy-start | bytes 98308
  338.7 6.3 %copy-start.4 = (bf16[1024,2048]{1,0:T(8,128)(2,1)S(1)}, bf16[1024,2048]{1,0:T(8,128)(2,1)}, u32[]{:S(2)}) copy-start(bf16[1024,2048]{1,0:T(8,128)(2,1)} %fusion.6) | copy-start | bytes 12582916
  346.8 38.4 %collective-permute-start.23 = (bf16[1024,1024]{1,0:T(8,128)(2,1)}, bf16[1024,1024]{1,0:T(8,128)(2,1)}, u32[]{:S(2)}, u32[]{:S(2)}) collective-permute-start(bf16[1024,1024]{1,0:T(8,128)(2,1)} %pad_maximum_fusion.3), channel_id=1, source_target_pairs={{0,1},{1,0},{2,3},{3,2},{4,5},{5,4},{6,7},{7,6},{8,9},{9,8},{10,11... | collective-permute-start | bytes 6291464 | tf_op jit(solution)/shard_map/ppermute | solution.py:987
  346.8 26.8 %collective-permute-start.19 = (bf16[1072,512]{1,0:T(8,128)(2,1)}, bf16[1072,512]{1,0:T(8,128)(2,1)S(1)}, u32[]{:S(2)}, u32[]{:S(2)}) collective-permute-start(bf16[1072,512]{1,0:T(8,128)(2,1)} %pad_maximum_fusion.8), channel_id=1, source_target_pairs={{0,4},{4,0},{8,12},{12,8},{16,20},{20,16},{24,28},{28,24},{1,5},{5... | collective-permute-start | bytes 3293192 | tf_op jit(solution)/shard_map/ppermute | solution.py:901
  348.4 25.2 %copy-start.36 = (bf16[2,2,256,512]{3,2,1,0:T(8,128)(2,1)S(1)}, bf16[2,2,256,512]{3,2,1,0:T(8,128)(2,1)}, u32[]{:S(2)}) copy-start(bf16[2,2,256,512]{3,2,1,0:T(8,128)(2,1)} %dynamic-slice_bitcast_fusion) | copy-start | bytes 3145732
  350.0 24.8 %copy-start.41 = (f32[12,512]{1,0:T(8,128)S(1)}, f32[12,512]{1,0:T(8,128)}, u32[]{:S(2)}) copy-start(f32[12,512]{1,0:T(8,128)} %copy-done.40) | copy-start | bytes 73732
  350.0 24.8 %copy-start.44 = (f32[16,512]{1,0:T(8,128)S(1)}, f32[16,512]{1,0:T(8,128)}, u32[]{:S(2)}) copy-start(f32[16,512]{1,0:T(8,128)} %copy-done.43) | copy-start | bytes 98308
  350.0 24.8 %copy-start.47 = (f32[9,512]{1,0:T(8,128)S(1)}, f32[9,512]{1,0:T(8,128)}, u32[]{:S(2)}) copy-start(f32[9,512]{1,0:T(8,128)} %copy-done.46) | copy-start | bytes 55300
  350.0 61.5 %collective-permute-start.13 = (bf16[1024,1024]{1,0:T(8,128)(2,1)}, bf16[1024,1024]{1,0:T(8,128)(2,1)}, u32[]{:S(2)}, u32[]{:S(2)}) collective-permute-start(bf16[1024,1024]{1,0:T(8,128)(2,1)} %pad_maximum_fusion.2), channel_id=1, source_target_pairs={{0,1},{1,0},{2,3},{3,2},{4,5},{5,4},{6,7},{7,6},{8,9},{9,8},{10,11... | collective-permute-start | bytes 6291464 | tf_op jit(solution)/shard_map/ppermute | solution.py:987
  350.0 35.1 %collective-permute-start.17 = (bf16[256,1408]{1,0:T(8,128)(2,1)}, bf16[256,1408]{1,0:T(8,128)(2,1)S(1)}, u32[]{:S(2)}, u32[]{:S(2)}) collective-permute-start(bf16[256,1408]{1,0:T(8,128)(2,1)} %fusion.61), channel_id=1, source_target_pairs={{0,16},{4,20},{8,24},{12,28},{16,0},{20,4},{24,8},{28,12},{1,17},{... | collective-permute-start | bytes 2162696 | tf_op jit(solution)/shard_map/ppermute | solution.py:901
  352.7 27.6 %collective-permute-start.18 = (bf16[2,256,512]{2,1,0:T(8,128)(2,1)}, bf16[2,256,512]{2,1,0:T(8,128)(2,1)S(1)}, u32[]{:S(2)}, u32[]{:S(2)}) collective-permute-start(bf16[2,256,512]{2,1,0:T(8,128)(2,1)} %fusion.65), channel_id=1, source_target_pairs={{0,8},{4,12},{8,0},{12,4},{16,24},{20,28},{24,16},{28,20},{1,9},{5... | collective-permute-start | bytes 1572872 | tf_op jit(solution)/shard_map/ppermute | solution.py:901
  373.6 44.1 %collective-permute-start.15 = (bf16[2,2,256,512]{3,2,1,0:T(8,128)(2,1)S(1)}, bf16[2,2,256,512]{3,2,1,0:T(8,128)(2,1)}, u32[]{:S(2)}, u32[]{:S(2)}) collective-permute-start(bf16[2,2,256,512]{3,2,1,0:T(8,128)(2,1)S(1)} %copy-done.36), channel_id=1, source_target_pairs={{0,4},{4,0},{8,12},{12,8},{16,20},{20,16},{24,28},{28,24},{1,5},{5... | collective-permute-start | bytes 3145736 | tf_op jit(solution)/shard_map/ppermute | solution.py:901
  380.2 35.5 %collective-permute-start.16 = (bf16[2,256,512]{2,1,0:T(8,128)(2,1)}, bf16[2,256,512]{2,1,0:T(8,128)(2,1)}, u32[]{:S(2)}, u32[]{:S(2)}) collective-permute-start(bf16[2,256,512]{2,1,0:T(8,128)(2,1)} %fusion.64), channel_id=1, source_target_pairs={{0,8},{4,12},{8,0},{12,4},{16,24},{20,28},{24,16},{28,20},{1,9},{5... | collective-permute-start | bytes 1572872 | tf_op jit(solution)/shard_map/ppermute | solution.py:901
  385.2 23.5 %collective-permute-start.22 = (bf16[560,512]{1,0:T(8,128)(2,1)}, bf16[560,512]{1,0:T(8,128)(2,1)}, u32[]{:S(2)}, u32[]{:S(2)}) collective-permute-start(bf16[560,512]{1,0:T(8,128)(2,1)} %pad_maximum_fusion.9), channel_id=1, source_target_pairs={{0,8},{4,12},{8,0},{12,4},{16,24},{20,28},{24,16},{28,20},{1,9},{5... | collective-permute-start | bytes 1720328 | tf_op jit(solution)/shard_map/ppermute | solution.py:901
  388.0 32.2 %collective-permute-start.24 = (bf16[1024,512]{1,0:T(8,128)(2,1)}, bf16[1024,512]{1,0:T(8,128)(2,1)}, u32[]{:S(2)}, u32[]{:S(2)}) collective-permute-start(bf16[1024,512]{1,0:T(8,128)(2,1)} %add_convert_fusion.4), channel_id=1, source_target_pairs={{0,2},{1,3},{2,0},{3,1},{4,6},{5,7},{6,4},{7,5},{8,10},{9,11},{10,... | collective-permute-start | bytes 3145736 | tf_op jit(solution)/shard_map/ppermute | solution.py:987
  392.5 23.2 %copy-start.56 = (bf16[256,512]{1,0:T(8,128)(2,1)S(1)}, bf16[256,512]{1,0:T(8,128)(2,1)}, u32[]{:S(2)}) copy-start(bf16[256,512]{1,0:T(8,128)(2,1)} %fusion.84) | copy-start | bytes 786436
  408.7 50.1 %collective-permute-start.21 = (bf16[256,1408]{1,0:T(8,128)(2,1)}, bf16[256,1408]{1,0:T(8,128)(2,1)S(1)}, u32[]{:S(2)}, u32[]{:S(2)}) collective-permute-start(bf16[256,1408]{1,0:T(8,128)(2,1)} %fusion.60), channel_id=1, source_target_pairs={{0,16},{4,20},{8,24},{12,28},{16,0},{20,4},{24,8},{28,12},{1,17},{... | collective-permute-start | bytes 2162696 | tf_op jit(solution)/shard_map/ppermute | solution.py:901
  410.5 15.8 %copy-start.23 = (bf16[512,512]{1,0:T(8,128)(2,1)}, bf16[512,512]{1,0:T(8,128)(2,1)S(1)}, u32[]{:S(2)}) copy-start(bf16[512,512]{1,0:T(8,128)(2,1)S(1)} %slice.70) | copy-start | bytes 1572868
  411.5 87.6 %collective-permute-start.26 = (bf16[256,896]{1,0:T(8,128)(2,1)}, bf16[256,896]{1,0:T(8,128)(2,1)S(1)}, u32[]{:S(2)}, u32[]{:S(2)}) collective-permute-start(bf16[256,896]{1,0:T(8,128)(2,1)} %fusion.68), channel_id=1, source_target_pairs={{0,16},{4,20},{8,24},{12,28},{16,0},{20,4},{24,8},{28,12},{1,17},{... | collective-permute-start | bytes 1376264 | tf_op jit(solution)/shard_map/ppermute | solution.py:901
  415.7 7.0 %copy-start.22 = (f32[1024,512]{1,0:T(8,128)S(1)}, f32[1024,512]{1,0:T(8,128)}, u32[]{:S(2)}) copy-start(f32[1024,512]{1,0:T(8,128)} %get-tuple-element.143) | copy-start | bytes 6291460
  415.7 75.4 %collective-permute-start.25 = (bf16[256,512]{1,0:T(8,128)(2,1)S(1)}, bf16[256,512]{1,0:T(8,128)(2,1)S(1)}, u32[]{:S(2)}, u32[]{:S(2)}) collective-permute-start(bf16[256,512]{1,0:T(8,128)(2,1)S(1)} %copy-done.56), channel_id=1, source_target_pairs={{0,16},{4,20},{8,24},{12,28},{16,0},{20,4},{24,8},{28,12},{1,17},{... | collective-permute-start | bytes 786440 | tf_op jit(solution)/shard_map/ppermute | solution.py:901
  417.7 80.5 %collective-permute-start.14 = (bf16[1024,512]{1,0:T(8,128)(2,1)S(1)}, bf16[1024,512]{1,0:T(8,128)(2,1)S(1)}, u32[]{:S(2)}, u32[]{:S(2)}) collective-permute-start(bf16[1024,512]{1,0:T(8,128)(2,1)S(1)} %add_convert_fusion.5), channel_id=1, source_target_pairs={{0,2},{1,3},{2,0},{3,1},{4,6},{5,7},{6,4},{7,5},{8,10},{9,11},{10,... | collective-permute-start | bytes 3145736 | tf_op jit(solution)/shard_map/ppermute | solution.py:987
  420.2 40.5 %collective-permute-start.20 = (bf16[2,256,512]{2,1,0:T(8,128)(2,1)S(1)}, bf16[2,256,512]{2,1,0:T(8,128)(2,1)S(1)}, u32[]{:S(2)}, u32[]{:S(2)}) collective-permute-start(bf16[2,256,512]{2,1,0:T(8,128)(2,1)S(1)} %fusion.62), channel_id=1, source_target_pairs={{0,8},{4,12},{8,0},{12,4},{16,24},{20,28},{24,16},{28,20},{1,9},{5... | collective-permute-start | bytes 1572872 | tf_op jit(solution)/shard_map/ppermute | solution.py:901
  428.0 32.7 %copy-start.57 = (bf16[256,512]{1,0:T(8,128)(2,1)S(1)}, bf16[256,512]{1,0:T(8,128)(2,1)}, u32[]{:S(2)}) copy-start(bf16[256,512]{1,0:T(8,128)(2,1)} %fusion.83) | copy-start | bytes 786436
  458.8 32.3 %collective-permute-start.28 = (bf16[256,512]{1,0:T(8,128)(2,1)S(1)}, bf16[256,512]{1,0:T(8,128)(2,1)S(1)}, u32[]{:S(2)}, u32[]{:S(2)}) collective-permute-start(bf16[256,512]{1,0:T(8,128)(2,1)S(1)} %fusion.82), channel_id=1, source_target_pairs={{0,16},{4,20},{8,24},{12,28},{16,0},{20,4},{24,8},{28,12},{1,17},{... | collective-permute-start | bytes 786440 | tf_op jit(solution)/shard_map/ppermute | solution.py:901
  460.7 37.5 %copy-start.54 = (bf16[2,256,512]{2,1,0:T(8,128)(2,1)}, bf16[2,256,512]{2,1,0:T(8,128)(2,1)S(1)}, u32[]{:S(2)}) copy-start(bf16[2,256,512]{2,1,0:T(8,128)(2,1)S(1)} %collective-permute-done.20) | copy-start | bytes 1572868
  461.0 48.0 %collective-permute-start.30 = (bf16[256,512]{1,0:T(8,128)(2,1)S(1)}, bf16[256,512]{1,0:T(8,128)(2,1)S(1)}, u32[]{:S(2)}, u32[]{:S(2)}) collective-permute-start(bf16[256,512]{1,0:T(8,128)(2,1)S(1)} %copy-done.57), channel_id=1, source_target_pairs={{0,16},{4,20},{8,24},{12,28},{16,0},{20,4},{24,8},{28,12},{1,17},{... | collective-permute-start | bytes 786440 | tf_op jit(solution)/shard_map/ppermute | solution.py:901
  491.1 29.2 %collective-permute-start.27 = (bf16[304,512]{1,0:T(8,128)(2,1)}, bf16[304,512]{1,0:T(8,128)(2,1)}, u32[]{:S(2)}, u32[]{:S(2)}) collective-permute-start(bf16[304,512]{1,0:T(8,128)(2,1)} %pad_maximum_fusion.10), channel_id=1, source_target_pairs={{0,16},{4,20},{8,24},{12,28},{16,0},{20,4},{24,8},{28,12},{1,17},{... | collective-permute-start | bytes 933896 | tf_op jit(solution)/shard_map/ppermute | solution.py:901
  491.1 33.7 %collective-permute-start.29 = (bf16[256,512]{1,0:T(8,128)(2,1)}, bf16[256,512]{1,0:T(8,128)(2,1)}, u32[]{:S(2)}, u32[]{:S(2)}) collective-permute-start(bf16[256,512]{1,0:T(8,128)(2,1)} %fusion.79), channel_id=1, source_target_pairs={{0,16},{4,20},{8,24},{12,28},{16,0},{20,4},{24,8},{28,12},{1,17},{... | collective-permute-start | bytes 786440 | tf_op jit(solution)/shard_map/ppermute | solution.py:901
  496.1 12.9 %copy-start.53 = (bf16[2,256,512]{2,1,0:T(8,128)(2,1)S(1)}, bf16[2,256,512]{2,1,0:T(8,128)(2,1)}, u32[]{:S(2)}) copy-start(bf16[2,256,512]{2,1,0:T(8,128)(2,1)} %copy-done.52) | copy-start | bytes 1572868
  517.0 5.2 copy-start.24
  (35 other events, 99.5 us)
